TPU v7x, 32 devices: a whole 2x2x4 slice. The times are simulated.
32 devices in a mesh: hp: 4 (over x, y), cp: 8 (over z, core).
Axes of the slice: x: 2, y: 2, z: 4, core: 2. Of those that a mesh axis runs over, the one named last changes fastest.
Arguments:
- q: bfloat16 [6144, 16, 64], P('cp', 'hp'), parts along dimension 1
- k: bfloat16 [6144, 16, 64], P('cp', 'hp'), parts along dimension 1
- v: bfloat16 [6144, 16, 64], P('cp', 'hp'), parts along dimension 1
- u_bias: float32 [16, 64], P('hp'), parts along dimension 0
- v_bias: float32 [16, 64], P('hp'), parts along dimension 0
- rel_table: bfloat16 [6144, 1024], P('cp')
- w_rel: bfloat16 [1024, 16, 64], P(None, 'hp'), parts along dimension 1
- d_out: bfloat16 [6144, 16, 64], P('cp', 'hp'), parts along dimension 1
Outputs:
- output 1: bfloat16 [6144, 16, 64], P('cp', 'hp'), parts along dimension 1
- output 2: bfloat16 [6144, 16, 64], P('cp', 'hp'), parts along dimension 1
- output 3: bfloat16 [6144, 16, 64], P('cp', 'hp'), parts along dimension 1
- output 4: bfloat16 [6144, 16, 64], P('cp', 'hp'), parts along dimension 1
- output 5: float32 [16, 64], P('hp'), parts along dimension 0
- output 6: float32 [16, 64], P('hp'), parts along dimension 0
- output 7: float32 [1024, 16, 64], P(None, 'hp'), parts along dimension 1
There are 4 independent parts. A program takes and returns all parts, laid end to end along the dimension named above; an argument that names none is the same for every part.
All inputs are finite; a program needn't handle non-finite values.
Results may differ from a plain program's by a relative error of at most 0.0151205.
Values are sent between devices in bfloat16 or wider.
A program may use at most 1 GiB of HBM per device.

v0:
```python
import jax
import jax.numpy as jnp
from jax import lax
from jax.sharding import PartitionSpec as P


def skew_scores(by_offset):
    lead_dims = by_offset.shape[:-2]
    block_len = by_offset.shape[-2]
    flat_view = by_offset.reshape(lead_dims + (2 * block_len * block_len,))
    kept_view = flat_view[..., block_len - 1:block_len - 1 + block_len * (2 * block_len - 1)]
    return kept_view.reshape(lead_dims + (block_len, 2 * block_len - 1))[..., :block_len]


def unskew_scores(by_key):
    lead_dims = by_key.shape[:-2]
    block_len = by_key.shape[-1]
    pad_lead = [(0, 0)] * len(lead_dims)
    widened = jnp.pad(by_key, pad_lead + [(0, 0), (0, block_len - 1)])
    flat_view = widened.reshape(lead_dims + (block_len * (2 * block_len - 1),))
    flat_view = jnp.pad(flat_view, pad_lead + [(block_len - 1, 1)])
    return flat_view.reshape(lead_dims + (block_len, 2 * block_len))


def solution(mesh):
    n_dev = mesh.shape['cp']
    shift_pairs = [(src_dev, (src_dev + 1) % n_dev) for src_dev in range(n_dev)]
    last_step = n_dev - 1
    seq_spec = P('cp', 'hp', None)
    head_spec = P('hp', None)
    weight_spec = P(None, 'hp', None)

    def local_fn(q, k, v, u_bias, v_bias, rel_table, w_rel, d_out):
        block_len, num_heads, head_dim = q.shape
        inv_sqrt = head_dim ** -0.5
        my_block = lax.axis_index('cp')
        rel_mine = jnp.einsum('uo,ojf->ujf', rel_table, w_rel, preferred_element_type=jnp.float32).astype(jnp.bfloat16)
        rel_flipped = lax.all_gather(rel_mine[::-1], 'cp')
        q_wide = q.astype(jnp.float32)
        q_u = (q_wide + u_bias).astype(jnp.bfloat16)
        q_v = (q_wide + v_bias).astype(jnp.bfloat16)
        row_ids = jnp.arange(block_len)
        above_diag = row_ids[None, :] > row_ids[:, None]

        def rel_window(distance):
            near_blk = lax.dynamic_index_in_dim(rel_flipped, distance, 0, keepdims=False)
            far_blk = lax.dynamic_index_in_dim(rel_flipped, jnp.maximum(distance - 1, 0), 0, keepdims=False)
            return jnp.concatenate([near_blk, far_blk], axis=0)

        def block_scores(k_blk, window, distance):
            content = jnp.einsum('qhd,khd->hqk', q_u, k_blk, preferred_element_type=jnp.float32)
            by_offset = jnp.einsum('qhd,shd->hqs', q_v, window, preferred_element_type=jnp.float32)
            score_ij = (content + skew_scores(by_offset)) * inv_sqrt
            return jnp.where(above_diag & (distance == 0), -jnp.inf, score_ij)

        def attend(distance, k_blk, v_blk, run_stats):
            run_max, run_sum, out_acc = run_stats
            score_ij = block_scores(k_blk, rel_window(distance), distance)
            new_max = jnp.maximum(run_max, score_ij.max(axis=-1))
            prob_ij = jnp.exp(score_ij - new_max[..., None])
            rescale = jnp.exp(run_max - new_max)
            run_sum = rescale * run_sum + prob_ij.sum(axis=-1)
            out_acc = out_acc * rescale.T[:, :, None] + jnp.einsum('hqk,khd->qhd', prob_ij.astype(jnp.bfloat16), v_blk, preferred_element_type=jnp.float32)
            return new_max, run_sum, out_acc

        def fwd_step(step_idx, carry):
            k_blk, v_blk, run_stats = carry
            run_stats = lax.cond(step_idx <= my_block, lambda stats_in: attend(step_idx, k_blk, v_blk, stats_in), lambda stats_in: stats_in, run_stats)
            k_blk = lax.ppermute(k_blk, 'cp', shift_pairs)
            v_blk = lax.ppermute(v_blk, 'cp', shift_pairs)
            return k_blk, v_blk, run_stats

        run_stats = (
            jnp.full((num_heads, block_len), -jnp.inf, jnp.float32),
            jnp.zeros((num_heads, block_len), jnp.float32),
            jnp.zeros((block_len, num_heads, head_dim), jnp.float32),
        )
        k_blk, v_blk, run_stats = lax.fori_loop(0, last_step, fwd_step, (k, v, run_stats))
        run_stats = lax.cond(last_step <= my_block, lambda stats_in: attend(last_step, k_blk, v_blk, stats_in), lambda stats_in: stats_in, run_stats)
        run_max, run_sum, out_acc = run_stats
        out_full = out_acc / run_sum.T[:, :, None]
        log_norm = run_max + jnp.log(run_sum)
        row_delta = jnp.sum(d_out.astype(jnp.float32) * out_full, axis=-1).T

        def grad_block(distance, k_blk, v_blk, grad_state):
            dk_acc, dv_acc, grad_qu, grad_qv, grad_rel = grad_state
            window = rel_window(distance)
            score_ij = block_scores(k_blk, window, distance)
            prob_ij = jnp.exp(score_ij - log_norm[..., None])
            d_prob = jnp.einsum('qhd,khd->hqk', d_out, v_blk, preferred_element_type=jnp.float32)
            d_score = (prob_ij * (d_prob - row_delta[..., None]) * inv_sqrt).astype(jnp.bfloat16)
            dv_acc = dv_acc + jnp.einsum('hqk,qhd->khd', prob_ij.astype(jnp.bfloat16), d_out, preferred_element_type=jnp.float32)
            dk_acc = dk_acc + jnp.einsum('hqk,qhd->khd', d_score, q_u, preferred_element_type=jnp.float32)
            grad_qu = grad_qu + jnp.einsum('hqk,khd->qhd', d_score, k_blk, preferred_element_type=jnp.float32)
            d_wide = unskew_scores(d_score)
            grad_qv = grad_qv + jnp.einsum('hqs,shd->qhd', d_wide, window, preferred_element_type=jnp.float32)
            d_window = jnp.einsum('hqs,qhd->shd', d_wide, q_v, preferred_element_type=jnp.float32)
            near_sum = lax.dynamic_index_in_dim(grad_rel, distance, 0, keepdims=False) + d_window[:block_len]
            grad_rel = lax.dynamic_update_index_in_dim(grad_rel, near_sum, distance, 0)
            far_idx = jnp.maximum(distance - 1, 0)
            far_sum = lax.dynamic_index_in_dim(grad_rel, far_idx, 0, keepdims=False) + d_window[block_len:]
            grad_rel = lax.dynamic_update_index_in_dim(grad_rel, far_sum, far_idx, 0)
            return dk_acc, dv_acc, grad_qu, grad_qv, grad_rel

        def bwd_step(step_idx, carry):
            k_blk, v_blk, grad_state = carry
            grad_state = lax.cond(step_idx <= my_block, lambda grads_in: grad_block(step_idx, k_blk, v_blk, grads_in), lambda grads_in: grads_in, grad_state)
            dk_acc, dv_acc, grad_qu, grad_qv, grad_rel = grad_state
            k_blk = lax.ppermute(k_blk, 'cp', shift_pairs)
            v_blk = lax.ppermute(v_blk, 'cp', shift_pairs)
            dk_acc = lax.ppermute(dk_acc, 'cp', shift_pairs)
            dv_acc = lax.ppermute(dv_acc, 'cp', shift_pairs)
            return k_blk, v_blk, (dk_acc, dv_acc, grad_qu, grad_qv, grad_rel)

        blk_zeros = jnp.zeros((block_len, num_heads, head_dim), jnp.float32)
        grad_state = (blk_zeros, blk_zeros, blk_zeros, blk_zeros, jnp.zeros((n_dev, block_len, num_heads, head_dim), jnp.float32))
        k_blk, v_blk, grad_state = lax.fori_loop(0, last_step, bwd_step, (k, v, grad_state))
        grad_state = lax.cond(last_step <= my_block, lambda grads_in: grad_block(last_step, k_blk, v_blk, grads_in), lambda grads_in: grads_in, grad_state)
        dk_acc, dv_acc, grad_qu, grad_qv, grad_rel = grad_state
        dk_acc = lax.ppermute(dk_acc, 'cp', shift_pairs)
        dv_acc = lax.ppermute(dv_acc, 'cp', shift_pairs)
        rel_grad_mine = lax.psum_scatter(grad_rel, 'cp', scatter_dimension=0, tiled=False)
        d_rel = rel_grad_mine[::-1].astype(jnp.bfloat16)
        d_w_rel = lax.psum(jnp.einsum('uo,ujf->ojf', rel_table, d_rel, preferred_element_type=jnp.float32), 'cp')
        d_u_bias = lax.psum(grad_qu.sum(axis=0), 'cp')
        d_v_bias = lax.psum(grad_qv.sum(axis=0), 'cp')
        return (
            out_full.astype(jnp.bfloat16),
            (grad_qu + grad_qv).astype(jnp.bfloat16),
            dk_acc.astype(jnp.bfloat16),
            dv_acc.astype(jnp.bfloat16),
            d_u_bias,
            d_v_bias,
            d_w_rel,
        )

    return jax.shard_map(
        local_fn,
        mesh=mesh,
        in_specs=(seq_spec, seq_spec, seq_spec, head_spec, head_spec, P('cp', None), weight_spec, seq_spec),
        out_specs=(seq_spec, seq_spec, seq_spec, seq_spec, head_spec, head_spec, weight_spec),
        check_vma=False,
    )
```

profile of v0, /device:TPU:0, one launch (start us, length us, event | category | flops | bytes accessed | tf_op | source)
XLA Modules:
  0.0 3826.9 jit_solution(17494995196550410463)
XLA Ops:
  17.5 37.6 all-gather.3.cloned.1.call-done
  63.6 1127.4 %while.48 = (s32[]{:T(128)}, bf16[768,4,64]{0,2,1:T(8,128)(2,1)S(1)}, bf16[768,4,64]{0,2,1:T(8,128)(2,1)S(1)}, f32[4,768]{1,0:T(4,128)S(1)}, f32[4,768]{1,0:T(4,...) while((s32[]{:T(128)}, ...), condition=%wide.region_5.6_spmd.clone, body=%wide.region_0.5_spmd.clone.sunk | while | flops 1229988864 | bytes 304079264 | solution.py:78
  92.5 175.9 %conditional.10 = ((f32[4,768]{1,0:T(4,128)S(1)}, f32[4,768]{1,0:T(4,128)S(1)}, f32[768,4,64]{0,2,1:T(8,128)S(1)})) conditional(s32[]{:T(128)} %convert_element_type.127, (f32[4,768]{1,0:T(4,128)S(1)}, f32[4,768]{1,0:T(4,128)S(1)}, f32[768,4,64]{0,2,1:T(8,128)S(1)}) %tuple.139, (s32[]{:T(128)}, s32[768,768]{0,1:T(8,128)}, ...), branch_computations={%region_1.0_spmd, %region_2.4_spmd} | conditional | flops 1229988864 | bytes 294641760 | solution.py:68
  155.0 53.7 %reshape.67 = f32[4715520]{0:T(1024)} reshape(f32[4,1178880]{1,0:T(4,128)} %slice.44) | data formatting | bytes 37724160 | tf_op jit(solution)/shard_map/while/body/eval_jaxpr/cond
  208.7 29.4 reshape.50
  283.2 168.0 %collective-permute-start = (bf16[768,4,64]{0,2,1:T(8,128)(2,1)}, bf16[768,4,64]{0,2,1:T(8,128)(2,1)S(1)}, u32[]{:S(2)}, u32[]{:S(2)}) collective-permute-start(bf16[768,4,64]{0,2,1:T(8,128)(2,1)} %copy.102), channel_id=1, source_target_pairs={{0,1},{1,2},{2,3},{3,4},{4,5},{5,6},{6,7},{7,0},{8,9},{9,10},{10,1... | collective-permute-start | bytes 1179656 | tf_op jit(solution)/shard_map/while/body/eval_jaxpr/ppermute | solution.py:69
  464.6 170.7 %collective-permute-start.1 = (bf16[768,4,64]{0,2,1:T(8,128)(2,1)}, bf16[768,4,64]{0,2,1:T(8,128)(2,1)S(1)}, u32[]{:S(2)}, u32[]{:S(2)}) collective-permute-start(bf16[768,4,64]{0,2,1:T(8,128)(2,1)} %copy.103), channel_id=1, source_target_pairs={{0,1},{1,2},{2,3},{3,4},{4,5},{5,6},{6,7},{7,0},{8,9},{9,10},{10,1... | collective-permute-start | bytes 1179656 | tf_op jit(solution)/shard_map/while/body/eval_jaxpr/ppermute | solution.py:70
  650.6 170.7 %collective-permute-done = bf16[768,4,64]{0,2,1:T(8,128)(2,1)S(1)} collective-permute-done((bf16[768,4,64]{0,2,1:T(8,128)(2,1)}, bf16[768,4,64]{0,2,1:T(8,128)(2,1)S(1)}, u32[]{:S(2)}, u32[]{:S(2)}) %collective-permute-start) | collective-permute-done | bytes 393248 | tf_op jit(solution)/shard_map/while/body/eval_jaxpr/ppermute | solution.py:69
  830.1 171.8 %collective-permute-done = bf16[768,4,64]{0,2,1:T(8,128)(2,1)S(1)} collective-permute-done((bf16[768,4,64]{0,2,1:T(8,128)(2,1)}, bf16[768,4,64]{0,2,1:T(8,128)(2,1)S(1)}, u32[]{:S(2)}, u32[]{:S(2)}) %collective-permute-start) | collective-permute-done | bytes 393248 | tf_op jit(solution)/shard_map/while/body/eval_jaxpr/ppermute | solution.py:69
  1010.6 171.8 %collective-permute-done = bf16[768,4,64]{0,2,1:T(8,128)(2,1)S(1)} collective-permute-done((bf16[768,4,64]{0,2,1:T(8,128)(2,1)}, bf16[768,4,64]{0,2,1:T(8,128)(2,1)S(1)}, u32[]{:S(2)}, u32[]{:S(2)}) %collective-permute-start) | collective-permute-done | bytes 393248 | tf_op jit(solution)/shard_map/while/body/eval_jaxpr/ppermute | solution.py:69
  1209.0 2239.3 %while.49 = (s32[]{:T(128)}, bf16[768,4,64]{0,2,1:T(8,128)(2,1)S(1)}, bf16[768,4,64]{0,2,1:T(8,128)(2,1)}, f32[768,4,64]{0,2,1:T(8,128)S(1)}, f32[768,4,64]{0,2,...) while((s32[]{:T(128)}, ...), condition=%wide.region_14.15_spmd.clone, body=%wide.region_11.14_spmd.clone.sunk | while | flops 3348627456 | bytes 511095776 | solution.py:117
  1214.9 239.7 %conditional.11 = ((f32[768,4,64]{0,2,1:T(8,128)S(1)}, f32[768,4,64]{0,2,1:T(8,128)}, f32[768,4,64]{0,2,1:T(8,128)S(1)}, f32[768,4,64]{0,2,1:T(8,128)}, f32[8,768,4,64]{1,3,2,0:T(8,128)})) conditional(s32[]{:T(128)} %convert_element_type.128, (f32[768,4,64]{0,2,1:T(8,128)S(1)}, f32[768,4,64]{0,2,1:T(8,128)}, f32[768,4,64]{0,2,1:T(8,128)S(1)}, ...), branch_computations={%region_12.12_spmd, %region_13.13_spmd} | conditional | flops 3348627456 | bytes 492220928 | solution.py:107
  1279.4 53.9 %reshape.69 = f32[4715520]{0:T(1024)} reshape(f32[4,1178880]{1,0:T(4,128)} %slice.46) | data formatting | bytes 37724160 | tf_op jit(solution)/shard_map/while/body/eval_jaxpr/cond
  1333.3 29.4 reshape.54
  1454.9 344.3 %collective-permute-done.4 = f32[768,4,64]{0,2,1:T(8,128)} collective-permute-done((f32[768,4,64]{0,2,1:T(8,128)S(1)}, f32[768,4,64]{0,2,1:T(8,128)}, u32[]{:S(2)}, u32[]{:S(2)}) %collective-permute-start.4) | collective-permute-done | bytes 786464 | tf_op jit(solution)/shard_map/while/body/eval_jaxpr/ppermute | solution.py:111
  1824.8 50.8 %collective-permute-start.5 = (f32[768,4,64]{0,2,1:T(8,128)}, f32[768,4,64]{0,2,1:T(8,128)}, u32[]{:S(2)}, u32[]{:S(2)}) collective-permute-start(f32[768,4,64]{0,2,1:T(8,128)} %get-tuple-element.1113), channel_id=1, source_target_pairs={{0,1},{1,2},{2,3},{3,4},{4,5},{5,6},{6,7},{7,0},{8,9},{9,10},{10,1... | collective-permute-start | bytes 2359304 | tf_op jit(solution)/shard_map/while/body/eval_jaxpr/ppermute | solution.py:112
  1875.6 165.9 %collective-permute-start.2 = (bf16[768,4,64]{0,2,1:T(8,128)(2,1)}, bf16[768,4,64]{0,2,1:T(8,128)(2,1)S(1)}, u32[]{:S(2)}, u32[]{:S(2)}) collective-permute-start(bf16[768,4,64]{0,2,1:T(8,128)(2,1)} %copy.128), channel_id=1, source_target_pairs={{0,1},{1,2},{2,3},{3,4},{4,5},{5,6},{6,7},{7,0},{8,9},{9,10},{10,1... | collective-permute-start | bytes 1179656 | tf_op jit(solution)/shard_map/while/body/eval_jaxpr/ppermute | solution.py:109
  2092.9 213.9 %collective-permute-start.5 = (f32[768,4,64]{0,2,1:T(8,128)}, f32[768,4,64]{0,2,1:T(8,128)}, u32[]{:S(2)}, u32[]{:S(2)}) collective-permute-start(f32[768,4,64]{0,2,1:T(8,128)} %get-tuple-element.1113), channel_id=1, source_target_pairs={{0,1},{1,2},{2,3},{3,4},{4,5},{5,6},{6,7},{7,0},{8,9},{9,10},{10,1... | collective-permute-start | bytes 2359304 | tf_op jit(solution)/shard_map/while/body/eval_jaxpr/ppermute | solution.py:112
  2364.3 226.5 %collective-permute-start.2 = (bf16[768,4,64]{0,2,1:T(8,128)(2,1)}, bf16[768,4,64]{0,2,1:T(8,128)(2,1)S(1)}, u32[]{:S(2)}, u32[]{:S(2)}) collective-permute-start(bf16[768,4,64]{0,2,1:T(8,128)(2,1)} %copy.128), channel_id=1, source_target_pairs={{0,1},{1,2},{2,3},{3,4},{4,5},{5,6},{6,7},{7,0},{8,9},{9,10},{10,1... | collective-permute-start | bytes 1179656 | tf_op jit(solution)/shard_map/while/body/eval_jaxpr/ppermute | solution.py:109
  2635.6 231.5 %collective-permute-start.3 = (bf16[768,4,64]{0,2,1:T(8,128)(2,1)}, bf16[768,4,64]{0,2,1:T(8,128)(2,1)}, u32[]{:S(2)}, u32[]{:S(2)}) collective-permute-start(bf16[768,4,64]{0,2,1:T(8,128)(2,1)} %copy.129), channel_id=1, source_target_pairs={{0,1},{1,2},{2,3},{3,4},{4,5},{5,6},{6,7},{7,0},{8,9},{9,10},{10,1... | collective-permute-start | bytes 1179656 | tf_op jit(solution)/shard_map/while/body/eval_jaxpr/ppermute | solution.py:110
  2906.9 248.9 %collective-permute-done.4 = f32[768,4,64]{0,2,1:T(8,128)} collective-permute-done((f32[768,4,64]{0,2,1:T(8,128)S(1)}, f32[768,4,64]{0,2,1:T(8,128)}, u32[]{:S(2)}, u32[]{:S(2)}) %collective-permute-start.4) | collective-permute-done | bytes 786464 | tf_op jit(solution)/shard_map/while/body/eval_jaxpr/ppermute | solution.py:111
  3178.4 248.6 %collective-permute-done.4 = f32[768,4,64]{0,2,1:T(8,128)} collective-permute-done((f32[768,4,64]{0,2,1:T(8,128)S(1)}, f32[768,4,64]{0,2,1:T(8,128)}, u32[]{:S(2)}, u32[]{:S(2)}) %collective-permute-start.4) | collective-permute-done | bytes 786464 | tf_op jit(solution)/shard_map/while/body/eval_jaxpr/ppermute | solution.py:111
  3458.9 292.8 %reduce-scatter.2.cloned.1.call-done = f32[1,768,4,64]{1,3,2,0:T(8,128)} async-done(((f32[8,768,4,64]{1,3,2,0:T(8,128)}), f32[1,768,4,64]{1,3,2,0:T(8,128)}) %reduce-scatter.2.cloned.1.call-update) | async-done | bytes 786448 | tf_op jit(solution)/shard_map/reduce_scatter | solution.py:122
  3782.7 33.6 all-reduce.7.cloned.1.call-done
  (265 shorter events, 666.5 us)
Async XLA Ops:
  14.3 3737.4 %reduce-scatter.2.cloned.1.call-start = ((), (), s32[]{:S(2)}) async-start(), calls=%async_computation.1 | async-start | bytes 7077888 | tf_op jit(solution)/shard_map/reduce_scatter | solution.py:122
  1454.6 344.6 %collective-permute-start.4 = (f32[768,4,64]{0,2,1:T(8,128)S(1)}, f32[768,4,64]{0,2,1:T(8,128)}, u32[]{:S(2)}, u32[]{:S(2)}) collective-permute-start(f32[768,4,64]{0,2,1:T(8,128)S(1)} %get-tuple-element.1112), channel_id=1, source_target_pairs={{0,1},{1,2},{2,3},{3,4},{4,5},{5,6},{6,7},{7,0},{8,9},{9,10},{10,1... | collective-permute-start | bytes 2359304 | tf_op jit(solution)/shard_map/while/body/eval_jaxpr/ppermute | solution.py:111
  1454.7 352.9 %collective-permute-start.5 = (f32[768,4,64]{0,2,1:T(8,128)}, f32[768,4,64]{0,2,1:T(8,128)}, u32[]{:S(2)}, u32[]{:S(2)}) collective-permute-start(f32[768,4,64]{0,2,1:T(8,128)} %get-tuple-element.1113), channel_id=1, source_target_pairs={{0,1},{1,2},{2,3},{3,4},{4,5},{5,6},{6,7},{7,0},{8,9},{9,10},{10,1... | collective-permute-start | bytes 2359304 | tf_op jit(solution)/shard_map/while/body/eval_jaxpr/ppermute | solution.py:112
  1454.7 357.1 %collective-permute-start.2 = (bf16[768,4,64]{0,2,1:T(8,128)(2,1)}, bf16[768,4,64]{0,2,1:T(8,128)(2,1)S(1)}, u32[]{:S(2)}, u32[]{:S(2)}) collective-permute-start(bf16[768,4,64]{0,2,1:T(8,128)(2,1)} %copy.128), channel_id=1, source_target_pairs={{0,1},{1,2},{2,3},{3,4},{4,5},{5,6},{6,7},{7,0},{8,9},{9,10},{10,1... | collective-permute-start | bytes 1179656 | tf_op jit(solution)/shard_map/while/body/eval_jaxpr/ppermute | solution.py:109
  1454.8 361.2 %collective-permute-start.3 = (bf16[768,4,64]{0,2,1:T(8,128)(2,1)}, bf16[768,4,64]{0,2,1:T(8,128)(2,1)}, u32[]{:S(2)}, u32[]{:S(2)}) collective-permute-start(bf16[768,4,64]{0,2,1:T(8,128)(2,1)} %copy.129), channel_id=1, source_target_pairs={{0,1},{1,2},{2,3},{3,4},{4,5},{5,6},{6,7},{7,0},{8,9},{9,10},{10,1... | collective-permute-start | bytes 1179656 | tf_op jit(solution)/shard_map/while/body/eval_jaxpr/ppermute | solution.py:110
  1824.8 254.1 %collective-permute-start.5 = (f32[768,4,64]{0,2,1:T(8,128)}, f32[768,4,64]{0,2,1:T(8,128)}, u32[]{:S(2)}, u32[]{:S(2)}) collective-permute-start(f32[768,4,64]{0,2,1:T(8,128)} %get-tuple-element.1113), channel_id=1, source_target_pairs={{0,1},{1,2},{2,3},{3,4},{4,5},{5,6},{6,7},{7,0},{8,9},{9,10},{10,1... | collective-permute-start | bytes 2359304 | tf_op jit(solution)/shard_map/while/body/eval_jaxpr/ppermute | solution.py:112
  2092.9 249.0 %collective-permute-start.4 = (f32[768,4,64]{0,2,1:T(8,128)S(1)}, f32[768,4,64]{0,2,1:T(8,128)}, u32[]{:S(2)}, u32[]{:S(2)}) collective-permute-start(f32[768,4,64]{0,2,1:T(8,128)S(1)} %get-tuple-element.1112), channel_id=1, source_target_pairs={{0,1},{1,2},{2,3},{3,4},{4,5},{5,6},{6,7},{7,0},{8,9},{9,10},{10,1... | collective-permute-start | bytes 2359304 | tf_op jit(solution)/shard_map/while/body/eval_jaxpr/ppermute | solution.py:111
  2092.9 257.4 %collective-permute-start.5 = (f32[768,4,64]{0,2,1:T(8,128)}, f32[768,4,64]{0,2,1:T(8,128)}, u32[]{:S(2)}, u32[]{:S(2)}) collective-permute-start(f32[768,4,64]{0,2,1:T(8,128)} %get-tuple-element.1113), channel_id=1, source_target_pairs={{0,1},{1,2},{2,3},{3,4},{4,5},{5,6},{6,7},{7,0},{8,9},{9,10},{10,1... | collective-permute-start | bytes 2359304 | tf_op jit(solution)/shard_map/while/body/eval_jaxpr/ppermute | solution.py:112
  2364.3 248.7 %collective-permute-start.4 = (f32[768,4,64]{0,2,1:T(8,128)S(1)}, f32[768,4,64]{0,2,1:T(8,128)}, u32[]{:S(2)}, u32[]{:S(2)}) collective-permute-start(f32[768,4,64]{0,2,1:T(8,128)S(1)} %get-tuple-element.1112), channel_id=1, source_target_pairs={{0,1},{1,2},{2,3},{3,4},{4,5},{5,6},{6,7},{7,0},{8,9},{9,10},{10,1... | collective-permute-start | bytes 2359304 | tf_op jit(solution)/shard_map/while/body/eval_jaxpr/ppermute | solution.py:111
  2364.3 257.1 %collective-permute-start.5 = (f32[768,4,64]{0,2,1:T(8,128)}, f32[768,4,64]{0,2,1:T(8,128)}, u32[]{:S(2)}, u32[]{:S(2)}) collective-permute-start(f32[768,4,64]{0,2,1:T(8,128)} %get-tuple-element.1113), channel_id=1, source_target_pairs={{0,1},{1,2},{2,3},{3,4},{4,5},{5,6},{6,7},{7,0},{8,9},{9,10},{10,1... | collective-permute-start | bytes 2359304 | tf_op jit(solution)/shard_map/while/body/eval_jaxpr/ppermute | solution.py:112
  2364.3 261.4 %collective-permute-start.2 = (bf16[768,4,64]{0,2,1:T(8,128)(2,1)}, bf16[768,4,64]{0,2,1:T(8,128)(2,1)S(1)}, u32[]{:S(2)}, u32[]{:S(2)}) collective-permute-start(bf16[768,4,64]{0,2,1:T(8,128)(2,1)} %copy.128), channel_id=1, source_target_pairs={{0,1},{1,2},{2,3},{3,4},{4,5},{5,6},{6,7},{7,0},{8,9},{9,10},{10,1... | collective-permute-start | bytes 1179656 | tf_op jit(solution)/shard_map/while/body/eval_jaxpr/ppermute | solution.py:109
  2635.5 248.8 %collective-permute-start.4 = (f32[768,4,64]{0,2,1:T(8,128)S(1)}, f32[768,4,64]{0,2,1:T(8,128)}, u32[]{:S(2)}, u32[]{:S(2)}) collective-permute-start(f32[768,4,64]{0,2,1:T(8,128)S(1)} %get-tuple-element.1112), channel_id=1, source_target_pairs={{0,1},{1,2},{2,3},{3,4},{4,5},{5,6},{6,7},{7,0},{8,9},{9,10},{10,1... | collective-permute-start | bytes 2359304 | tf_op jit(solution)/shard_map/while/body/eval_jaxpr/ppermute | solution.py:111
  2635.5 257.2 %collective-permute-start.5 = (f32[768,4,64]{0,2,1:T(8,128)}, f32[768,4,64]{0,2,1:T(8,128)}, u32[]{:S(2)}, u32[]{:S(2)}) collective-permute-start(f32[768,4,64]{0,2,1:T(8,128)} %get-tuple-element.1113), channel_id=1, source_target_pairs={{0,1},{1,2},{2,3},{3,4},{4,5},{5,6},{6,7},{7,0},{8,9},{9,10},{10,1... | collective-permute-start | bytes 2359304 | tf_op jit(solution)/shard_map/while/body/eval_jaxpr/ppermute | solution.py:112
  2635.5 261.4 %collective-permute-start.2 = (bf16[768,4,64]{0,2,1:T(8,128)(2,1)}, bf16[768,4,64]{0,2,1:T(8,128)(2,1)S(1)}, u32[]{:S(2)}, u32[]{:S(2)}) collective-permute-start(bf16[768,4,64]{0,2,1:T(8,128)(2,1)} %copy.128), channel_id=1, source_target_pairs={{0,1},{1,2},{2,3},{3,4},{4,5},{5,6},{6,7},{7,0},{8,9},{9,10},{10,1... | collective-permute-start | bytes 1179656 | tf_op jit(solution)/shard_map/while/body/eval_jaxpr/ppermute | solution.py:109
  2635.6 265.6 %collective-permute-start.3 = (bf16[768,4,64]{0,2,1:T(8,128)(2,1)}, bf16[768,4,64]{0,2,1:T(8,128)(2,1)}, u32[]{:S(2)}, u32[]{:S(2)}) collective-permute-start(bf16[768,4,64]{0,2,1:T(8,128)(2,1)} %copy.129), channel_id=1, source_target_pairs={{0,1},{1,2},{2,3},{3,4},{4,5},{5,6},{6,7},{7,0},{8,9},{9,10},{10,1... | collective-permute-start | bytes 1179656 | tf_op jit(solution)/shard_map/while/body/eval_jaxpr/ppermute | solution.py:110
  2906.8 249.0 %collective-permute-start.4 = (f32[768,4,64]{0,2,1:T(8,128)S(1)}, f32[768,4,64]{0,2,1:T(8,128)}, u32[]{:S(2)}, u32[]{:S(2)}) collective-permute-start(f32[768,4,64]{0,2,1:T(8,128)S(1)} %get-tuple-element.1112), channel_id=1, source_target_pairs={{0,1},{1,2},{2,3},{3,4},{4,5},{5,6},{6,7},{7,0},{8,9},{9,10},{10,1... | collective-permute-start | bytes 2359304 | tf_op jit(solution)/shard_map/while/body/eval_jaxpr/ppermute | solution.py:111
  2906.8 257.4 %collective-permute-start.5 = (f32[768,4,64]{0,2,1:T(8,128)}, f32[768,4,64]{0,2,1:T(8,128)}, u32[]{:S(2)}, u32[]{:S(2)}) collective-permute-start(f32[768,4,64]{0,2,1:T(8,128)} %get-tuple-element.1113), channel_id=1, source_target_pairs={{0,1},{1,2},{2,3},{3,4},{4,5},{5,6},{6,7},{7,0},{8,9},{9,10},{10,1... | collective-permute-start | bytes 2359304 | tf_op jit(solution)/shard_map/while/body/eval_jaxpr/ppermute | solution.py:112
  2906.8 261.6 %collective-permute-start.2 = (bf16[768,4,64]{0,2,1:T(8,128)(2,1)}, bf16[768,4,64]{0,2,1:T(8,128)(2,1)S(1)}, u32[]{:S(2)}, u32[]{:S(2)}) collective-permute-start(bf16[768,4,64]{0,2,1:T(8,128)(2,1)} %copy.128), channel_id=1, source_target_pairs={{0,1},{1,2},{2,3},{3,4},{4,5},{5,6},{6,7},{7,0},{8,9},{9,10},{10,1... | collective-permute-start | bytes 1179656 | tf_op jit(solution)/shard_map/while/body/eval_jaxpr/ppermute | solution.py:109
  2906.8 265.8 %collective-permute-start.3 = (bf16[768,4,64]{0,2,1:T(8,128)(2,1)}, bf16[768,4,64]{0,2,1:T(8,128)(2,1)}, u32[]{:S(2)}, u32[]{:S(2)}) collective-permute-start(bf16[768,4,64]{0,2,1:T(8,128)(2,1)} %copy.129), channel_id=1, source_target_pairs={{0,1},{1,2},{2,3},{3,4},{4,5},{5,6},{6,7},{7,0},{8,9},{9,10},{10,1... | collective-permute-start | bytes 1179656 | tf_op jit(solution)/shard_map/while/body/eval_jaxpr/ppermute | solution.py:110
  3178.2 248.7 %collective-permute-start.4 = (f32[768,4,64]{0,2,1:T(8,128)S(1)}, f32[768,4,64]{0,2,1:T(8,128)}, u32[]{:S(2)}, u32[]{:S(2)}) collective-permute-start(f32[768,4,64]{0,2,1:T(8,128)S(1)} %get-tuple-element.1112), channel_id=1, source_target_pairs={{0,1},{1,2},{2,3},{3,4},{4,5},{5,6},{6,7},{7,0},{8,9},{9,10},{10,1... | collective-permute-start | bytes 2359304 | tf_op jit(solution)/shard_map/while/body/eval_jaxpr/ppermute | solution.py:111
  3178.2 257.1 %collective-permute-start.5 = (f32[768,4,64]{0,2,1:T(8,128)}, f32[768,4,64]{0,2,1:T(8,128)}, u32[]{:S(2)}, u32[]{:S(2)}) collective-permute-start(f32[768,4,64]{0,2,1:T(8,128)} %get-tuple-element.1113), channel_id=1, source_target_pairs={{0,1},{1,2},{2,3},{3,4},{4,5},{5,6},{6,7},{7,0},{8,9},{9,10},{10,1... | collective-permute-start | bytes 2359304 | tf_op jit(solution)/shard_map/while/body/eval_jaxpr/ppermute | solution.py:112
  3178.2 261.4 %collective-permute-start.2 = (bf16[768,4,64]{0,2,1:T(8,128)(2,1)}, bf16[768,4,64]{0,2,1:T(8,128)(2,1)S(1)}, u32[]{:S(2)}, u32[]{:S(2)}) collective-permute-start(bf16[768,4,64]{0,2,1:T(8,128)(2,1)} %copy.128), channel_id=1, source_target_pairs={{0,1},{1,2},{2,3},{3,4},{4,5},{5,6},{6,7},{7,0},{8,9},{9,10},{10,1... | collective-permute-start | bytes 1179656 | tf_op jit(solution)/shard_map/while/body/eval_jaxpr/ppermute | solution.py:109
  3178.3 265.5 %collective-permute-start.3 = (bf16[768,4,64]{0,2,1:T(8,128)(2,1)}, bf16[768,4,64]{0,2,1:T(8,128)(2,1)}, u32[]{:S(2)}, u32[]{:S(2)}) collective-permute-start(bf16[768,4,64]{0,2,1:T(8,128)(2,1)} %copy.129), channel_id=1, source_target_pairs={{0,1},{1,2},{2,3},{3,4},{4,5},{5,6},{6,7},{7,0},{8,9},{9,10},{10,1... | collective-permute-start | bytes 1179656 | tf_op jit(solution)/shard_map/while/body/eval_jaxpr/ppermute | solution.py:110
  3458.8 357.6 %all-reduce.7.cloned.1.call-start = ((), (), s32[]{:S(2)}) async-start(), calls=%async_computation.2 | async-start | bytes 2097152 | tf_op jit(solution)/shard_map/psum | solution.py:124
  (40 other events, 2871.2 us)
Sparse Core Ops, SparseCore 0:
  14.4 40.5 all-gather.2
  3458.9 292.7 reduce-scatter.1
  3756.5 59.7 all-reduce.6
where the time goes:
time: 3840 us; the launch traced here: 3830 us
  waiting for transfers between devices  1940 us (51%)
  starting transfers between devices  1250 us (33%)
  local copies, waits for them, and re-layouts  473 us (12%)
  matrix products  58.3 us (2%)
  loops' own time  55.8 us (1%)
    ppermute x7, waiting for transfers between devices, bwd_step(): dk_acc = lax.ppermute(dk_acc, 'cp', shift_pairs)  928 us
    ppermute x7, waiting for transfers between devices, fwd_step(): k_blk = lax.ppermute(k_blk, 'cp', shift_pairs)  524 us
    ppermute x7, starting transfers between devices, bwd_step(): k_blk = lax.ppermute(k_blk, 'cp', shift_pairs)  403 us
    reduce_scatter x1, waiting for transfers between devices, local_fn(): lax.psum_scatter(grad_rel, 'cp', scatter_dimension=0, tiled=False)  293 us
    ppermute x7, starting transfers between devices, bwd_step(): dv_acc = lax.ppermute(dv_acc, 'cp', shift_pairs)  265 us
    ppermute x7, starting transfers between devices, bwd_step(): v_blk = lax.ppermute(v_blk, 'cp', shift_pairs)  239 us
    cond x33, local copies, waits for them, and re-layouts  184 us
    ppermute x7, starting transfers between devices, fwd_step(): v_blk = lax.ppermute(v_blk, 'cp', shift_pairs)  174 us
  transfers between devices with their start and end apart: 47, of which 43 were waited for; matrix products, arithmetic and copies ran while one was open for 6% of the time, Pallas kernels for 0%

commit v1 on v0

v1 whole, which is shorter than its diff:
```python
import functools
import math
import jax
import jax.numpy as jnp
from jax import lax
from jax.experimental import pallas as pl
from jax.experimental.pallas import tpu as pltpu
from jax.sharding import PartitionSpec as P

F32, BF16 = jnp.float32, jnp.bfloat16
LOG2E = math.log2(math.e)
BQ = 256
BK = 512
NC = BK // 128
PAD = 512
MESH_ID = pl.DeviceIdType.MESH


def dot_nn(a, b):
    return lax.dot_general(a, b, (((1,), (0,)), ((), ())), preferred_element_type=F32)


def dot_nt(a, b):
    return lax.dot_general(a, b, (((1,), (1,)), ((), ())), preferred_element_type=F32)


def aligned(x, m):
    return pl.multiple_of(x, m)


def anti_eye(n):
    rows = lax.broadcasted_iota(jnp.int32, (n, n), 0)
    cols = lax.broadcasted_iota(jnp.int32, (n, n), 1)
    return (rows + cols == n - 1).astype(F32).astype(BF16)


def flip_lanes(x, eye):
    n, w = x.shape[1], eye.shape[0]
    parts = [dot_nn(x[:, s:s + w], eye).astype(BF16) for s in range(0, n, w)]
    return jnp.concatenate(parts[::-1], axis=1)


def reverse_rows(x):
    ix = 7 - lax.broadcasted_iota(jnp.int32, (8, x.shape[1]), 0)
    n = x.shape[0] // 8
    return jnp.concatenate([jnp.take_along_axis(x[(n - 1 - g) * 8:(n - g) * 8], ix, axis=0) for g in range(n)], 0)


def owner_core(rb):
    return lax.rem(rb + rb // 2, 2)


def barrier_all(n):
    me, hp = lax.axis_index('cp'), lax.axis_index('hp')
    bar = pltpu.get_barrier_semaphore()
    for o in range(1, n):
        pl.semaphore_signal(bar, 1, device_id=(hp, lax.rem(me + o, n)), device_id_type=MESH_ID)
    pl.semaphore_wait(bar, n - 1)


def gather_kernel(n, q_in, k_in, v_in, do_in, table, w_rel, q_out, do_out, k_out, v_out, r_out,
                  rel_buf, send_d, send_f, send_q, recv_b, recv_q, loc_b, loc_q):
    me, hp = lax.axis_index('cp'), lax.axis_index('hp')
    chip, core = me // 2, lax.rem(me, 2)
    heads, _, blk = q_in.shape
    per_blk = blk // BQ
    nslot = q_out.shape[1] // BQ
    srcs = (k_in, v_in, rel_buf)
    fulls = (k_out, v_out, r_out)
    barrier_all(n)

    def col(t, b):
        b = (n - 1 - b) if t == 2 else b
        return pl.ds(aligned(b * blk, blk), blk)

    def direct(t, i):
        h = lax.rem(chip + i, heads)
        return pltpu.make_async_remote_copy(
            srcs[t].at[h], fulls[t].at[:, col(t, me)], send_d.at[t, i], recv_b.at[t, me],
            device_id=(hp, 2 * h + core), device_id_type=MESH_ID)

    def forward(t, i):
        b = 2 * lax.rem(chip + i, heads) + core
        src = srcs[t].at[chip] if i == 0 else fulls[t].at[:, col(t, b)]
        return pltpu.make_async_remote_copy(
            src, fulls[t].at[:, col(t, b)], send_f.at[t, i], recv_b.at[t, b],
            device_id=(hp, 2 * chip + 1 - core), device_id_type=MESH_ID)

    def wait_block(t, b):
        pltpu.make_async_remote_copy(
            srcs[t].at[0], fulls[t].at[:, col(t, b)], send_f.at[t, 0], recv_b.at[t, b],
            device_id=(hp, me), device_id_type=MESH_ID).wait_recv()

    def own(t):
        return pltpu.make_async_copy(srcs[t].at[chip], fulls[t].at[:, col(t, me)], loc_b.at[t])

    def rows(t, h, j):
        rb = me * per_blk + j
        src = (q_in, do_in)[t].at[h, :, pl.ds(j * BQ, BQ)]
        dst = (q_out, do_out)[t].at[:, pl.ds(aligned(rb // 2 * BQ, BQ), BQ)]
        return rb, src, dst

    def send_rows(t, i, j, wait):
        h = lax.rem(chip + i, heads)
        rb, src, dst = rows(t, h, j)
        to = 2 * h + owner_core(rb)

        @pl.when(to != me)
        def _():
            c = pltpu.make_async_remote_copy(src, dst, send_q.at[t, i, j], recv_q.at[t, rb // 2],
                                             device_id=(hp, to), device_id_type=MESH_ID)
            c.wait_send() if wait else c.start()

        @pl.when(to == me)
        def _():
            c = pltpu.make_async_copy(src, dst, loc_q.at[t, j])
            c.wait() if wait else c.start()

    for t in (0, 1):
        for i in range(1, heads):
            direct(t, i).start()
        forward(t, 0).start()
        own(t).start()
    rel = dot_nt(w_rel[...], table[...]).astype(BF16)
    rel = flip_lanes(rel, anti_eye(256))
    for h in range(heads):
        rel_buf[h] = rel[h * 64:(h + 1) * 64]
    r_out_pad = r_out.at[:, pl.ds(n * blk, PAD)]
    r_out_pad[...] = jnp.zeros(r_out_pad.shape, BF16)
    for i in range(1, heads):
        direct(2, i).start()
    forward(2, 0).start()
    own(2).start()
    for t in (0, 1):
        for i in range(heads):
            for j in range(per_blk):
                send_rows(t, i, j, False)
    for t in range(3):
        for i in range(1, heads):
            wait_block(t, 2 * lax.rem(chip + i, heads) + core)
            forward(t, i).start()
    for t in range(3):
        own(t).wait()
        for i in range(heads):
            wait_block(t, 2 * i + 1 - core)
            forward(t, i).wait_send()
            if i:
                direct(t, i).wait_send()
    for t in (0, 1):
        for k in range(nslot):
            rb = 2 * k + lax.rem(k + core, 2)

            @pl.when(rb // per_blk != me)
            def _():
                dst = (q_out, do_out)[t].at[:, pl.ds(k * BQ, BQ)]
                pltpu.make_async_remote_copy(
                    (q_in, do_in)[t].at[0, :, pl.ds(0, BQ)], dst, send_q.at[t, 0, 0], recv_q.at[t, k],
                    device_id=(hp, me), device_id_type=MESH_ID).wait_recv()
        for i in range(heads):
            for j in range(per_blk):
                send_rows(t, i, j, True)


def attention_kernel(qT, doT, kT, vT, relF, ub, vb, oT, dqT, dkT, dvT, drF, du, dv, s_scr, r_scr, q_scr):
    me = lax.axis_index('cp')
    chip, core = me // 2, lax.rem(me, 2)
    dim, seq = kT.shape
    nslot = seq // BQ // 2
    scale = dim ** -0.5
    for ref in (dkT, dvT, drF, du, dv):
        ref[...] = jnp.zeros_like(ref)
    eye = anti_eye(BQ)

    def bias_col(ref):
        pick = lax.broadcasted_iota(jnp.int32, ref.shape, 0) == chip
        row = jnp.sum(jnp.where(pick, ref[...], 0.0), axis=0, keepdims=True)
        return jnp.broadcast_to(row, (128, dim)).T[:, :1]

    u_col, v_col = bias_col(ub), bias_col(vb)

    def row_block(k, _):
        rb = 2 * k + lax.rem(k + core, 2)
        tiles = (rb + 2) // 2
        i0 = rb * BQ
        qs = pl.ds(aligned(k * BQ, BQ), BQ)
        q = qT[:, qs].astype(F32)
        quT, qvT = (q + u_col).astype(BF16), (q + v_col).astype(BF16)
        qv = qvT.astype(F32).T.astype(BF16)
        quTr, qvTr, doTr = (flip_lanes(x, eye) for x in (quT, qvT, doT[:, qs]))
        qur, dor = quTr.astype(F32).T.astype(BF16), doTr.astype(F32).T.astype(BF16)
        q_scr[0], q_scr[1], q_scr[2] = qv, qur, dor
        base = seq - i0
        lane = lax.broadcasted_iota(jnp.int32, (128, 128), 1)
        row = lax.broadcasted_iota(jnp.int32, (128, 128), 0)
        past = lane > row

        def skew(t):
            return pltpu.roll(t, 1, 1, stride=1, stride_axis=0)

        t0 = dot_nn(qv, relF[:, pl.ds(aligned(base - 256, 128), 256)])
        r_scr[:, :128], r_scr[:, 128:] = skew(t0[:, :128]), skew(t0[:, 128:])

        def scores(t, mx, last):
            j0 = aligned(t * BK, BK)
            by_offset = dot_nn(q_scr[0], relF[:, pl.ds(aligned(base + j0, 128), BK)])
            content = dot_nn(q_scr[1], kT[:, pl.ds(j0, BK)])
            rolled = [r_scr[:, :128], r_scr[:, 128:]]
            rolled += [skew(by_offset[:, m * 128:(m + 1) * 128]) for m in range(NC)]
            for m in range(NC):
                top = jnp.where(past, rolled[m + 2][:128], rolled[m + 1][:128])
                bot = jnp.where(past, rolled[m + 1][128:], rolled[m][128:])
                s = content[:, m * 128:(m + 1) * 128] + reverse_rows(jnp.concatenate([top, bot], 0))
                s = s * (scale * LOG2E)
                if last:
                    ip = i0 + BQ - 1 - lax.broadcasted_iota(jnp.int32, (BQ, 128), 0)
                    jp = j0 + m * 128 + lax.broadcasted_iota(jnp.int32, (BQ, 128), 1)
                    s = jnp.where(jp > ip, -jnp.inf, s)
                s_scr[t, :, m * 128:(m + 1) * 128] = s
                mx = jnp.maximum(mx, s)
            r_scr[:, :128], r_scr[:, 128:] = rolled[NC], rolled[NC + 1]
            return mx

        mx = jnp.full((BQ, 128), -jnp.inf, F32)
        mx = lax.fori_loop(0, tiles - 1, lambda t, mx: scores(t, mx, False), mx)
        mx = jnp.max(scores(tiles - 1, mx, True), axis=1, keepdims=True)

        def weigh(t, carry):
            total, out = carry
            parts = []
            for m in range(NC):
                p = jnp.exp2(s_scr[t, :, m * 128:(m + 1) * 128] - mx)
                s_scr[t, :, m * 128:(m + 1) * 128] = p
                total = total + p
                parts.append(p.astype(BF16))
            out = out + dot_nt(jnp.concatenate(parts, 1), vT[:, pl.ds(aligned(t * BK, BK), BK)])
            return total, out

        total, out = lax.fori_loop(0, tiles, weigh, (jnp.zeros((BQ, 128), F32), jnp.zeros((BQ, dim), F32)))
        inv = 1.0 / jnp.sum(total, axis=1, keepdims=True)
        out = out * inv
        delta = jnp.sum(q_scr[2].astype(F32) * out, axis=1, keepdims=True)
        oT[:, qs] = flip_lanes(out.T.astype(BF16), eye)

        before = lane < row
        none = jnp.zeros((BQ, 128), BF16)

        def unskew(held, m):
            top = jnp.where(before, held[m + 1][:128], held[m + 2][:128])
            bot = jnp.where(before, held[m][128:], held[m + 1][128:])
            return jnp.concatenate([top, bot], 0)

        def offset_grads(by_offset, us, gv):
            drF[:, us] += dot_nn(qvTr, by_offset)
            return gv + dot_nt(by_offset, relF[:, us])

        def grads(t, carry):
            gu, gv, held_a, held_b = carry
            j0 = aligned(t * BK, BK)
            js = pl.ds(j0, BK)
            dp = dot_nn(q_scr[2], vT[:, js])
            ps, dss, held = [], [], [held_a, held_b]
            for m in range(NC):
                p = s_scr[t, :, m * 128:(m + 1) * 128] * inv
                ds = (p * ((dp[:, m * 128:(m + 1) * 128] - delta) * scale)).astype(BF16)
                ps.append(p.astype(BF16))
                dss.append(ds)
                held.append(pltpu.roll(ds, 0, 1, stride=1, stride_axis=0))
            p_all, ds_all = jnp.concatenate(ps, 1), jnp.concatenate(dss, 1)
            dvT[:, js] += dot_nn(doTr, p_all)
            dkT[:, js] += dot_nn(quTr, ds_all)
            gu = gu + dot_nt(ds_all, kT[:, js])
            by_offset = jnp.concatenate([unskew(held, m) for m in range(NC)], 1)
            gv = offset_grads(by_offset, pl.ds(aligned(base + j0 - 256, 128), BK), gv)
            return gu, gv, held[NC], held[NC + 1]

        zero = jnp.zeros((BQ, dim), F32)
        gu, gv, held_a, held_b = lax.fori_loop(0, tiles, grads, (zero, zero, none, none))
        held = [held_a, held_b, none, none]
        rest = jnp.concatenate([unskew(held, 0), unskew(held, 1)], 1)
        gv = offset_grads(rest, pl.ds(aligned(base + tiles * BK - 256, 128), 256), gv)
        dqT[:, qs] = flip_lanes((gu + gv).T.astype(BF16), eye)
        du[...] += jnp.sum(gu.reshape(BQ // 8, 8, dim), axis=0)
        dv[...] += jnp.sum(gv.reshape(BQ // 8, 8, dim), axis=0)
        return 0

    lax.fori_loop(0, nslot, row_block, 0)


def scatter_kernel(n, oT, dqT, dkT, dvT, drF, du, dv, table, o_out, dq_out, dk_out, dv_out, bias_out, dw_out,
                   pair_buf, send_buf, dr_buf, bias_buf, half_in, half_sum, part_in, w_acc,
                   send_p, recv_p, send_q, recv_q, loc_q, send_s, recv_s, send_b, recv_b, send_w, recv_w):
    me, hp = lax.axis_index('cp'), lax.axis_index('hp')
    chip, core = me // 2, lax.rem(me, 2)
    mate = 2 * chip + 1 - core
    heads, dim, blk = o_out.shape
    per_blk = blk // BQ
    nslot = oT.shape[1] // BQ
    parts = (dkT, dvT, drF)
    sinks = (dk_out, dv_out, dr_buf)

    def remote(src, dst, ss, rs, to):
        return pltpu.make_async_remote_copy(src, dst, ss, rs, device_id=(hp, to), device_id_type=MESH_ID)

    def col(t, b):
        b = (n - 1 - b) if t == 2 else b
        return pl.ds(aligned(b * blk, blk), blk)

    bias_buf[me, 0] = jnp.sum(du[...], axis=0, keepdims=True) + jnp.zeros((8, dim), F32)
    bias_buf[me, 1] = jnp.sum(dv[...], axis=0, keepdims=True) + jnp.zeros((8, dim), F32)
    barrier_all(n)

    def pair(t, i):
        return remote(parts[t].at[:, col(t, 2 * i + 1 - core)], pair_buf.at[t, i], send_p.at[t, i], recv_p.at[t, i], mate)

    for t in (2, 0, 1):
        for i in range(heads):
            pair(t, i).start()

    def rows(t, k, wait):
        rb = 2 * k + lax.rem(k + core, 2)
        to = rb // per_blk
        src = (oT, dqT)[t].at[:, pl.ds(k * BQ, BQ)]
        dst = (o_out, dq_out)[t].at[chip, :, pl.ds(aligned(lax.rem(rb, per_blk) * BQ, BQ), BQ)]

        @pl.when(to != me)
        def _():
            c = remote(src, dst, send_q.at[t, k], recv_q.at[t, chip, lax.rem(rb, per_blk)], to)
            c.wait_send() if wait else c.start()

        @pl.when(to == me)
        def _():
            c = pltpu.make_async_copy(src, dst, loc_q.at[t, lax.rem(rb, per_blk)])
            c.wait() if wait else c.start()

    def bias(o):
        return remote(bias_buf.at[me], bias_buf.at[me], send_b.at[o], recv_b.at[me], lax.rem(me + o, n))

    for o in range(1, n):
        bias(o).start()

    def sink(t, i):
        b = lax.rem(chip + i, heads)
        return remote(send_buf.at[t, b], sinks[t].at[chip], send_s.at[t, i], recv_s.at[t, chip], 2 * b + core)

    def combine(t):
        for i in (1, 2, 3, 0):
            b = lax.rem(chip + i, heads)
            remote(parts[t].at[:, col(t, 2 * b + core)], pair_buf.at[t, b], send_p.at[t, 0], recv_p.at[t, b], mate).wait_recv()
            both = (parts[t][:, col(t, 2 * b + core)] + pair_buf[t, b]).astype(BF16)
            if i:
                send_buf[t, b] = both
                sink(t, i).start()
            else:
                sinks[t][chip] = both

    combine(2)
    for k in range(nslot):
        rows(0, k, False)
    for k in range(nslot):
        rows(1, k, False)
    combine(0)
    combine(1)
    for i in range(1, heads):
        h = lax.rem(chip + i, heads)
        remote(send_buf.at[2, 0], dr_buf.at[h], send_s.at[2, 0], recv_s.at[2, h], me).wait_recv()
    eye = anti_eye(256)
    for h in range(heads):
        w_acc[h * dim:(h + 1) * dim] = dot_nn(flip_lanes(dr_buf[h], eye), table[...])
    half = heads * dim // 2
    piece = half // heads

    def swap():
        return remote(w_acc.at[pl.ds(aligned((1 - core) * half, half), half)], half_in, send_w.at[0], recv_w.at[0], mate)

    swap().start()
    swap().wait()
    half_sum[...] = w_acc[pl.ds(aligned(core * half, half), half)] + half_in[...]

    def spread(i):
        z = lax.rem(chip + i, heads)
        return remote(half_sum.at[pl.ds(aligned(z * piece, piece), piece)], part_in.at[i], send_w.at[i], recv_w.at[i], 2 * z + core)

    for i in range(1, heads):
        spread(i).start()
    for i in range(1, heads):
        spread(i).wait()
    mine = half_sum[pl.ds(aligned(chip * piece, piece), piece)]
    for i in range(1, heads):
        mine = mine + part_in[i]
    half_in[pl.ds(0, piece)] = mine

    def place(c, z):
        return dw_out.at[pl.ds(aligned(c * half + z * piece, piece), piece)]

    def collect(i):
        z = lax.rem(chip + i, heads)
        return remote(half_in.at[pl.ds(0, piece)], place(core, chip), send_w.at[4 + i], recv_w.at[4 + chip], 2 * z + core)

    def hand_over(i):
        z = lax.rem(chip + i, heads)
        src = half_in.at[pl.ds(0, piece)] if i == 0 else place(core, z)
        return remote(src, place(core, z), send_w.at[8 + i], recv_w.at[8 + z], mate)

    for i in range(1, heads):
        collect(i).start()
    hand_over(0).start()
    place(core, chip)[...] = mine
    for i in range(1, heads):
        z = lax.rem(chip + i, heads)
        remote(half_in.at[pl.ds(0, piece)], place(core, z), send_w.at[0], recv_w.at[4 + z], me).wait_recv()
        hand_over(i).start()
    for o in range(1, n):
        b = lax.rem(me + o, n)
        remote(bias_buf.at[b], bias_buf.at[b], send_b.at[0], recv_b.at[b], me).wait_recv()
    for h in range(heads):
        bias_out[h] = bias_buf[2 * h] + bias_buf[2 * h + 1]
    for i in range(heads):
        remote(half_in.at[pl.ds(0, piece)], place(1 - core, i), send_w.at[0], recv_w.at[8 + i], me).wait_recv()
        hand_over(i).wait_send()
        if i:
            collect(i).wait_send()
    for o in range(1, n):
        bias(o).wait_send()
    for t in range(3):
        for i in range(heads):
            pair(t, i).wait_send()
            if i:
                h = lax.rem(chip + i, heads)
                sink(t, i).wait_send()
                if t < 2:
                    remote(send_buf.at[t, 0], sinks[t].at[h], send_s.at[t, 0], recv_s.at[t, h], me).wait_recv()
    for t in (0, 1):
        for k in range(nslot):
            rows(t, k, True)
        for h in range(heads):
            for j in range(per_blk):
                rb = me * per_blk + j

                @pl.when(2 * h + owner_core(rb) != me)
                def _():
                    remote((oT, dqT)[t].at[:, pl.ds(0, BQ)], (o_out, dq_out)[t].at[h, :, pl.ds(j * BQ, BQ)],
                           send_q.at[t, 0], recv_q.at[t, h, j], me).wait_recv()


def solution(mesh):
    n = mesh.shape['cp']
    seq_spec, head_spec, weight_spec = P('cp', 'hp', None), P('hp', None), P(None, 'hp', None)
    vmem = pl.BlockSpec(memory_space=pltpu.VMEM)
    hbm = pl.BlockSpec(memory_space=pl.ANY)
    dma, sds = pltpu.SemaphoreType.DMA, jax.ShapeDtypeStruct

    def local_fn(q, k, v, u_bias, v_bias, rel_table, w_rel, d_out):
        blk, heads, dim = q.shape
        seq = n * blk
        rows = seq // 2
        nslot = rows // BQ
        per_blk = blk // BQ
        qT, kT, vT, doT = (x.transpose(1, 2, 0) for x in (q, k, v, d_out))
        wT = w_rel.transpose(1, 2, 0).reshape(heads * dim, -1)
        model = wT.shape[1]
        q_h, do_h, k_h, v_h, r_h = pl.pallas_call(
            functools.partial(gather_kernel, n),
            out_shape=[sds((dim, rows), BF16), sds((dim, rows), BF16), sds((dim, seq), BF16), sds((dim, seq), BF16),
                       sds((dim, seq + PAD), BF16)],
            in_specs=[vmem] * 6, out_specs=[vmem] * 5,
            scratch_shapes=[pltpu.VMEM((heads, dim, blk), BF16), dma((3, heads)), dma((3, heads)), dma((2, heads, per_blk)),
                            dma((3, n)), dma((2, nslot)), dma((3,)), dma((2, per_blk))],
            compiler_params=pltpu.CompilerParams(collective_id=0, has_side_effects=True),
            name='gather_heads',
        )(qT, kT, vT, doT, rel_table, wT)
        oT, dqT, dkT, dvT, drF, du, dv = pl.pallas_call(
            attention_kernel,
            out_shape=[sds((dim, rows), BF16), sds((dim, rows), BF16), sds((dim, seq), F32), sds((dim, seq), F32),
                       sds((dim, seq + PAD), F32), sds((8, dim), F32), sds((8, dim), F32)],
            in_specs=[vmem] * 7, out_specs=[vmem] * 7,
            scratch_shapes=[pltpu.VMEM((seq // BK, BQ, BK), F32), pltpu.VMEM((BQ, 256), F32), pltpu.VMEM((3, BQ, dim), BF16)],
            compiler_params=pltpu.CompilerParams(vmem_limit_bytes=56 << 20),
            name='attention',
        )(q_h, do_h, k_h, v_h, r_h, u_bias, v_bias)
        o, dq, dk, dvv, bias, dw = pl.pallas_call(
            functools.partial(scatter_kernel, n),
            out_shape=[sds((heads, dim, blk), BF16)] * 4 + [sds((heads, 2, 8, dim), F32), sds((heads * dim, model), F32)],
            in_specs=[vmem] * 8, out_specs=[vmem] * 6,
            scratch_shapes=[pltpu.VMEM((3, heads, dim, blk), F32), pltpu.VMEM((3, heads, dim, blk), BF16),
                            pltpu.VMEM((heads, dim, blk), BF16), pltpu.VMEM((n, 2, 8, dim), F32),
                            pltpu.VMEM((heads * dim // 2, model), F32), pltpu.VMEM((heads * dim // 2, model), F32),
                            pltpu.VMEM((heads, heads * dim // 8, model), F32), pltpu.VMEM((heads * dim, model), F32),
                            dma((3, heads)), dma((3, heads)), dma((2, nslot)), dma((2, heads, per_blk)), dma((2, per_blk)),
                            dma((3, heads)), dma((3, heads)), dma((n,)), dma((n,)), dma((12,)), dma((12,))],
            compiler_params=pltpu.CompilerParams(collective_id=1, has_side_effects=True, vmem_limit_bytes=56 << 20),
            name='scatter_rows',
        )(oT, dqT, dkT, dvT, drF, du, dv, rel_table)
        back = lambda x: x.transpose(2, 0, 1)
        return (back(o), back(dq), back(dk), back(dvv), bias[:, 0, 0], bias[:, 1, 0],
                back(dw.reshape(heads, dim, model)))

    return jax.shard_map(
        local_fn, mesh=mesh,
        in_specs=(seq_spec, seq_spec, seq_spec, head_spec, head_spec, P('cp', None), weight_spec, seq_spec),
        out_specs=(seq_spec, seq_spec, seq_spec, seq_spec, head_spec, head_spec, weight_spec),
        check_vma=False,
    )
```

time: 3840 us -> 248 us (0.06)
  waiting for transfers between devices: 1940 us -> 0 us
  starting transfers between devices: 1250 us -> 0 us
  local copies, waits for them, and re-layouts: 473 us -> 7.48 us
  Pallas kernels: 0 us -> 238 us
  matrix products: 58.3 us -> 0 us
  loops' own time: 55.8 us -> 0 us
    ppermute x44 -> x0, waiting for transfers between devices: 1570 us -> none  [the longest x7 928 us: bwd_step(): dk_acc = lax.ppermute(dk_acc, 'cp', shift_pairs)]
    ppermute x44 -> x0, starting transfers between devices: 1250 us -> none  [the longest x7 403 us: bwd_step(): k_blk = lax.ppermute(k_blk, 'cp', shift_pairs)]
    reduce_scatter x1 -> x0, waiting for transfers between devices: 293 us -> none  [local_fn(): lax.psum_scatter(grad_rel, 'cp', scatter_dimension=0, tiled=False)]
    pallas_call x0 -> x3, Pallas kernels: none -> 238 us  [the longest x1 108 us: local_fn(): pl.pallas_call(attention_kernel, out_shape=[sds((dim, rows), BF16), sds((...]
    cond x33 -> x0, local copies, waits for them, and re-layouts: 184 us -> none
    reshape x3 -> x0, local copies, waits for them, and re-layouts: 77.8 us -> none  [the longest x2 58.8 us: skew_scores(): kept_view.reshape(lead_dims + (block_len, 2 * block_len - 1))]
    dot_general x12 -> x0, matrix products: 56.7 us -> none  [the longest x2 17.8 us: block_scores(): jnp.einsum('qhd,shd->hqs', q_v, window, preferred_element_type=jnp.float32)]
    another operation x18 -> x0, loops' own time: 55.8 us -> none  [the longest x1 27.6 us: local_fn(): lax.fori_loop(0, last_step, fwd_step, (k, v, run_stats))]
  transfers between devices with their start and end apart: 47 -> 0, of which waited for: 43 -> 0; matrix products, arithmetic and copies ran while one was open for 6% -> 0% of each run, Pallas kernels for 0% -> 0%
where the time goes in v1:
time: 248 us; the launch traced here: 246 us
  Pallas kernels  238 us (96%)
  local copies, waits for them, and re-layouts  7.48 us (3%)
    pallas_call x1, Pallas kernels, local_fn(): pl.pallas_call(attention_kernel, out_shape=[sds((dim, rows), BF16), sds((...  108 us
    pallas_call x1, Pallas kernels, local_fn(): pl.pallas_call(functools.partial(scatter_kernel, n), out_shape=[sds((head...  79.6 us
    pallas_call x1, Pallas kernels, local_fn(): pl.pallas_call(functools.partial(gather_kernel, n), out_shape=[sds((dim,...  50.1 us
    unnamed x11, local copies, waits for them, and re-layouts  6.09 us

profile of v1, /device:TPU:0, one launch (start us, length us, event | category | flops | bytes accessed | tf_op | source)
XLA Modules:
  0.0 246.2 jit_solution(11518977420988581948)
XLA Ops:
  0.6 50.1 %gather_heads.1 = (bf16[64,3072]{1,0:T(8,128)(2,1)}, bf16[64,3072]{1,0:T(8,128)(2,1)}, bf16[64,6144]{1,0:T(8,128)(2,1)}, bf16[64,6144]{1,0:T(8,128)(2,1)}, bf16[64,6656]{1,0:T(8,128)(2,1)}) custom-call(bf16[4,64,768]{2,1,0:T(8,128)(2,1)} %bitcast.18, bf16[4,64,768]{2,1,0:T(8,128)(2,1)} %bitcast.19, bf16[4,64,768]{2,1,0:T(8,128)(2,1)} %bitcast.20, ...), custom_call_target="tpu_custom_call" | custom-call | tf_op jit(solution)/shard_map/gather_heads/pallas_call | solution.py:461
  50.7 108.3 %attention.1 = (bf16[64,3072]{1,0:T(8,128)(2,1)}, bf16[64,3072]{1,0:T(8,128)(2,1)}, f32[64,6144]{1,0:T(8,128)}, f32[64,6144]{1,0:T(8,128)}, f32[64,6656]{1,0:T(8...) custom-call(bf16[64,3072]{1,0:T(8,128)(2,1)} %get-tuple-element.25.qT, bf16[64,3072]{1,0:T(8,128)(2,1)} %get-tuple-element.26.doT, ...), custom_call_target="tpu_custom_call" | custom-call | tf_op jit(solution)/shard_map/attention/pallas_call | solution.py:471
  159.0 79.6 %scatter_rows.1 = (bf16[4,64,768]{2,1,0:T(8,128)(2,1)}, bf16[4,64,768]{2,1,0:T(8,128)(2,1)}, bf16[4,64,768]{2,1,0:T(8,128)(2,1)}, bf16[4,64,768]{2,1,0:T(8,128)(...) custom-call(bf16[64,3072]{1,0:T(8,128)(2,1)} %get-tuple-element.30.oT, bf16[64,3072]{1,0:T(8,128)(2,1)} %get-tuple-element.31.dqT, ...), custom_call_target="tpu_custom_call" | custom-call | tf_op jit(solution)/shard_map/scatter_rows/pallas_call | solution.py:480
  238.6 0.0 copy-start.2
  238.7 0.0 copy-start.1
  238.7 1.4 fusion
  240.1 0.0 copy-start
  240.1 1.9 copy.20
  241.9 1.8 copy.21
  243.7 0.0 copy-done.2
  243.7 0.7 copy.22
  244.4 0.0 copy-done.1
  244.4 0.7 copy.23
  245.2 0.0 copy-done
  245.2 1.0 copy.24
Async XLA Ops:
  238.6 5.0 %copy-start.2 = (bf16[4,64,768]{2,1,0:T(8,128)(2,1)S(1)}, bf16[4,64,768]{2,1,0:T(8,128)(2,1)}, u32[]{:S(2)}) copy-start(bf16[4,64,768]{2,1,0:T(8,128)(2,1)} %get-tuple-element.39) | copy-start | bytes 1179652
  238.7 5.8 %copy-start.1 = (bf16[4,64,768]{2,1,0:T(8,128)(2,1)S(1)}, bf16[4,64,768]{2,1,0:T(8,128)(2,1)}, u32[]{:S(2)}) copy-start(bf16[4,64,768]{2,1,0:T(8,128)(2,1)} %get-tuple-element.40) | copy-start | bytes 1179652
  240.1 5.1 %copy-start = (f32[256,1024]{1,0:T(8,128)S(1)}, f32[256,1024]{1,0:T(8,128)}, u32[]{:S(2)}) copy-start(f32[256,1024]{1,0:T(8,128)} %get-tuple-element.42) | copy-start | bytes 3145732

commit v2 on v0

v2 whole, which is shorter than its diff:
```python
import functools
import math
import jax
import jax.numpy as jnp
from jax import lax
from jax.experimental import pallas as pl
from jax.experimental.pallas import tpu as pltpu
from jax.sharding import PartitionSpec as P

F32, BF16 = jnp.float32, jnp.bfloat16
LOG2E = math.log2(math.e)
BQ = 256
BK = 512
NC = BK // 128
PAD = 512
KX = 80
GROUP = 3
UNROLL = 3
MESH_ID = pl.DeviceIdType.MESH


def dot_nn(a, b):
    return lax.dot_general(a, b, (((1,), (0,)), ((), ())), preferred_element_type=F32)


def dot_nt(a, b):
    return lax.dot_general(a, b, (((1,), (1,)), ((), ())), preferred_element_type=F32)


def aligned(x, m):
    return pl.multiple_of(x, m)


def anti_eye(n):
    rows = lax.broadcasted_iota(jnp.int32, (n, n), 0)
    cols = lax.broadcasted_iota(jnp.int32, (n, n), 1)
    return (rows + cols == n - 1).astype(F32).astype(BF16)


def flip_lanes(x, eye):
    n, w = x.shape[1], eye.shape[0]
    parts = [dot_nn(x[:, s:s + w], eye).astype(BF16) for s in range(0, n, w)]
    return jnp.concatenate(parts[::-1], axis=1)


def reverse_rows(x):
    ix = 7 - lax.broadcasted_iota(jnp.int32, (8, x.shape[1]), 0)
    n = x.shape[0] // 8
    return jnp.concatenate([jnp.take_along_axis(x[(n - 1 - g) * 8:(n - g) * 8], ix, axis=0) for g in range(n)], 0)


def owner_core(rb):
    return lax.rem(rb + rb // 2, 2)


def remote_copy(src, dst, send_sem, recv_sem, to):
    return pltpu.make_async_remote_copy(src, dst, send_sem, recv_sem, device_id=(lax.axis_index('hp'), to),
                                        device_id_type=MESH_ID)


def barrier_all(n):
    me, hp = lax.axis_index('cp'), lax.axis_index('hp')
    bar = pltpu.get_barrier_semaphore()
    for o in range(1, n):
        pl.semaphore_signal(bar, 1, device_id=(hp, lax.rem(me + o, n)), device_id_type=MESH_ID)
    pl.semaphore_wait(bar, n - 1)


def rel_kernel(table, w_rel, out):
    rel = dot_nt(w_rel[...], table[...]).astype(BF16)
    rel = flip_lanes(rel, anti_eye(256))
    heads, dim, _ = out.shape
    for h in range(heads):
        out[h] = rel[h * dim:(h + 1) * dim]


def attention_kernel(n, q_in, k_in, v_in, do_in, r_in, ub, vb,
                     o_out, dq_out, dk_out, dv_out, dr_out, du, dv,
                     qT, doT, kT, vT, relX, oT, dqT, dkT, dvT, drF,
                     s_all, q_off, q_row, do_row, q_col, qo_col, do_col, mx, total, o_acc, gu, gv, r_scr, h_scr,
                     pair_buf, send_buf,
                     send_d, send_f, send_q, recv_b, recv_q, loc_b, loc_q,
                     send_o, recv_o, loc_o, send_p, recv_p, send_s, recv_s, loc_s):
    me = lax.axis_index('cp')
    chip, core = me // 2, lax.rem(me, 2)
    mate = 2 * chip + 1 - core
    heads, dim, blk = q_in.shape
    seq = n * blk
    per_blk = blk // BQ
    groups = n // 2
    nslot = qT.shape[1] // BQ
    scale = dim ** -0.5
    barrier_all(n)

    srcs, fulls = (r_in, k_in, v_in), (relX, kT, vT)

    def col(t, b, flipped):
        b = (n - 1 - b) if t == flipped else b
        return pl.ds(aligned(b * blk, blk), blk)

    def full_at(t, b):
        return fulls[t].at[pl.ds(0, dim), col(t, b, 0)]

    def direct(t, i):
        h = lax.rem(chip + i, heads)
        return remote_copy(srcs[t].at[h], full_at(t, me), send_d.at[t, i], recv_b.at[t, me], 2 * h + core)

    def own(t):
        return pltpu.make_async_copy(srcs[t].at[chip], full_at(t, me), loc_b.at[t])

    def to_mate(t):
        return remote_copy(srcs[t].at[chip], full_at(t, me), send_f.at[t, chip], recv_b.at[t, me], mate)

    def forward(t, g):
        b = 2 * g + core
        return remote_copy(full_at(t, b), full_at(t, b), send_f.at[t, g], recv_b.at[t, b], mate)

    def landed(t, b):
        remote_copy(srcs[t].at[0], full_at(t, b), send_f.at[t, 0], recv_b.at[t, b], me).wait_recv()

    def pass_on(t, g):
        @pl.when(g != chip)
        def _():
            landed(t, 2 * g + core)
            forward(t, g).start()

        @pl.when(g == chip)
        def _():
            own(t).wait()

    def from_mate(t, g):
        landed(t, 2 * g + 1 - core)

    def row_copy(t, i, j, wait):
        h = lax.rem(chip + i, heads)
        rb = me * per_blk + j
        src = (q_in, do_in)[t].at[h, :, pl.ds(j * BQ, BQ)]
        dst = (qT, doT)[t].at[:, pl.ds(aligned(rb // 2 * BQ, BQ), BQ)]
        to = 2 * h + owner_core(rb)

        @pl.when(to != me)
        def _():
            c = remote_copy(src, dst, send_q.at[t, i, j], recv_q.at[t, rb // 2], to)
            c.wait_send() if wait else c.start()

        @pl.when(to == me)
        def _():
            c = pltpu.make_async_copy(src, dst, loc_q.at[t, j])
            c.wait() if wait else c.start()

    def row_block(k):
        return 2 * k + lax.rem(k + core, 2)

    def row_landed(t, k):
        src = (q_in, do_in)[t].at[0, :, pl.ds(0, BQ)]
        dst = (qT, doT)[t].at[:, pl.ds(aligned(k * BQ, BQ), BQ)]
        rb = row_block(k)

        @pl.when(rb // per_blk != me)
        def _():
            remote_copy(src, dst, send_q.at[t, 0, 0], recv_q.at[t, k], me).wait_recv()

        @pl.when(rb // per_blk == me)
        def _():
            pltpu.make_async_copy(src, dst, loc_q.at[t, lax.rem(rb, per_blk)]).wait()

    order = (1, 3, 2)
    for t in (0, 1):
        to_mate(t).start()
        own(t).start()
    for i in order:
        direct(0, i).start()
        direct(1, i).start()
        for j in range(per_blk):
            row_copy(0, i, j, False)
    for j in range(per_blk):
        row_copy(0, 0, j, False)
    to_mate(2).start()
    own(2).start()
    for i in order:
        direct(2, i).start()
    for i in order + (0,):
        for j in range(per_blk):
            row_copy(1, i, j, False)

    for ref in (dkT, dvT, drF, du, dv, total, o_acc, h_scr):
        ref[...] = jnp.zeros_like(ref)
    mx[...] = jnp.full(mx.shape, -jnp.inf, F32)
    relX[pl.ds(0, dim), pl.ds(seq, PAD)] = jnp.zeros((dim, PAD), BF16)
    first = lax.broadcasted_iota(jnp.int32, (KX - dim, PAD), 0) == 0
    relX[pl.ds(dim, KX - dim), pl.ds(0, seq)] = jnp.zeros((KX - dim, seq), BF16)
    relX[pl.ds(dim, KX - dim), pl.ds(seq, PAD)] = jnp.where(first, -jnp.inf, 0.0).astype(BF16)
    ones_col = (lax.broadcasted_iota(jnp.int32, (BQ, KX - dim), 1) == 0).astype(F32).astype(BF16)
    eye = anti_eye(BQ)
    lane = lax.broadcasted_iota(jnp.int32, (128, 128), 1)
    row = lax.broadcasted_iota(jnp.int32, (128, 128), 0)
    past, before = lane > row, lane < row

    def bias_col(ref):
        pick = lax.broadcasted_iota(jnp.int32, ref.shape, 0) == chip
        r = jnp.sum(jnp.where(pick, ref[...], 0.0), axis=0, keepdims=True)
        return jnp.broadcast_to(r, (128, dim)).T[:, :1]

    u_col, v_col = bias_col(ub), bias_col(vb)

    def skew(t):
        return pltpu.roll(t, 1, 1, stride=1, stride_axis=0)

    def slot_cols(k):
        return pl.ds(aligned(k * BQ, BQ), BQ)

    def transposed(x):
        return x.astype(F32).T.astype(BF16)

    def prepare(k, i):
        q = qT[:, slot_cols(k)].astype(F32)
        quT, qvT = (q + u_col).astype(BF16), (q + v_col).astype(BF16)
        q_off[k] = jnp.concatenate([transposed(qvT), ones_col], 1)
        q_col[k] = flip_lanes(quT, eye)
        q_row[k] = transposed(q_col[k])
        qo_col[k] = flip_lanes(qvT, eye)
        base = seq - row_block(k) * BQ
        t0 = dot_nn(q_off[k], relX[:, pl.ds(aligned(base - 256, 128), 256)])
        r_scr[i, :, :128], r_scr[i, :, 128:] = skew(t0[:, :128]), skew(t0[:, 128:])

    def scores(tile, k, t):
        j0 = aligned(t * BK, BK)
        base = seq - row_block(k) * BQ
        by_offset = dot_nn(q_off[k], relX[:, pl.ds(aligned(base + j0, 128), BK)])
        content = dot_nn(q_row[k], kT[:, pl.ds(j0, BK)])
        ri = jnp.where(t == 0, lax.rem(k, GROUP), GROUP)
        rolled = [r_scr[ri, :, :128], r_scr[ri, :, 128:]]
        rolled += [skew(by_offset[:, m * 128:(m + 1) * 128]) for m in range(NC)]
        top_s = mx[k]
        for m in range(NC):
            top = jnp.where(past, rolled[m + 2][:128], rolled[m + 1][:128])
            bot = jnp.where(past, rolled[m + 1][128:], rolled[m][128:])
            s = content[:, m * 128:(m + 1) * 128] + reverse_rows(jnp.concatenate([top, bot], 0))
            s = s * (scale * LOG2E)
            s_all[tile, :, m * 128:(m + 1) * 128] = s
            top_s = jnp.maximum(top_s, s)
        mx[k] = top_s
        r_scr[GROUP, :, :128], r_scr[GROUP, :, 128:] = rolled[NC], rolled[NC + 1]

    def weigh(tile, k, t):
        top_s, tot = mx[k], total[k]
        parts = []
        for m in range(NC):
            p = jnp.exp2(s_all[tile, :, m * 128:(m + 1) * 128] - top_s)
            s_all[tile, :, m * 128:(m + 1) * 128] = p
            tot = tot + p
            parts.append(p.astype(BF16))
        total[k] = tot
        o_acc[k] += dot_nt(jnp.concatenate(parts, 1), vT[:, pl.ds(aligned(t * BK, BK), BK)])

    def finish_rows(k):
        do_col[k] = flip_lanes(doT[:, slot_cols(k)], eye)
        do_row[k] = transposed(do_col[k])
        inv = 1.0 / jnp.sum(total[k], axis=1, keepdims=True)
        out = o_acc[k] * inv
        delta = jnp.sum(do_row[k].astype(F32) * out, axis=1, keepdims=True)
        total[k] = jnp.broadcast_to(inv, (BQ, 128))
        mx[k] = jnp.broadcast_to(delta, (BQ, 128))
        oT[:, slot_cols(k)] = flip_lanes(out.T.astype(BF16), eye)

    def grads(tile, k, t):
        j0 = aligned(t * BK, BK)
        base = seq - row_block(k) * BQ
        js, us = pl.ds(j0, BK), pl.ds(aligned(base + j0 - 256, 128), BK)
        i = lax.rem(k, GROUP)
        dp = dot_nn(do_row[k], vT[:, js])
        inv, delta = total[k], mx[k]
        hi = jnp.where(t == 0, 0, 1)
        ps, dss, held = [], [], [h_scr[hi, :, :128], h_scr[hi, :, 128:]]
        for m in range(NC):
            p = s_all[tile, :, m * 128:(m + 1) * 128] * inv
            ds = (p * ((dp[:, m * 128:(m + 1) * 128] - delta) * scale)).astype(BF16)
            ps.append(p.astype(BF16))
            dss.append(ds)
            held.append(pltpu.roll(ds, 0, 1, stride=1, stride_axis=0))
        h_scr[1, :, :128], h_scr[1, :, 128:] = held[NC], held[NC + 1]
        by_offset = []
        for m in range(NC):
            top = jnp.where(before, held[m + 1][:128], held[m + 2][:128])
            bot = jnp.where(before, held[m][128:], held[m + 1][128:])
            by_offset.append(jnp.concatenate([top, bot], 0))
        p_all, ds_all, by_offset = (jnp.concatenate(x, 1) for x in (ps, dss, by_offset))
        dvT[:, js] += dot_nn(do_col[k], p_all)
        dkT[:, js] += dot_nn(q_col[k], ds_all)
        drF[:, us] += dot_nn(qo_col[k], by_offset)
        gu[i] += dot_nt(ds_all, kT[:, js])
        gv[i] += dot_nt(by_offset, relX[:dim, us])

    def over_tiles(step, g):
        k0 = GROUP * g
        tile0 = k0 * (k0 + 1) // 2

        def some(i, kt):
            k, t = kt
            for u in range(UNROLL):
                step(tile0 + UNROLL * i + u, k, t)
                last = t == k
                k, t = jnp.where(last, k + 1, k), jnp.where(last, 0, t + 1)
            return k, t

        lax.fori_loop(0, (GROUP * GROUP * g + GROUP * (GROUP + 1) // 2) // UNROLL, some, (k0, 0))

    def each(fn):
        lax.fori_loop(0, groups, lambda g, c: (fn(g), c)[1], 0)

    def forward_scores(g):
        for t in (0, 1):
            pass_on(t, g)
        for t in (0, 1):
            from_mate(t, g)
        for i in range(GROUP):
            row_landed(0, GROUP * g + i)
        for i in range(GROUP):
            prepare(GROUP * g + i, i)
        over_tiles(scores, g)

    each(forward_scores)
    each(lambda g: pass_on(2, g))

    def row_max(g):
        for i in range(GROUP):
            k = GROUP * g + i
            mx[k] = jnp.broadcast_to(jnp.max(mx[k], axis=1, keepdims=True), (BQ, 128))

    each(row_max)

    def weigh_group(g):
        from_mate(2, g)
        over_tiles(weigh, g)

    each(weigh_group)

    def out_rows(t, k, wait):
        rb = row_block(k)
        to, j = rb // per_blk, lax.rem(rb, per_blk)
        src = (oT, dqT)[t].at[:, slot_cols(k)]
        dst = (o_out, dq_out)[t].at[chip, :, pl.ds(aligned(j * BQ, BQ), BQ)]

        @pl.when(to != me)
        def _():
            c = remote_copy(src, dst, send_o.at[t, k], recv_o.at[t, chip, j], to)
            c.wait_send() if wait else c.start()

        @pl.when(to == me)
        def _():
            c = pltpu.make_async_copy(src, dst, loc_o.at[t, j])
            c.wait() if wait else c.start()

    def finish_group(g):
        for i in range(GROUP):
            row_landed(1, GROUP * g + i)
        for i in range(GROUP):
            finish_rows(GROUP * g + i)
        for i in range(GROUP):
            out_rows(0, GROUP * g + i, False)

    each(finish_group)

    parts, sinks = (drF, dkT, dvT), (dr_out, dk_out, dv_out)

    def pair(t, g):
        return remote_copy(parts[t].at[:, col(t, 2 * g + 1 - core, 0)], pair_buf.at[t, g], send_p.at[t, g], recv_p.at[t, g], mate)

    def sink(t, g):
        return remote_copy(send_buf.at[t, g], sinks[t].at[chip], send_s.at[t, g], recv_s.at[t, chip], 2 * g + core)

    def keep(t, g):
        return pltpu.make_async_copy(send_buf.at[t, g], sinks[t].at[chip], loc_s.at[t])

    def combine(g):
        for t in range(3):
            mine = col(t, 2 * g + core, 0)
            remote_copy(parts[t].at[:, mine], pair_buf.at[t, g], send_p.at[t, g], recv_p.at[t, g], mate).wait_recv()
            send_buf[t, g] = (parts[t][:, mine] + pair_buf[t, g]).astype(BF16)
        for t in range(3):
            @pl.when(g != chip)
            def _():
                sink(t, g).start()

            @pl.when(g == chip)
            def _():
                keep(t, g).start()

    def backward_group(step):
        g = groups - 1 - step
        gu[...] = jnp.zeros_like(gu)
        gv[...] = jnp.zeros_like(gv)
        over_tiles(grads, g)
        for t in range(3):
            pair(t, g).start()
        for i in range(GROUP):
            dqT[:, slot_cols(GROUP * g + i)] = flip_lanes((gu[i] + gv[i]).T.astype(BF16), eye)
            du[...] += jnp.sum(gu[i].reshape(BQ // 8, 8, dim), axis=0)
            dv[...] += jnp.sum(gv[i].reshape(BQ // 8, 8, dim), axis=0)
        for i in range(GROUP):
            out_rows(1, GROUP * g + i, False)
        combine(g)

    each(backward_group)

    for t in range(3):
        for i in range(heads):
            h = lax.rem(chip + i, heads)
            pair(t, i).wait_send()
            if i:
                direct(t, i).wait_send()
                sink(t, h).wait_send()
                remote_copy(send_buf.at[t, 0], sinks[t].at[h], send_s.at[t, 0], recv_s.at[t, h], me).wait_recv()
                forward(t, h).wait_send()
            else:
                to_mate(t).wait_send()
                keep(t, chip).wait()
    for t in (0, 1):
        for i in range(heads):
            for j in range(per_blk):
                to = 2 * lax.rem(chip + i, heads) + owner_core(me * per_blk + j)

                @pl.when(to != me)
                def _():
                    remote_copy((q_in, do_in)[t].at[0, :, pl.ds(0, BQ)], (qT, doT)[t].at[:, pl.ds(0, BQ)],
                                send_q.at[t, i, j], recv_q.at[t, 0], to).wait_send()
        for k in range(nslot):
            out_rows(t, k, True)
        for h in range(heads):
            for j in range(per_blk):
                @pl.when(2 * h + owner_core(me * per_blk + j) != me)
                def _():
                    remote_copy((oT, dqT)[t].at[:, pl.ds(0, BQ)], (o_out, dq_out)[t].at[h, :, pl.ds(j * BQ, BQ)],
                                send_o.at[t, 0], recv_o.at[t, h, j], me).wait_recv()


def table_grad_kernel(n, dr, du, dv, table, bias_out, dw_out, bias_buf, half_in, half_sum, part_in, w_acc,
                      send_b, recv_b, send_w, recv_w):
    me = lax.axis_index('cp')
    chip, core = me // 2, lax.rem(me, 2)
    mate = 2 * chip + 1 - core
    heads, dim, _ = dr.shape
    bias_buf[me, 0] = jnp.sum(du[...], axis=0, keepdims=True) + jnp.zeros((8, dim), F32)
    bias_buf[me, 1] = jnp.sum(dv[...], axis=0, keepdims=True) + jnp.zeros((8, dim), F32)
    eye = anti_eye(256)
    for h in range(heads):
        w_acc[h * dim:(h + 1) * dim] = dot_nn(flip_lanes(dr[h], eye), table[...])
    barrier_all(n)

    def bias(o):
        return remote_copy(bias_buf.at[me], bias_buf.at[me], send_b.at[o], recv_b.at[me], lax.rem(me + o, n))

    half = heads * dim // 2
    piece = half // heads

    def swap():
        return remote_copy(w_acc.at[pl.ds(aligned((1 - core) * half, half), half)], half_in, send_w.at[0], recv_w.at[0], mate)

    swap().start()
    for o in range(1, n):
        bias(o).start()
    swap().wait()
    half_sum[...] = w_acc[pl.ds(aligned(core * half, half), half)] + half_in[...]

    def spread(i):
        z = lax.rem(chip + i, heads)
        return remote_copy(half_sum.at[pl.ds(aligned(z * piece, piece), piece)], part_in.at[i], send_w.at[i], recv_w.at[i], 2 * z + core)

    for i in range(1, heads):
        spread(i).start()
    for i in range(1, heads):
        spread(i).wait()
    mine = half_sum[pl.ds(aligned(chip * piece, piece), piece)]
    for i in range(1, heads):
        mine = mine + part_in[i]
    half_in[pl.ds(0, piece)] = mine
    whole = half_in.at[pl.ds(0, piece)]

    def place(c, z):
        return dw_out.at[pl.ds(aligned(c * half + z * piece, piece), piece)]

    def collect(i):
        z = lax.rem(chip + i, heads)
        return remote_copy(whole, place(core, chip), send_w.at[4 + i], recv_w.at[4 + chip], 2 * z + core)

    def hand_over(i):
        z = lax.rem(chip + i, heads)
        return remote_copy(whole if i == 0 else place(core, z), place(core, z), send_w.at[8 + i], recv_w.at[8 + z], mate)

    for i in range(1, heads):
        collect(i).start()
    hand_over(0).start()
    place(core, chip)[...] = mine
    for i in range(1, heads):
        z = lax.rem(chip + i, heads)
        remote_copy(whole, place(core, z), send_w.at[0], recv_w.at[4 + z], me).wait_recv()
        hand_over(i).start()
    for o in range(1, n):
        b = lax.rem(me + o, n)
        remote_copy(bias_buf.at[b], bias_buf.at[b], send_b.at[0], recv_b.at[b], me).wait_recv()
    for h in range(heads):
        bias_out[h] = bias_buf[2 * h] + bias_buf[2 * h + 1]
    for i in range(heads):
        remote_copy(whole, place(1 - core, i), send_w.at[0], recv_w.at[8 + i], me).wait_recv()
        hand_over(i).wait_send()
        if i:
            collect(i).wait_send()
    for o in range(1, n):
        bias(o).wait_send()


def solution(mesh):
    n = mesh.shape['cp']
    seq_spec, head_spec, weight_spec = P('cp', 'hp', None), P('hp', None), P(None, 'hp', None)
    vmem = pl.BlockSpec(memory_space=pltpu.VMEM)
    hbm = pl.BlockSpec(memory_space=pl.ANY)
    dma, sds, buf = pltpu.SemaphoreType.DMA, jax.ShapeDtypeStruct, pltpu.VMEM

    def local_fn(q, k, v, u_bias, v_bias, rel_table, w_rel, d_out):
        blk, heads, dim = q.shape
        seq = n * blk
        rows = seq // 2
        nslot = rows // BQ
        per_blk = blk // BQ
        tiles = nslot * (nslot + 1) // 2
        qT, kT, vT, doT = (x.transpose(1, 2, 0) for x in (q, k, v, d_out))
        wT = w_rel.transpose(1, 2, 0).reshape(heads * dim, -1)
        model = wT.shape[1]
        relT = pl.pallas_call(rel_kernel, out_shape=sds((heads, dim, blk), BF16), in_specs=[vmem] * 2, out_specs=vmem,
                              name='rel_project')(rel_table, wT)
        o, dq, dk, dvv, dr, du, dv = pl.pallas_call(
            functools.partial(attention_kernel, n),
            out_shape=[sds((heads, dim, blk), BF16)] * 5 + [sds((8, dim), F32)] * 2,
            in_specs=[hbm] * 5 + [vmem] * 2, out_specs=[hbm] * 5 + [vmem] * 2,
            scratch_shapes=[
                buf((dim, rows), BF16), buf((dim, rows), BF16), buf((dim, seq), BF16), buf((dim, seq), BF16), buf((KX, seq + PAD), BF16),
                buf((dim, rows), BF16), buf((dim, rows), BF16), buf((dim, seq), F32), buf((dim, seq), F32), buf((dim, seq + PAD), F32),
                buf((tiles, BQ, BK), F32), buf((nslot, BQ, KX), BF16), buf((nslot, BQ, dim), BF16), buf((nslot, BQ, dim), BF16),
                buf((nslot, dim, BQ), BF16), buf((nslot, dim, BQ), BF16), buf((nslot, dim, BQ), BF16),
                buf((nslot, BQ, 128), F32), buf((nslot, BQ, 128), F32), buf((nslot, BQ, dim), F32),
                buf((GROUP, BQ, dim), F32), buf((GROUP, BQ, dim), F32), buf((GROUP + 1, BQ, 256), F32), buf((2, BQ, 256), BF16),
                buf((3, heads, dim, blk), F32), buf((3, heads, dim, blk), BF16),
                dma((3, heads)), dma((3, heads)), dma((2, heads, per_blk)), dma((3, n)), dma((2, nslot)), dma((3,)), dma((2, per_blk)),
                dma((2, nslot)), dma((2, heads, per_blk)), dma((2, per_blk)), dma((3, heads)), dma((3, heads)),
                dma((3, heads)), dma((3, heads)), dma((3,))],
            compiler_params=pltpu.CompilerParams(collective_id=0, has_side_effects=True, vmem_limit_bytes=67043328),
            name='attention',
        )(qT, kT, vT, doT, relT, u_bias, v_bias)
        half = heads * dim // 2
        bias, dw = pl.pallas_call(
            functools.partial(table_grad_kernel, n),
            out_shape=[sds((heads, 2, 8, dim), F32), sds((heads * dim, model), F32)],
            in_specs=[vmem] * 4, out_specs=[vmem] * 2,
            scratch_shapes=[buf((n, 2, 8, dim), F32), buf((half, model), F32), buf((half, model), F32),
                            buf((heads, half // heads, model), F32), buf((heads * dim, model), F32),
                            dma((n,)), dma((n,)), dma((12,)), dma((12,))],
            compiler_params=pltpu.CompilerParams(collective_id=1, has_side_effects=True),
            name='table_grad',
        )(dr, du, dv, rel_table)
        back = lambda x: x.transpose(2, 0, 1)
        return (back(o), back(dq), back(dk), back(dvv), bias[:, 0, 0], bias[:, 1, 0],
                back(dw.reshape(heads, dim, model)))

    return jax.shard_map(
        local_fn, mesh=mesh,
        in_specs=(seq_spec, seq_spec, seq_spec, head_spec, head_spec, P('cp', None), weight_spec, seq_spec),
        out_specs=(seq_spec, seq_spec, seq_spec, seq_spec, head_spec, head_spec, weight_spec),
        check_vma=False,
    )
```

time: 3840 us -> 186 us (0.05)
  waiting for transfers between devices: 1940 us -> 0 us
  starting transfers between devices: 1250 us -> 0 us
  local copies, waits for them, and re-layouts: 473 us -> 5.34 us
  Pallas kernels: 0 us -> 179 us
  matrix products: 58.3 us -> 0 us
  loops' own time: 55.8 us -> 0 us
    ppermute x44 -> x0, waiting for transfers between devices: 1570 us -> none  [the longest x7 928 us: bwd_step(): dk_acc = lax.ppermute(dk_acc, 'cp', shift_pairs)]
    ppermute x44 -> x0, starting transfers between devices: 1250 us -> none  [the longest x7 403 us: bwd_step(): k_blk = lax.ppermute(k_blk, 'cp', shift_pairs)]
    reduce_scatter x1 -> x0, waiting for transfers between devices: 293 us -> none  [local_fn(): lax.psum_scatter(grad_rel, 'cp', scatter_dimension=0, tiled=False)]
    cond x33 -> x0, local copies, waits for them, and re-layouts: 184 us -> none
    pallas_call x0 -> x3, Pallas kernels: none -> 179 us  [the longest x1 144 us: local_fn(): pl.pallas_call(functools.partial(attention_kernel, n), out_shape=[sds((he...]
    reshape x3 -> x0, local copies, waits for them, and re-layouts: 77.8 us -> none  [the longest x2 58.8 us: skew_scores(): kept_view.reshape(lead_dims + (block_len, 2 * block_len - 1))]
    dot_general x12 -> x0, matrix products: 56.7 us -> none  [the longest x2 17.8 us: block_scores(): jnp.einsum('qhd,shd->hqs', q_v, window, preferred_element_type=jnp.float32)]
    another operation x18 -> x0, loops' own time: 55.8 us -> none  [the longest x1 27.6 us: local_fn(): lax.fori_loop(0, last_step, fwd_step, (k, v, run_stats))]
  transfers between devices with their start and end apart: 47 -> 0, of which waited for: 43 -> 0; matrix products, arithmetic and copies ran while one was open for 6% -> 0% of each run, Pallas kernels for 0% -> 0%
where the time goes in v2:
time: 186 us; the launch traced here: 185 us
  Pallas kernels  179 us (96%)
  local copies, waits for them, and re-layouts  5.34 us (3%)
    pallas_call x1, Pallas kernels, local_fn(): pl.pallas_call(functools.partial(attention_kernel, n), out_shape=[sds((he...  144 us
    pallas_call x1, Pallas kernels, local_fn(): pl.pallas_call(functools.partial(table_grad_kernel, n), out_shape=[sds((h...  32.3 us
    unnamed x15, local copies, waits for them, and re-layouts  3.97 us

profile of v2, /device:TPU:0, one launch (start us, length us, event | category | flops | bytes accessed | tf_op | source)
XLA Modules:
  0.0 185.2 jit_solution(14770549373750247178)
XLA Ops:
  0.6 3.1 %rel_project.1.r_in = bf16[4,64,768]{2,1,0:T(8,128)(2,1)} custom-call(bf16[768,1024]{1,0:T(8,128)(2,1)} %table.3, bf16[256,1024]{1,0:T(8,128)(2,1)} %bitcast.17), custom_call_target="tpu_custom_call" | custom-call | tf_op jit(solution)/shard_map/rel_project/pallas_call | solution.py:529
  3.8 143.8 %attention.1 = (bf16[4,64,768]{2,1,0:T(8,128)(2,1)}, bf16[4,64,768]{2,1,0:T(8,128)(2,1)}, bf16[4,64,768]{2,1,0:T(8,128)(2,1)}, bf16[4,64,768]{2,1,0:T(8,128)(2,1...) custom-call(bf16[4,64,768]{2,1,0:T(8,128)(2,1)} %bitcast.22, bf16[4,64,768]{2,1,0:T(8,128)(2,1)} %bitcast.23, ...), custom_call_target="tpu_custom_call" | custom-call | tf_op jit(solution)/shard_map/attention/pallas_call | solution.py:531
  147.5 0.0 copy-start.4
  147.5 0.0 copy-start.3
  147.6 0.0 copy-start.2
  147.6 32.3 %table_grad.1 = (f32[4,2,8,64]{3,2,1,0:T(8,128)}, f32[256,1024]{1,0:T(8,128)}) custom-call(bf16[4,64,768]{2,1,0:T(8,128)(2,1)} %get-tuple-element.20.dr, f32[8,64]{1,0:T(8,128)} %get-tuple-element.21.du, f32[8,64]{1,0:T(8,128)} %get-tuple-element.22.dv, bf16[768,1024]{1,0:T(8,128)(2,1)} %table.3), custom_call_target="tpu_custom_call" | custom-call | tf_op jit(solution)/shard_map/table_grad/pallas_call | solution.py:550
  179.9 0.0 copy-start.1
  179.9 1.4 fusion
  181.2 0.0 copy-done.4
  181.2 0.0 copy-start
  181.2 0.7 copy.20
  182.0 0.0 copy-done.3
  182.0 0.7 copy.21
  182.7 0.0 copy-done.2
  182.7 0.7 copy.22
  183.5 0.0 copy-done.1
  183.5 0.7 copy.23
  184.2 0.0 copy-done
  184.2 1.0 copy.24
Async XLA Ops:
  147.5 33.7 %copy-start.4 = (bf16[4,64,768]{2,1,0:T(8,128)(2,1)S(1)}, bf16[4,64,768]{2,1,0:T(8,128)(2,1)}, u32[]{:S(2)}) copy-start(bf16[4,64,768]{2,1,0:T(8,128)(2,1)} %get-tuple-element.16) | copy-start | bytes 1179652
  147.5 34.4 %copy-start.3 = (bf16[4,64,768]{2,1,0:T(8,128)(2,1)S(1)}, bf16[4,64,768]{2,1,0:T(8,128)(2,1)}, u32[]{:S(2)}) copy-start(bf16[4,64,768]{2,1,0:T(8,128)(2,1)} %get-tuple-element.17) | copy-start | bytes 1179652
  147.6 35.2 %copy-start.2 = (bf16[4,64,768]{2,1,0:T(8,128)(2,1)S(1)}, bf16[4,64,768]{2,1,0:T(8,128)(2,1)}, u32[]{:S(2)}) copy-start(bf16[4,64,768]{2,1,0:T(8,128)(2,1)} %get-tuple-element.18) | copy-start | bytes 1179652
  179.9 3.6 %copy-start.1 = (bf16[4,64,768]{2,1,0:T(8,128)(2,1)S(1)}, bf16[4,64,768]{2,1,0:T(8,128)(2,1)}, u32[]{:S(2)}) copy-start(bf16[4,64,768]{2,1,0:T(8,128)(2,1)} %get-tuple-element.19) | copy-start | bytes 1179652
  181.2 3.0 %copy-start = (f32[256,1024]{1,0:T(8,128)S(1)}, f32[256,1024]{1,0:T(8,128)}, u32[]{:S(2)}) copy-start(f32[256,1024]{1,0:T(8,128)} %get-tuple-element.24) | copy-start | bytes 3145732

commit v3 on v2

v3 whole, which is shorter than its diff:
```python
import functools
import math
import jax
import jax.numpy as jnp
from jax import lax
from jax.experimental import pallas as pl
from jax.experimental.pallas import tpu as pltpu
from jax.sharding import PartitionSpec as P

F32, BF16 = jnp.float32, jnp.bfloat16
LOG2E = math.log2(math.e)
BQ = 256
BK = 512
NC = BK // 128
PAD = 512
KX = 80
GROUP = 3
UNROLL = 3
MESH_ID = pl.DeviceIdType.MESH


def dot_nn(a, b):
    return lax.dot_general(a, b, (((1,), (0,)), ((), ())), preferred_element_type=F32)


def dot_nt(a, b):
    return lax.dot_general(a, b, (((1,), (1,)), ((), ())), preferred_element_type=F32)


def aligned(x, m):
    return pl.multiple_of(x, m)


def anti_eye(n):
    rows = lax.broadcasted_iota(jnp.int32, (n, n), 0)
    cols = lax.broadcasted_iota(jnp.int32, (n, n), 1)
    return (rows + cols == n - 1).astype(F32).astype(BF16)


def flip_lanes(x, eye):
    n, w = x.shape[1], eye.shape[0]
    parts = [dot_nn(x[:, s:s + w], eye).astype(BF16) for s in range(0, n, w)]
    return jnp.concatenate(parts[::-1], axis=1)


def reverse_rows(x):
    ix = 7 - lax.broadcasted_iota(jnp.int32, (8, x.shape[1]), 0)
    n = x.shape[0] // 8
    return jnp.concatenate([jnp.take_along_axis(x[(n - 1 - g) * 8:(n - g) * 8], ix, axis=0) for g in range(n)], 0)


def owner_core(rb):
    return lax.rem(rb + rb // 2, 2)


def remote_copy(src, dst, send_sem, recv_sem, to):
    return pltpu.make_async_remote_copy(src, dst, send_sem, recv_sem, device_id=(lax.axis_index('hp'), to),
                                        device_id_type=MESH_ID)


def barrier_all(n):
    me, hp = lax.axis_index('cp'), lax.axis_index('hp')
    bar = pltpu.get_barrier_semaphore()
    for o in range(1, n):
        pl.semaphore_signal(bar, 1, device_id=(hp, lax.rem(me + o, n)), device_id_type=MESH_ID)
    pl.semaphore_wait(bar, n - 1)


def hand_off_kernel(o, dq, dk, dv, dw, bias, o_out, dq_out, dk_out, dv_out, dw_out, u_out, v_out):
    for src, dst in ((o, o_out), (dq, dq_out), (dk, dk_out), (dv, dv_out), (dw, dw_out)):
        dst[...] = src[...]
    u_out[...], v_out[...] = bias[0], bias[1]


def attention_kernel(n, q_in, k_in, v_in, do_in, table_in, w_rel, ub, vb,
                     o_out, dq_out, dk_out, dv_out, dw_out, bias_out,
                     qT, doT, kT, vT, relX, oT, dqT, dkT, dvT, drF,
                     s_all, q_off, q_row, do_row, q_col, qo_col, do_col, mx, total, acc, gv, r_scr,
                     pair_buf, send_buf, dr_buf, table, bias_buf,
                     send_d, send_f, send_q, recv_b, recv_q, loc_b, loc_q,
                     send_o, recv_o, loc_o, send_p, recv_p, send_s, recv_s, loc_s,
                     loc_t, send_w, recv_w, loc_w, send_b, recv_b2):
    me = lax.axis_index('cp')
    chip, core = me // 2, lax.rem(me, 2)
    mate = 2 * chip + 1 - core
    heads, dim, blk = q_in.shape
    seq = n * blk
    per_blk = blk // BQ
    groups = n // 2
    nslot = qT.shape[1] // BQ
    scale = dim ** -0.5
    pltpu.make_async_copy(table_in, table, loc_t).start()
    barrier_all(n)

    rel_buf = dr_buf
    srcs, fulls = (rel_buf, k_in, v_in), (relX, kT, vT)

    def col(t, b, flipped):
        b = (n - 1 - b) if t == flipped else b
        return pl.ds(aligned(b * blk, blk), blk)

    def full_at(t, b):
        return fulls[t].at[pl.ds(0, dim), col(t, b, 0)]

    def direct(t, i):
        h = lax.rem(chip + i, heads)
        return remote_copy(srcs[t].at[h], full_at(t, me), send_d.at[t, i], recv_b.at[t, me], 2 * h + core)

    def own(t):
        return pltpu.make_async_copy(srcs[t].at[chip], full_at(t, me), loc_b.at[t])

    def to_mate(t):
        return remote_copy(srcs[t].at[chip], full_at(t, me), send_f.at[t, chip], recv_b.at[t, me], mate)

    def forward(t, g):
        b = 2 * g + core
        return remote_copy(full_at(t, b), full_at(t, b), send_f.at[t, g], recv_b.at[t, b], mate)

    def landed(t, b):
        remote_copy(srcs[t].at[0], full_at(t, b), send_f.at[t, 0], recv_b.at[t, b], me).wait_recv()

    def pass_on(t, g):
        @pl.when(g != chip)
        def _():
            landed(t, 2 * g + core)
            forward(t, g).start()

        pl.when(g == chip)(own(t).wait)

    def from_mate(t, g):
        landed(t, 2 * g + 1 - core)

    def row_copy(t, i, j, wait):
        h = lax.rem(chip + i, heads)
        rb = me * per_blk + j
        src = (q_in, do_in)[t].at[h, :, pl.ds(j * BQ, BQ)]
        dst = (qT, doT)[t].at[:, pl.ds(aligned(rb // 2 * BQ, BQ), BQ)]
        to = 2 * h + owner_core(rb)

        @pl.when(to != me)
        def _():
            c = remote_copy(src, dst, send_q.at[t, i, j], recv_q.at[t, rb // 2], to)
            c.wait_send() if wait else c.start()

        @pl.when(to == me)
        def _():
            c = pltpu.make_async_copy(src, dst, loc_q.at[t, j])
            c.wait() if wait else c.start()

    def row_block(k):
        return 2 * k + lax.rem(k + core, 2)

    def row_landed(t, k):
        src = (q_in, do_in)[t].at[0, :, pl.ds(0, BQ)]
        dst = (qT, doT)[t].at[:, pl.ds(aligned(k * BQ, BQ), BQ)]
        rb = row_block(k)

        @pl.when(rb // per_blk != me)
        def _():
            remote_copy(src, dst, send_q.at[t, 0, 0], recv_q.at[t, k], me).wait_recv()

        @pl.when(rb // per_blk == me)
        def _():
            pltpu.make_async_copy(src, dst, loc_q.at[t, lax.rem(rb, per_blk)]).wait()

    order = (1, 3, 2)
    eye = anti_eye(BQ)
    pltpu.make_async_copy(table_in, table, loc_t).wait()
    rel = flip_lanes(dot_nt(w_rel[...], table[...]).astype(BF16), eye)
    for h in range(heads):
        rel_buf[h] = rel[h * dim:(h + 1) * dim]
    to_mate(1).start()
    own(1).start()
    for i in order:
        direct(1, i).start()
        direct(0, i).start()
        for j in range(per_blk):
            row_copy(0, i, j, False)
    for j in range(per_blk):
        row_copy(0, 0, j, False)
    to_mate(0).start()
    own(0).start()

    def send_values():
        to_mate(2).start()
        own(2).start()
        for i in order:
            direct(2, i).start()

    def send_cotangent():
        for i in range(1, heads):
            direct(0, i).wait_send()
        to_mate(0).wait_send()
        for i in order + (0,):
            for j in range(per_blk):
                row_copy(1, i, j, False)

    for ref in (dkT, dvT, drF, total, acc, gv):
        ref[...] = jnp.zeros_like(ref)
    mx[...] = jnp.full(mx.shape, -jnp.inf, F32)
    relX[pl.ds(0, dim), pl.ds(seq, PAD)] = jnp.zeros((dim, PAD), BF16)
    first = lax.broadcasted_iota(jnp.int32, (KX - dim, PAD), 0) == 0
    relX[pl.ds(dim, KX - dim), pl.ds(0, seq)] = jnp.zeros((KX - dim, seq), BF16)
    relX[pl.ds(dim, KX - dim), pl.ds(seq, PAD)] = jnp.where(first, -jnp.inf, 0.0).astype(BF16)
    ones_col = (lax.broadcasted_iota(jnp.int32, (BQ, KX - dim), 1) == 0).astype(F32).astype(BF16)
    lane = lax.broadcasted_iota(jnp.int32, (128, 128), 1)
    row = lax.broadcasted_iota(jnp.int32, (128, 128), 0)
    past, before = lane > row, lane < row

    def bias_col(ref):
        pick = lax.broadcasted_iota(jnp.int32, ref.shape, 0) == chip
        r = jnp.sum(jnp.where(pick, ref[...], 0.0), axis=0, keepdims=True)
        return jnp.broadcast_to(r, (128, dim)).T[:, :1]

    u_col, v_col = bias_col(ub), bias_col(vb)

    def skew(t):
        return pltpu.roll(t, 1, 1, stride=1, stride_axis=0)

    def slot_cols(k):
        return pl.ds(aligned(k * BQ, BQ), BQ)

    def transposed(x):
        return x.astype(F32).T.astype(BF16)

    def prepare(k, i):
        q = qT[:, slot_cols(k)].astype(F32)
        quT, qvT = (q + u_col).astype(BF16), (q + v_col).astype(BF16)
        q_off[k] = jnp.concatenate([transposed(qvT), ones_col], 1)
        q_col[k] = flip_lanes(quT, eye)
        q_row[k] = transposed(q_col[k])
        qo_col[k] = flip_lanes(qvT, eye)
        base = seq - row_block(k) * BQ
        t0 = dot_nn(q_off[k], relX[:, pl.ds(aligned(base - 256, 128), 256)])
        r_scr[i, :, :128], r_scr[i, :, 128:] = skew(t0[:, :128]), skew(t0[:, 128:])

    def scores(tile, k, t):
        j0 = aligned(t * BK, BK)
        base = seq - row_block(k) * BQ
        by_offset = dot_nn(q_off[k], relX[:, pl.ds(aligned(base + j0, 128), BK)])
        content = dot_nn(q_row[k], kT[:, pl.ds(j0, BK)])
        ri = jnp.where(t == 0, lax.rem(k, GROUP), GROUP)
        rolled = [r_scr[ri, :, :128], r_scr[ri, :, 128:]]
        rolled += [skew(by_offset[:, m * 128:(m + 1) * 128]) for m in range(NC)]
        top_s = mx[k]
        for m in range(NC):
            top = jnp.where(past, rolled[m + 2][:128], rolled[m + 1][:128])
            bot = jnp.where(past, rolled[m + 1][128:], rolled[m][128:])
            s = content[:, m * 128:(m + 1) * 128] + reverse_rows(jnp.concatenate([top, bot], 0))
            s = s * (scale * LOG2E)
            s_all[tile, :, m * 128:(m + 1) * 128] = s
            top_s = jnp.maximum(top_s, s)
        mx[k] = top_s
        r_scr[GROUP, :, :128], r_scr[GROUP, :, 128:] = rolled[NC], rolled[NC + 1]

    def weigh(tile, k, t):
        top_s, tot = mx[k], total[k]
        parts = []
        for m in range(NC):
            p = jnp.exp2(s_all[tile, :, m * 128:(m + 1) * 128] - top_s)
            s_all[tile, :, m * 128:(m + 1) * 128] = p
            tot = tot + p
            parts.append(p.astype(BF16))
        total[k] = tot
        acc[k] += dot_nt(jnp.concatenate(parts, 1), vT[:, pl.ds(aligned(t * BK, BK), BK)])

    def finish_rows(k):
        do_col[k] = flip_lanes(doT[:, slot_cols(k)], eye)
        do_row[k] = transposed(do_col[k])
        inv = 1.0 / jnp.sum(total[k], axis=1, keepdims=True)
        out = acc[k] * inv
        delta = jnp.sum(do_row[k].astype(F32) * out, axis=1, keepdims=True)
        total[k] = jnp.broadcast_to(inv, (BQ, 128))
        mx[k] = jnp.broadcast_to(delta, (BQ, 128))
        oT[:, slot_cols(k)] = flip_lanes(out.T.astype(BF16), eye)
        acc[k] = jnp.zeros((BQ, dim), F32)

    def grads(tile, k, t):
        j0 = aligned(t * BK, BK)
        base = seq - row_block(k) * BQ
        js, us = pl.ds(j0, BK), pl.ds(aligned(base + j0 - 256, 128), BK)
        dp = dot_nn(do_row[k], vT[:, js])
        inv, delta = total[k], mx[k]
        prev = jnp.maximum(tile - 1, 0)
        ps, dss = [], []
        held = [jnp.where(t > 0, s_all[prev, :, m * 128:(m + 1) * 128], 0.0).astype(BF16) for m in range(2)]
        for m in range(NC):
            p = s_all[tile, :, m * 128:(m + 1) * 128] * inv
            ds = (p * ((dp[:, m * 128:(m + 1) * 128] - delta) * scale)).astype(BF16)
            ps.append(p.astype(BF16))
            dss.append(ds)
            held.append(pltpu.roll(ds, 0, 1, stride=1, stride_axis=0))
        for m in range(2):
            s_all[tile, :, m * 128:(m + 1) * 128] = held[NC + m].astype(F32)
        by_offset = []
        for m in range(NC):
            top = jnp.where(before, held[m + 1][:128], held[m + 2][:128])
            bot = jnp.where(before, held[m][128:], held[m + 1][128:])
            by_offset.append(jnp.concatenate([top, bot], 0))
        p_all, ds_all, by_offset = (jnp.concatenate(x, 1) for x in (ps, dss, by_offset))
        dvT[:, js] += dot_nn(do_col[k], p_all)
        dkT[:, js] += dot_nn(q_col[k], ds_all)
        drF[:, us] += dot_nn(qo_col[k], by_offset)
        acc[k] += dot_nt(ds_all, kT[:, js])
        gv[k] += dot_nt(by_offset, relX[:dim, us])

    def walk(step, count, k, t_low, t_cap):
        def some(i, kt):
            k, t = kt
            for u in range(UNROLL):
                step(k * (k + 1) // 2 + t, k, t)
                last = t == jnp.minimum(k, t_cap)
                k, t = jnp.where(last, k + 1, k), jnp.where(last, t_low, t + 1)
            return k, t

        lax.fori_loop(0, count // UNROLL, some, (k, t_low))

    def group_tiles(g):
        return GROUP * GROUP * g + GROUP * (GROUP + 1) // 2

    def over_tiles(step, g):
        walk(step, group_tiles(g), GROUP * g, 0, nslot)

    def each(fn):
        lax.fori_loop(0, groups, lambda g, c: (fn(g), c)[1], 0)

    def forward_scores(g):
        for t in (0, 1):
            pass_on(t, g)
        for t in (0, 1):
            from_mate(t, g)
        for i in range(GROUP):
            row_landed(0, GROUP * g + i)
        for i in range(GROUP):
            prepare(GROUP * g + i, i)
        lower = chip < groups // 2
        pl.when(g == jnp.where(lower, 3, 1))(send_values)
        pl.when((g == 2) & ~lower)(send_cotangent)
        over_tiles(scores, g)

    each(forward_scores)
    pl.when(chip < groups // 2)(send_cotangent)
    each(lambda g: pass_on(2, g))

    def row_max(g):
        for i in range(GROUP):
            k = GROUP * g + i
            mx[k] = jnp.broadcast_to(jnp.max(mx[k], axis=1, keepdims=True), (BQ, 128))

    each(row_max)

    def weigh_group(g):
        from_mate(2, g)
        over_tiles(weigh, g)

    each(weigh_group)

    def out_rows(t, k, wait):
        rb = row_block(k)
        to, j = rb // per_blk, lax.rem(rb, per_blk)
        src = (oT, dqT)[t].at[:, slot_cols(k)]
        dst = (o_out, dq_out)[t].at[chip, :, pl.ds(aligned(j * BQ, BQ), BQ)]

        @pl.when(to != me)
        def _():
            c = remote_copy(src, dst, send_o.at[t, k], recv_o.at[t, chip, j], to)
            c.wait_send() if wait else c.start()

        @pl.when(to == me)
        def _():
            c = pltpu.make_async_copy(src, dst, loc_o.at[t, j])
            c.wait() if wait else c.start()

    def finish_group(g):
        for i in range(GROUP):
            row_landed(1, GROUP * g + i)
        for i in range(GROUP):
            finish_rows(GROUP * g + i)
        for i in range(GROUP):
            out_rows(0, GROUP * g + i, False)

    each(finish_group)

    parts, sinks = (drF, dkT, dvT), (dr_buf, dk_out, dv_out)

    def pair(t, g, s):
        return remote_copy(parts[t].at[:, col(t, 2 * g + 1 - core, 0)], pair_buf.at[t, s], send_p.at[t, s], recv_p.at[t, s], mate)

    def sink(t, g, s):
        return remote_copy(send_buf.at[t, s], sinks[t].at[chip], send_s.at[t, s], recv_s.at[t, chip], 2 * g + core)

    def keep(t, s):
        return pltpu.make_async_copy(send_buf.at[t, s], sinks[t].at[chip], loc_s.at[t])

    def out_groups(step):
        g = groups - 1 - step
        return g, jnp.where(chip < groups // 2, g, step)

    def combine(step, s):
        gd, gk = out_groups(step)
        for t, g in ((0, gd), (1, gk), (2, gk)):
            mine = col(t, 2 * g + core, 0)
            remote_copy(parts[t].at[:, mine], pair_buf.at[t, s], send_p.at[t, s], recv_p.at[t, s], mate).wait_recv()
            send_buf[t, s] = (parts[t][:, mine] + pair_buf[t, s]).astype(BF16)
        for t, g in ((0, gd), (1, gk), (2, gk)):
            @pl.when(g != chip)
            def _():
                sink(t, g, s).start()

            @pl.when(g == chip)
            def _():
                keep(t, s).start()

    w_acc, w_in, w_half, w_part, w_mine = (9, 0), (10, 0), (10, 1), (11, 0), (11, 1)

    def place(kt, c=0):
        return kt[0] * (kt[0] + 1) // 2 + kt[1] + c

    half = heads * dim // 2
    piece = half // heads

    def swap(c):
        return remote_copy(s_all.at[place(w_acc, c), pl.ds(aligned((1 - core) * half, half), half)],
                           s_all.at[place(w_in), pl.ds(c * half, half)], send_w.at[0, c], recv_w.at[0, c], mate)

    def spread(i, c):
        z = lax.rem(chip + i, heads)
        return remote_copy(s_all.at[place(w_half), pl.ds(aligned(c * half + z * piece, piece), piece)],
                           s_all.at[place(w_part), pl.ds((2 * i + c) * piece, piece)], send_w.at[i, c], recv_w.at[i, c], 2 * z + core)

    def table_grad():
        for h in range(heads):
            @pl.when(h != chip)
            def _():
                remote_copy(send_buf.at[0, 0], dr_buf.at[h], send_s.at[0, 0], recv_s.at[0, h], me).wait_recv()

            @pl.when(h == chip)
            def _():
                keep(0, 0).wait()
        dr = jnp.concatenate([flip_lanes(dr_buf[h], eye) for h in range(heads)], 0)
        for c in range(2):
            s_all[place(w_acc, c)] = dot_nn(dr, table[:, c * BK:(c + 1) * BK])
        for c in range(2):
            swap(c).start()
        for c in range(2):
            swap(c).wait()
            s_all[place(w_half), c * half:(c + 1) * half] = (
                s_all[place(w_acc, c), pl.ds(aligned(core * half, half), half)] + s_all[place(w_in), c * half:(c + 1) * half])
        for i in range(1, heads):
            for c in range(2):
                spread(i, c).start()

    def backward_step(step):
        gd, gk = out_groups(step)
        left = chip < groups // 2
        s = lax.rem(step, 2)
        walk(grads, group_tiles(gd), GROUP * gk, jnp.where(left, 0, GROUP * step), jnp.where(left, nslot, GROUP * step + GROUP - 1))

        @pl.when(step > 1)
        def _():
            pd, pk = out_groups(step - 2)
            for t, g, p in ((0, gd, pd), (1, gk, pk), (2, gk, pk)):
                pair(t, p, s).wait_send()

                @pl.when(p != chip)
                def _():
                    sink(t, p, s).wait_send()

                @pl.when((p == chip) & (t > 0))
                def _():
                    keep(t, s).wait()

        for t, g in ((0, gd), (1, gk), (2, gk)):
            pair(t, g, s).start()
        for i in range(GROUP):
            k = GROUP * gk + i
            dqT[:, slot_cols(k)] = flip_lanes((acc[k] + gv[k]).T.astype(BF16), eye)
        combine(step, s)
        for i in range(GROUP):
            out_rows(1, GROUP * gk + i, False)

        pl.when((step > 0) & (chip == groups - step))(table_grad)

    each(backward_step)
    for t, ref in ((0, acc), (1, gv)):
        rows_sum = jnp.sum(ref[...].reshape(nslot * BQ // 8, 8, dim), axis=0)
        bias_buf[me, t] = jnp.sum(rows_sum, axis=0, keepdims=True) + jnp.zeros((8, dim), F32)

    def bias(o):
        return remote_copy(bias_buf.at[me], bias_buf.at[me], send_b.at[o], recv_b2.at[me], lax.rem(me + o, n))

    for o in range(1, n):
        bias(o).start()
    pl.when(chip == 0)(table_grad)
    for i in range(1, heads):
        for c in range(2):
            spread(i, c).wait()
    mine = place(w_mine)
    for c in range(2):
        got = s_all[place(w_half), pl.ds(aligned(c * half + chip * piece, piece), piece)]
        for i in range(1, heads):
            got = got + s_all[place(w_part), (2 * i + c) * piece:(2 * i + c + 1) * piece]
        s_all[mine, c * piece:(c + 1) * piece] = got

    def home(co, z, c):
        return dw_out.at[pl.ds(aligned(co * half + z * piece, piece), piece), pl.ds(c * BK, BK)]

    def my_piece(c):
        return s_all.at[mine, pl.ds(c * piece, piece)]

    def collect(i, c):
        z = lax.rem(chip + i, heads)
        return remote_copy(my_piece(c), home(core, chip, c), send_w.at[4 + i, c], recv_w.at[4 + chip, c], 2 * z + core)

    def hand_over(i, c):
        z = lax.rem(chip + i, heads)
        return remote_copy(my_piece(c) if i == 0 else home(core, z, c), home(core, z, c), send_w.at[8 + i, c], recv_w.at[8 + z, c], mate)

    def stay(c):
        return pltpu.make_async_copy(my_piece(c), home(core, chip, c), loc_w.at[c])

    for c in range(2):
        for i in range(1, heads):
            collect(i, c).start()
        hand_over(0, c).start()
        stay(c).start()
    for i in range(1, heads):
        z = lax.rem(chip + i, heads)
        for c in range(2):
            remote_copy(my_piece(c), home(core, z, c), send_w.at[0, c], recv_w.at[4 + z, c], me).wait_recv()
            hand_over(i, c).start()
    for o in range(1, n):
        b = lax.rem(me + o, n)
        remote_copy(bias_buf.at[b], bias_buf.at[b], send_b.at[0], recv_b2.at[b], me).wait_recv()
    for t in range(2):
        bias_out[t] = jnp.concatenate([bias_buf[2 * h, t, :1] + bias_buf[2 * h + 1, t, :1] for h in range(heads)], 0)

    for c in range(2):
        stay(c).wait()
        for i in range(heads):
            remote_copy(my_piece(c), home(1 - core, i, c), send_w.at[0, c], recv_w.at[8 + i, c], me).wait_recv()
            hand_over(i, c).wait_send()
            if i:
                collect(i, c).wait_send()
    for o in range(1, n):
        bias(o).wait_send()
    for t in range(3):
        for step in (groups - 2, groups - 1):
            gd, gk = out_groups(step)
            g = gk if t else gd
            pair(t, g, step % 2).wait_send()

            @pl.when(g != chip)
            def _():
                sink(t, g, step % 2).wait_send()

            if t:
                @pl.when(g == chip)
                def _():
                    keep(t, step % 2).wait()
        if t:
            to_mate(t).wait_send()
        for i in range(1, heads):
            h = lax.rem(chip + i, heads)
            forward(t, h).wait_send()
            if t:
                direct(t, i).wait_send()
                remote_copy(send_buf.at[t, 0], sinks[t].at[h], send_s.at[t, 0], recv_s.at[t, h], me).wait_recv()
    for t in (0, 1):
        for i in range(heads):
            for j in range(per_blk):
                to = 2 * lax.rem(chip + i, heads) + owner_core(me * per_blk + j)

                @pl.when(to != me)
                def _():
                    remote_copy((q_in, do_in)[t].at[0, :, pl.ds(0, BQ)], (qT, doT)[t].at[:, pl.ds(0, BQ)],
                                send_q.at[t, i, j], recv_q.at[t, 0], to).wait_send()
        for k in range(nslot):
            out_rows(t, k, True)
        for h in range(heads):
            for j in range(per_blk):
                @pl.when(2 * h + owner_core(me * per_blk + j) != me)
                def _():
                    remote_copy((oT, dqT)[t].at[:, pl.ds(0, BQ)], (o_out, dq_out)[t].at[h, :, pl.ds(j * BQ, BQ)],
                                send_o.at[t, 0], recv_o.at[t, h, j], me).wait_recv()


def solution(mesh):
    n = mesh.shape['cp']
    seq_spec, head_spec, weight_spec = P('cp', 'hp', None), P('hp', None), P(None, 'hp', None)
    vmem = pl.BlockSpec(memory_space=pltpu.VMEM)
    hbm = pl.BlockSpec(memory_space=pl.ANY)
    dma, sds, buf = pltpu.SemaphoreType.DMA, jax.ShapeDtypeStruct, pltpu.VMEM

    def local_fn(q, k, v, u_bias, v_bias, rel_table, w_rel, d_out):
        blk, heads, dim = q.shape
        seq = n * blk
        rows = seq // 2
        nslot = rows // BQ
        per_blk = blk // BQ
        tiles = nslot * (nslot + 1) // 2
        qT, kT, vT, doT = (x.transpose(1, 2, 0) for x in (q, k, v, d_out))
        wT = w_rel.transpose(1, 2, 0).reshape(heads * dim, -1)
        model = wT.shape[1]
        o, dq, dk, dvv, dw, bias = pl.pallas_call(
            functools.partial(attention_kernel, n),
            out_shape=[sds((heads, dim, blk), BF16)] * 4 + [sds((heads * dim, model), F32), sds((2, heads, dim), F32)],
            in_specs=[hbm] * 5 + [vmem] * 3, out_specs=[hbm] * 5 + [vmem],
            scratch_shapes=[
                buf((dim, rows), BF16), buf((dim, rows), BF16), buf((dim, seq), BF16), buf((dim, seq), BF16), buf((KX, seq + PAD), BF16),
                buf((dim, rows), BF16), buf((dim, rows), BF16), buf((dim, seq), F32), buf((dim, seq), F32), buf((dim, seq + PAD), F32),
                buf((tiles, BQ, BK), F32), buf((nslot, BQ, KX), BF16), buf((nslot, BQ, dim), BF16), buf((nslot, BQ, dim), BF16),
                buf((nslot, dim, BQ), BF16), buf((nslot, dim, BQ), BF16), buf((nslot, dim, BQ), BF16),
                buf((nslot, BQ, 128), F32), buf((nslot, BQ, 128), F32), buf((nslot, BQ, dim), F32), buf((nslot, BQ, dim), F32),
                buf((GROUP + 1, BQ, 256), F32),
                buf((3, 2, dim, blk), F32), buf((3, 2, dim, blk), BF16), buf((heads, dim, blk), BF16), buf((blk, model), BF16),
                buf((n, 2, 8, dim), F32),
                dma((3, heads)), dma((3, heads)), dma((2, heads, per_blk)), dma((3, n)), dma((2, nslot)), dma((3,)), dma((2, per_blk)),
                dma((2, nslot)), dma((2, heads, per_blk)), dma((2, per_blk)), dma((3, 2)), dma((3, 2)),
                dma((3, 2)), dma((3, heads)), dma((3,)),
                dma, dma((12, 2)), dma((12, 2)), dma((2,)), dma((n,)), dma((n,))],
            compiler_params=pltpu.CompilerParams(collective_id=0, has_side_effects=True, vmem_limit_bytes=67043328),
            name='attention',
        )(qT, kT, vT, doT, rel_table, wT, u_bias, v_bias)
        steps = 2
        part = pl.BlockSpec((heads // steps, dim, blk), lambda i: (i, 0, 0))
        wide = pl.BlockSpec((heads * dim // steps, model), lambda i: (i, 0))
        whole = lambda *shape: pl.BlockSpec(shape, lambda i: (0,) * len(shape))
        o, dq, dk, dvv, dw, du, dv = pl.pallas_call(
            hand_off_kernel, grid=(steps,),
            out_shape=[sds((heads, dim, blk), BF16)] * 4 + [sds((heads * dim, model), F32)] + [sds((heads, dim), F32)] * 2,
            in_specs=[part] * 4 + [wide, whole(2, heads, dim)],
            out_specs=[part] * 4 + [wide, whole(heads, dim), whole(heads, dim)],
            name='hand_off',
        )(o, dq, dk, dvv, dw, bias)
        back = lambda x: x.transpose(2, 0, 1)
        return back(o), back(dq), back(dk), back(dvv), du, dv, back(dw.reshape(heads, dim, model))

    return jax.shard_map(
        local_fn, mesh=mesh,
        in_specs=(seq_spec, seq_spec, seq_spec, head_spec, head_spec, P('cp', None), weight_spec, seq_spec),
        out_specs=(seq_spec, seq_spec, seq_spec, seq_spec, head_spec, head_spec, weight_spec),
        check_vma=False,
    )
```

time: 186 us -> 165 us (0.89)
  Pallas kernels: 179 us -> 165 us
  local copies, waits for them, and re-layouts: 5.34 us -> 0 us
    pallas_call x2 -> x1, Pallas kernels: 35.4 us -> 3 us  [local_fn(): pl.pallas_call(hand_off_kernel, grid=(steps,), out_shape=[sds((heads, dim...]
    pallas_call x1, Pallas kernels: 144 us -> 162 us  [local_fn(): pl.pallas_call(functools.partial(attention_kernel, n), out_shape=[sds((he...]
    unnamed x15 -> x0, local copies, waits for them, and re-layouts: 3.97 us -> none
where the time goes in v3:
time: 165 us
  Pallas kernels  165 us (100%)
    pallas_call x1, Pallas kernels, local_fn(): pl.pallas_call(functools.partial(attention_kernel, n), out_shape=[sds((he...  162 us

profile of v3, /device:TPU:0, one launch (start us, length us, event | category | flops | bytes accessed | tf_op | source)
XLA Modules:
  0.0 165.2 jit_solution(3770404677607046170)
XLA Ops:
  0.6 161.6 %attention.1 = (bf16[4,64,768]{2,1,0:T(8,128)(2,1)}, bf16[4,64,768]{2,1,0:T(8,128)(2,1)}, bf16[4,64,768]{2,1,0:T(8,128)(2,1)}, bf16[4,64,768]{2,1,0:T(8,128)(2,1...) custom-call(bf16[4,64,768]{2,1,0:T(8,128)(2,1)} %bitcast.15, bf16[4,64,768]{2,1,0:T(8,128)(2,1)} %bitcast.16, ...), custom_call_target="tpu_custom_call" | custom-call | tf_op jit(solution)/shard_map/attention/pallas_call | solution.py:605
  162.2 3.0 %hand_off.1 = (bf16[4,64,768]{2,1,0:T(8,128)(2,1)}, bf16[4,64,768]{2,1,0:T(8,128)(2,1)}, bf16[4,64,768]{2,1,0:T(8,128)(2,1)}, bf16[4,64,768]{2,1,0:T(8,128)(2,1)...) custom-call(bf16[4,64,768]{2,1,0:T(8,128)(2,1)} %get-tuple-element.20.o, ...), custom_call_target="tpu_custom_call" | custom-call | tf_op jit(solution)/shard_map/hand_off/pallas_call | solution.py:629

commit v4 on v3

--- a/solution.py
+++ b/solution.py
@@ -16,6 +16,7 @@
 KX = 80
 GROUP = 3
 UNROLL = 3
+VALUES_AT = 6
 MESH_ID = pl.DeviceIdType.MESH
 
 
@@ -75,8 +76,8 @@
 def attention_kernel(n, q_in, k_in, v_in, do_in, table_in, w_rel, ub, vb,
                      o_out, dq_out, dk_out, dv_out, dw_out, bias_out,
                      qT, doT, kT, vT, relX, oT, dqT, dkT, dvT, drF,
-                     s_all, q_off, q_row, do_row, q_col, qo_col, do_col, mx, total, acc, gv, r_scr,
-                     pair_buf, send_buf, dr_buf, table, bias_buf,
+                     s_all, q_off, q_row, do_row, q_col, qo_col, do_col, mx, total, acc, r_scr,
+                     pair_buf, dr_send, send_buf, dr_buf, table, bias_buf,
                      send_d, send_f, send_q, recv_b, recv_q, loc_b, loc_q,
                      send_o, recv_o, loc_o, send_p, recv_p, send_s, recv_s, loc_s,
                      loc_t, send_w, recv_w, loc_w, send_b, recv_b2):
@@ -102,9 +103,8 @@
     def full_at(t, b):
         return fulls[t].at[pl.ds(0, dim), col(t, b, 0)]
 
-    def direct(t, i):
-        h = lax.rem(chip + i, heads)
-        return remote_copy(srcs[t].at[h], full_at(t, me), send_d.at[t, i], recv_b.at[t, me], 2 * h + core)
+    def direct(t, h):
+        return remote_copy(srcs[t].at[h], full_at(t, me), send_d.at[t, h], recv_b.at[t, me], 2 * h + core)
 
     def own(t):
         return pltpu.make_async_copy(srcs[t].at[chip], full_at(t, me), loc_b.at[t])
@@ -130,8 +130,7 @@
     def from_mate(t, g):
         landed(t, 2 * g + 1 - core)
 
-    def row_copy(t, i, j, wait):
-        h = lax.rem(chip + i, heads)
+    def row_copy(t, h, j, wait):
         rb = me * per_blk + j
         src = (q_in, do_in)[t].at[h, :, pl.ds(j * BQ, BQ)]
         dst = (qT, doT)[t].at[:, pl.ds(aligned(rb // 2 * BQ, BQ), BQ)]
@@ -139,7 +138,7 @@
 
         @pl.when(to != me)
         def _():
-            c = remote_copy(src, dst, send_q.at[t, i, j], recv_q.at[t, rb // 2], to)
+            c = remote_copy(src, dst, send_q.at[t, h, j], recv_q.at[t, rb // 2], to)
             c.wait_send() if wait else c.start()
 
         @pl.when(to == me)
@@ -163,39 +162,49 @@
         def _():
             pltpu.make_async_copy(src, dst, loc_q.at[t, lax.rem(rb, per_blk)]).wait()
 
-    order = (1, 3, 2)
+    lower = chip < groups // 2
+    side = chip + 1 - 2 * lax.rem(chip, 2)
+    near, far = jnp.where(lower, groups // 2, groups // 2 - 1), jnp.where(lower, groups - 1, 0)
+    across = near, far
+
+    def send_rows(t, h):
+        for j in range(per_blk):
+            row_copy(t, h, j, False)
+
+    def send_scores_input(h):
+        direct(1, h).start()
+        send_rows(0, h)
+
+    to_mate(1).start()
+    own(1).start()
+    send_scores_input(side)
+    send_rows(0, chip)
     eye = anti_eye(BQ)
     pltpu.make_async_copy(table_in, table, loc_t).wait()
     rel = flip_lanes(dot_nt(w_rel[...], table[...]).astype(BF16), eye)
     for h in range(heads):
         rel_buf[h] = rel[h * dim:(h + 1) * dim]
-    to_mate(1).start()
-    own(1).start()
-    for i in order:
-        direct(1, i).start()
-        direct(0, i).start()
-        for j in range(per_blk):
-            row_copy(0, i, j, False)
-    for j in range(per_blk):
-        row_copy(0, 0, j, False)
     to_mate(0).start()
     own(0).start()
+    for h in (side, *across):
+        direct(0, h).start()
+    for h in across:
+        send_scores_input(h)
 
     def send_values():
         to_mate(2).start()
         own(2).start()
-        for i in order:
-            direct(2, i).start()
+        for h in (side, *across):
+            direct(2, h).start()
 
     def send_cotangent():
-        for i in range(1, heads):
-            direct(0, i).wait_send()
+        for h in (side, *across):
+            direct(0, h).wait_send()
         to_mate(0).wait_send()
-        for i in order + (0,):
-            for j in range(per_blk):
-                row_copy(1, i, j, False)
-
-    for ref in (dkT, dvT, drF, total, acc, gv):
+        for h in (side, *across, chip):
+            send_rows(1, h)
+
+    for ref in (dkT, dvT, drF, total, acc):
         ref[...] = jnp.zeros_like(ref)
     mx[...] = jnp.full(mx.shape, -jnp.inf, F32)
     relX[pl.ds(0, dim), pl.ds(seq, PAD)] = jnp.zeros((dim, PAD), BF16)
@@ -223,23 +232,25 @@
     def transposed(x):
         return x.astype(F32).T.astype(BF16)
 
-    def prepare(k, i):
+    def prepare(k):
         q = qT[:, slot_cols(k)].astype(F32)
         quT, qvT = (q + u_col).astype(BF16), (q + v_col).astype(BF16)
-        q_off[k] = jnp.concatenate([transposed(qvT), ones_col], 1)
+        q_off[k, :, :KX] = jnp.concatenate([transposed(qvT), ones_col], 1)
         q_col[k] = flip_lanes(quT, eye)
-        q_row[k] = transposed(q_col[k])
+        q_row[k, :, :dim] = transposed(q_col[k])
         qo_col[k] = flip_lanes(qvT, eye)
-        base = seq - row_block(k) * BQ
-        t0 = dot_nn(q_off[k], relX[:, pl.ds(aligned(base - 256, 128), 256)])
+
+    def prepare_skew(k, i, t):
+        start = seq - row_block(k) * BQ + t * BK - 256
+        t0 = dot_nn(q_off[k, :, :KX], relX[:, pl.ds(aligned(start, 128), 256)])
         r_scr[i, :, :128], r_scr[i, :, 128:] = skew(t0[:, :128]), skew(t0[:, 128:])
 
     def scores(tile, k, t):
         j0 = aligned(t * BK, BK)
         base = seq - row_block(k) * BQ
-        by_offset = dot_nn(q_off[k], relX[:, pl.ds(aligned(base + j0, 128), BK)])
-        content = dot_nn(q_row[k], kT[:, pl.ds(j0, BK)])
-        ri = jnp.where(t == 0, lax.rem(k, GROUP), GROUP)
+        by_offset = dot_nn(q_off[k, :, :KX], relX[:, pl.ds(aligned(base + j0, 128), BK)])
+        content = dot_nn(q_row[k, :, :dim], kT[:, pl.ds(j0, BK)])
+        ri = jnp.where(lax.rem(t, GROUP) == 0, lax.rem(k, GROUP), GROUP)
         rolled = [r_scr[ri, :, :128], r_scr[ri, :, 128:]]
         rolled += [skew(by_offset[:, m * 128:(m + 1) * 128]) for m in range(NC)]
         top_s = mx[k]
@@ -262,28 +273,27 @@
             tot = tot + p
             parts.append(p.astype(BF16))
         total[k] = tot
-        acc[k] += dot_nt(jnp.concatenate(parts, 1), vT[:, pl.ds(aligned(t * BK, BK), BK)])
+        acc[k, :, :dim] += dot_nt(jnp.concatenate(parts, 1), vT[:, pl.ds(aligned(t * BK, BK), BK)])
 
     def finish_rows(k):
         do_col[k] = flip_lanes(doT[:, slot_cols(k)], eye)
         do_row[k] = transposed(do_col[k])
         inv = 1.0 / jnp.sum(total[k], axis=1, keepdims=True)
-        out = acc[k] * inv
+        out = acc[k, :, :dim] * inv
         delta = jnp.sum(do_row[k].astype(F32) * out, axis=1, keepdims=True)
         total[k] = jnp.broadcast_to(inv, (BQ, 128))
         mx[k] = jnp.broadcast_to(delta, (BQ, 128))
         oT[:, slot_cols(k)] = flip_lanes(out.T.astype(BF16), eye)
-        acc[k] = jnp.zeros((BQ, dim), F32)
-
-    def grads(tile, k, t):
-        j0 = aligned(t * BK, BK)
-        base = seq - row_block(k) * BQ
-        js, us = pl.ds(j0, BK), pl.ds(aligned(base + j0 - 256, 128), BK)
-        dp = dot_nn(do_row[k], vT[:, js])
+        acc[k] = jnp.zeros((BQ, 2 * dim), F32)
+
+    def score_grads(k, t):
+        return dot_nn(do_row[k], vT[:, pl.ds(aligned(t * BK, BK), BK)])
+
+    def split_grads(tile, k, t, dp):
         inv, delta = total[k], mx[k]
-        prev = jnp.maximum(tile - 1, 0)
+        carry = (q_off, q_row)
         ps, dss = [], []
-        held = [jnp.where(t > 0, s_all[prev, :, m * 128:(m + 1) * 128], 0.0).astype(BF16) for m in range(2)]
+        held = [jnp.where(t > 0, c[k], jnp.zeros((BQ, 128), BF16)) for c in carry]
         for m in range(NC):
             p = s_all[tile, :, m * 128:(m + 1) * 128] * inv
             ds = (p * ((dp[:, m * 128:(m + 1) * 128] - delta) * scale)).astype(BF16)
@@ -291,55 +301,126 @@
             dss.append(ds)
             held.append(pltpu.roll(ds, 0, 1, stride=1, stride_axis=0))
         for m in range(2):
-            s_all[tile, :, m * 128:(m + 1) * 128] = held[NC + m].astype(F32)
+            carry[m][k] = held[NC + m]
         by_offset = []
         for m in range(NC):
             top = jnp.where(before, held[m + 1][:128], held[m + 2][:128])
             bot = jnp.where(before, held[m][128:], held[m + 1][128:])
             by_offset.append(jnp.concatenate([top, bot], 0))
-        p_all, ds_all, by_offset = (jnp.concatenate(x, 1) for x in (ps, dss, by_offset))
+        return tuple(jnp.concatenate(x, 1) for x in (ps, dss, by_offset))
+
+    def add_grads(k, t, p_all, ds_all, by_offset):
+        j0 = aligned(t * BK, BK)
+        base = seq - row_block(k) * BQ
+        js, us = pl.ds(j0, BK), pl.ds(aligned(base + j0 - 256, 128), BK)
         dvT[:, js] += dot_nn(do_col[k], p_all)
         dkT[:, js] += dot_nn(q_col[k], ds_all)
         drF[:, us] += dot_nn(qo_col[k], by_offset)
-        acc[k] += dot_nt(ds_all, kT[:, js])
-        gv[k] += dot_nt(by_offset, relX[:dim, us])
-
-    def walk(step, count, k, t_low, t_cap):
+        none = jnp.zeros((dim, BK), BF16)
+        keys = jnp.concatenate([jnp.concatenate([kT[:, js], none], 0), jnp.concatenate([none, relX[:dim, us]], 0)], 1)
+        acc[k] += dot_nt(jnp.concatenate([ds_all, by_offset], 1), keys)
+
+    def walk(steps, count, k, t_low, t_cap):
         def some(i, kt):
             k, t = kt
+            at = []
             for u in range(UNROLL):
-                step(k * (k + 1) // 2 + t, k, t)
+                at.append((k, t))
                 last = t == jnp.minimum(k, t_cap)
                 k, t = jnp.where(last, k + 1, k), jnp.where(last, t_low, t + 1)
+            steps(at)
             return k, t
 
         lax.fori_loop(0, count // UNROLL, some, (k, t_low))
+
+    def tile_of(k, t):
+        return k * (k + 1) // 2 + t
+
+    def grads(at):
+        d0 = score_grads(*at[0])
+        d1 = score_grads(*at[1])
+        g0 = split_grads(tile_of(*at[0]), *at[0], d0)
+        add_grads(*at[0], *g0)
+        d2 = score_grads(*at[2])
+        g1 = split_grads(tile_of(*at[1]), *at[1], d1)
+        add_grads(*at[1], *g1)
+        g2 = split_grads(tile_of(*at[2]), *at[2], d2)
+        add_grads(*at[2], *g2)
 
     def group_tiles(g):
         return GROUP * GROUP * g + GROUP * (GROUP + 1) // 2
 
     def over_tiles(step, g):
-        walk(step, group_tiles(g), GROUP * g, 0, nslot)
+        def steps(at):
+            for k, t in at:
+                step(tile_of(k, t), k, t)
+
+        walk(steps, group_tiles(g), GROUP * g, 0, nslot)
 
     def each(fn):
         lax.fori_loop(0, groups, lambda g, c: (fn(g), c)[1], 0)
 
-    def forward_scores(g):
-        for t in (0, 1):
-            pass_on(t, g)
-        for t in (0, 1):
-            from_mate(t, g)
+    orders = (((0, 0), (1, 1), (1, 0), (3, 0), (3, 1), (3, 3), (2, 0), (2, 1), (2, 2), (3, 2)),
+              ((1, 1), (0, 0), (1, 0), (3, 0), (3, 1), (3, 3), (2, 0), (2, 1), (2, 2), (3, 2)),
+              ((2, 2), (3, 3), (3, 2), (0, 0), (2, 0), (3, 0), (1, 1), (1, 0), (2, 1), (3, 1)),
+              ((3, 3), (2, 2), (3, 2), (0, 0), (2, 0), (3, 0), (1, 1), (1, 0), (2, 1), (3, 1)))
+
+    def schedule(order):
+        seen = ([], [], [])
+        rows = []
+        for gq, gk in order:
+            row = [gq, gk]
+            for t, g in ((0, gq - gk), (0, gq - gk - 1), (1, gk), (2, gq)):
+                new = g >= 0 and g not in seen[t]
+                row.append(g if new else -1)
+                if new:
+                    seen[t].append(g)
+            rows.append(row)
+        return rows
+
+    schedules = [schedule(order) for order in orders]
+
+    def look_up(x, column):
+        value = jnp.int32(-1)
+        for at in range(len(orders[0])):
+            here = jnp.int32(schedules[-1][at][column])
+            for z in range(groups - 1):
+                here = jnp.where(chip == z, schedules[z][at][column], here)
+            value = jnp.where(x == at, here, value)
+        return value
+
+    def forward_scores(x):
+        gq, gk, *need, new_q = (look_up(x, column) for column in range(6))
+        *ahead, ahead_q = (look_up(x + 1, column) for column in range(2, 6))
+
+        def arrives_now(g, q):
+            return (q >= 0) & ((g < groups // 2) != lower)
+
+        for t, g in zip((0, 0, 1), need):
+            pl.when((g >= 0) & ((x == 0) | arrives_now(g, new_q)))(functools.partial(pass_on, t, g))
+        for t, g, g1 in zip((0, 0, 1), need, ahead):
+            pl.when((g1 >= 0) & ~arrives_now(g1, ahead_q))(functools.partial(pass_on, t, g1))
+            pl.when(g >= 0)(functools.partial(from_mate, t, g))
+
+        @pl.when(new_q >= 0)
+        def _():
+            for i in range(GROUP):
+                row_landed(0, GROUP * new_q + i)
+            for i in range(GROUP):
+                prepare(GROUP * new_q + i)
+
+        pl.when(x == VALUES_AT)(send_values)
         for i in range(GROUP):
-            row_landed(0, GROUP * g + i)
-        for i in range(GROUP):
-            prepare(GROUP * g + i, i)
-        lower = chip < groups // 2
-        pl.when(g == jnp.where(lower, 3, 1))(send_values)
-        pl.when((g == 2) & ~lower)(send_cotangent)
-        over_tiles(scores, g)
-
-    each(forward_scores)
-    pl.when(chip < groups // 2)(send_cotangent)
+            prepare_skew(GROUP * gq + i, i, GROUP * gk)
+        count = jnp.where(gq == gk, GROUP * (GROUP + 1) // 2, GROUP * GROUP)
+        walk(score_tiles, count, GROUP * gq, GROUP * gk, GROUP * gk + GROUP - 1)
+
+    def score_tiles(at):
+        for k, t in at:
+            scores(tile_of(k, t), k, t)
+
+    lax.fori_loop(0, len(orders[0]), lambda x, c: (forward_scores(x), c)[1], 0)
+    send_cotangent()
     each(lambda g: pass_on(2, g))
 
     def row_max(g):
@@ -383,130 +464,168 @@
 
     parts, sinks = (drF, dkT, dvT), (dr_buf, dk_out, dv_out)
 
-    def pair(t, g, s):
-        return remote_copy(parts[t].at[:, col(t, 2 * g + 1 - core, 0)], pair_buf.at[t, s], send_p.at[t, s], recv_p.at[t, s], mate)
-
-    def sink(t, g, s):
-        return remote_copy(send_buf.at[t, s], sinks[t].at[chip], send_s.at[t, s], recv_s.at[t, chip], 2 * g + core)
-
-    def keep(t, s):
-        return pltpu.make_async_copy(send_buf.at[t, s], sinks[t].at[chip], loc_s.at[t])
-
-    def out_groups(step):
-        g = groups - 1 - step
-        return g, jnp.where(chip < groups // 2, g, step)
-
-    def combine(step, s):
-        gd, gk = out_groups(step)
-        for t, g in ((0, gd), (1, gk), (2, gk)):
-            mine = col(t, 2 * g + core, 0)
-            remote_copy(parts[t].at[:, mine], pair_buf.at[t, s], send_p.at[t, s], recv_p.at[t, s], mate).wait_recv()
-            send_buf[t, s] = (parts[t][:, mine] + pair_buf[t, s]).astype(BF16)
-        for t, g in ((0, gd), (1, gk), (2, gk)):
-            @pl.when(g != chip)
-            def _():
-                sink(t, g, s).start()
-
-            @pl.when(g == chip)
-            def _():
-                keep(t, s).start()
+    hw = blk // 2
+    slots = pair_buf.shape[1]
+
+    def out_block(t, step):
+        return n - 1 - step if t == 0 else jnp.where(lower, n - 1 - step, step)
+
+    def half_of(t, step, c):
+        b = out_block(t, step)
+        b = n - 1 - b if t == 0 else b
+        return pl.ds(aligned(b * blk + c * hw, 128), hw)
+
+    def pair(t, step):
+        s = lax.rem(step, slots)
+        return remote_copy(parts[t].at[:, half_of(t, step, 1 - core)], pair_buf.at[t, s], send_p.at[t, s], recv_p.at[t, s], mate)
+
+    def ready(t, step):
+        return dr_send.at[step] if t == 0 else send_buf.at[t - 1, step]
+
+    def sink_at(t, h, c):
+        return sinks[t].at[h, :, pl.ds(aligned(c * hw, 128), hw)]
+
+    def sink(t, step):
+        return remote_copy(ready(t, step), sink_at(t, chip, core), send_s.at[t, step], recv_s.at[t, chip, core], out_block(t, step))
+
+    def keep(t, step):
+        return pltpu.make_async_copy(ready(t, step), sink_at(t, chip, core), loc_s.at[t])
+
+    def combine(t, step):
+        s = lax.rem(step, slots)
+        mine = half_of(t, step, core)
+        remote_copy(parts[t].at[:, mine], pair_buf.at[t, s], send_p.at[t, s], recv_p.at[t, s], mate).wait_recv()
+        ready(t, step)[...] = (parts[t][:, mine] + pair_buf[t, s]).astype(BF16)
+
+    def to_owner(t, step, wait):
+        b = out_block(t, step)
+
+        @pl.when(b != me)
+        def _():
+            sink(t, step).wait_send() if wait else sink(t, step).start()
+
+        @pl.when(b == me)
+        def _():
+            keep(t, step).wait() if wait else keep(t, step).start()
+
+    def arrived(t):
+        for h in range(heads):
+            for c in range(2):
+                @pl.when(2 * h + c != me)
+                def _():
+                    remote_copy(ready(t, 0), sink_at(t, h, c), send_s.at[t, 0], recv_s.at[t, h, c], me).wait_recv()
+
+    def final_slots(step, fn):
+        first, end = (3 * step + 1) // 2, (3 * step + 4) // 2
+        for i in range(2):
+            at = first + i
+            pl.when(at < end)(functools.partial(fn, jnp.where(lower, nslot - 1 - at, at)))
+
+    def row_grads(k):
+        dqT[:, slot_cols(k)] = flip_lanes((acc[k, :, :dim] + acc[k, :, dim:]).T.astype(BF16), eye)
+
+    def exchange(step):
+        for t in range(3):
+            pl.when(step >= slots)(pair(t, step - slots).wait_send)
+            pair(t, step).start()
+        final_slots(step, row_grads)
+
+    def release(step):
+        combine(0, step)
+        to_owner(0, step, False)
+        for t in (1, 2):
+            combine(t, step)
+        for t in (1, 2):
+            to_owner(t, step, False)
+        final_slots(step, lambda k: out_rows(1, k, False))
 
     w_acc, w_in, w_half, w_part, w_mine = (9, 0), (10, 0), (10, 1), (11, 0), (11, 1)
-
-    def place(kt, c=0):
-        return kt[0] * (kt[0] + 1) // 2 + kt[1] + c
-
+    chunks, wide = range(4), BK // 2
     half = heads * dim // 2
     piece = half // heads
 
+    def place(kt, c, row0, count):
+        at = kt[0] * (kt[0] + 1) // 2 + kt[1]
+        return s_all.at[at, pl.ds(row0, count), pl.ds(c % 2 * wide, wide)]
+
+    def acc_at(c, row0, count):
+        return place((w_acc[0], w_acc[1] + c // 2), c, row0, count)
+
     def swap(c):
-        return remote_copy(s_all.at[place(w_acc, c), pl.ds(aligned((1 - core) * half, half), half)],
-                           s_all.at[place(w_in), pl.ds(c * half, half)], send_w.at[0, c], recv_w.at[0, c], mate)
+        return remote_copy(acc_at(c, aligned((1 - core) * half, half), half), place(w_in, c, c // 2 * half, half),
+                           send_w.at[0, c], recv_w.at[0, c], mate)
 
     def spread(i, c):
         z = lax.rem(chip + i, heads)
-        return remote_copy(s_all.at[place(w_half), pl.ds(aligned(c * half + z * piece, piece), piece)],
-                           s_all.at[place(w_part), pl.ds((2 * i + c) * piece, piece)], send_w.at[i, c], recv_w.at[i, c], 2 * z + core)
+        return remote_copy(place(w_half, c, aligned(c // 2 * half + z * piece, piece), piece),
+                           place(w_part, c, (2 * i + c // 2) * piece, piece), send_w.at[i, c], recv_w.at[i, c], 2 * z + core)
 
     def table_grad():
-        for h in range(heads):
-            @pl.when(h != chip)
-            def _():
-                remote_copy(send_buf.at[0, 0], dr_buf.at[h], send_s.at[0, 0], recv_s.at[0, h], me).wait_recv()
-
-            @pl.when(h == chip)
-            def _():
-                keep(0, 0).wait()
+        arrived(0)
+        keep(0, 0).wait()
         dr = jnp.concatenate([flip_lanes(dr_buf[h], eye) for h in range(heads)], 0)
-        for c in range(2):
-            s_all[place(w_acc, c)] = dot_nn(dr, table[:, c * BK:(c + 1) * BK])
-        for c in range(2):
+        for c in chunks:
+            acc_at(c, 0, 2 * half)[...] = dot_nn(dr, table[:, c * wide:(c + 1) * wide])
+        for c in chunks:
             swap(c).start()
-        for c in range(2):
+        for c in chunks:
             swap(c).wait()
-            s_all[place(w_half), c * half:(c + 1) * half] = (
-                s_all[place(w_acc, c), pl.ds(aligned(core * half, half), half)] + s_all[place(w_in), c * half:(c + 1) * half])
-        for i in range(1, heads):
-            for c in range(2):
+            place(w_half, c, c // 2 * half, half)[...] = (
+                acc_at(c, aligned(core * half, half), half)[...] + place(w_in, c, c // 2 * half, half)[...])
+        for c in chunks:
+            for i in (3, 2, 1):
                 spread(i, c).start()
 
-    def backward_step(step):
-        gd, gk = out_groups(step)
-        left = chip < groups // 2
-        s = lax.rem(step, 2)
-        walk(grads, group_tiles(gd), GROUP * gk, jnp.where(left, 0, GROUP * step), jnp.where(left, nslot, GROUP * step + GROUP - 1))
-
-        @pl.when(step > 1)
-        def _():
-            pd, pk = out_groups(step - 2)
-            for t, g, p in ((0, gd, pd), (1, gk, pk), (2, gk, pk)):
-                pair(t, p, s).wait_send()
-
-                @pl.when(p != chip)
-                def _():
-                    sink(t, p, s).wait_send()
-
-                @pl.when((p == chip) & (t > 0))
-                def _():
-                    keep(t, s).wait()
-
-        for t, g in ((0, gd), (1, gk), (2, gk)):
-            pair(t, g, s).start()
-        for i in range(GROUP):
-            k = GROUP * gk + i
-            dqT[:, slot_cols(k)] = flip_lanes((acc[k] + gv[k]).T.astype(BF16), eye)
-        combine(step, s)
-        for i in range(GROUP):
-            out_rows(1, GROUP * gk + i, False)
-
-        pl.when((step > 0) & (chip == groups - step))(table_grad)
-
-    each(backward_step)
-    for t, ref in ((0, acc), (1, gv)):
-        rows_sum = jnp.sum(ref[...].reshape(nslot * BQ // 8, 8, dim), axis=0)
-        bias_buf[me, t] = jnp.sum(rows_sum, axis=0, keepdims=True) + jnp.zeros((8, dim), F32)
+    bodies, done = [], 0
+    for step in range(n):
+        tiles_done = sum(nslot - i for i in range((3 * step + 4) // 2))
+        bodies.append(-(-tiles_done // UNROLL) - done)
+        done += bodies[-1]
+    phases = [c for b in bodies[:-1] for c in (min(b, 1), max(b - 1, 0))]
+
+    def next_tile(k, t):
+        last = jnp.where(lower, t == k, k == nslot - 1)
+        k1 = jnp.where(lower, k - 1, t + 1)
+        return (jnp.where(last, k1, jnp.where(lower, k, k + 1)), jnp.where(last, jnp.where(lower, 0, t + 1), jnp.where(lower, t + 1, t)))
+
+    def phase(x, kt):
+        count = jnp.int32(0)
+        for at, c in enumerate(phases):
+            count = jnp.where(x == at, c, count)
+
+        def some(i, kt):
+            at = []
+            for u in range(UNROLL):
+                at.append(kt)
+                kt = next_tile(*kt)
+            grads(at)
+            return kt
+
+        kt = lax.fori_loop(0, count, some, kt)
+        pl.when(lax.rem(x, 2) == 1)(lambda: exchange(x // 2))
+        pl.when((lax.rem(x, 2) == 0) & (x > 0))(lambda: release(x // 2 - 1))
+        return kt
+
+    lax.fori_loop(0, len(phases), phase, (jnp.where(lower, nslot - 1, 0), jnp.int32(0)))
+    exchange(n - 1)
+    release(n - 2)
+    release(n - 1)
+    rows_sum = jnp.sum(jnp.sum(acc[...].reshape(nslot * BQ // 8, 8, 2 * dim), axis=0), axis=0, keepdims=True)
+    for t in range(2):
+        bias_buf[me, t] = rows_sum[:, t * dim:(t + 1) * dim] + jnp.zeros((8, dim), F32)
 
     def bias(o):
         return remote_copy(bias_buf.at[me], bias_buf.at[me], send_b.at[o], recv_b2.at[me], lax.rem(me + o, n))
 
     for o in range(1, n):
         bias(o).start()
-    pl.when(chip == 0)(table_grad)
-    for i in range(1, heads):
-        for c in range(2):
-            spread(i, c).wait()
-    mine = place(w_mine)
-    for c in range(2):
-        got = s_all[place(w_half), pl.ds(aligned(c * half + chip * piece, piece), piece)]
-        for i in range(1, heads):
-            got = got + s_all[place(w_part), (2 * i + c) * piece:(2 * i + c + 1) * piece]
-        s_all[mine, c * piece:(c + 1) * piece] = got
+    table_grad()
 
     def home(co, z, c):
-        return dw_out.at[pl.ds(aligned(co * half + z * piece, piece), piece), pl.ds(c * BK, BK)]
+        return dw_out.at[pl.ds(aligned(co * half + z * piece, piece), piece), pl.ds(c * wide, wide)]
 
     def my_piece(c):
-        return s_all.at[mine, pl.ds(c * piece, piece)]
+        return place(w_mine, c, c // 2 * piece, piece)
 
     def collect(i, c):
         z = lax.rem(chip + i, heads)
@@ -519,14 +638,20 @@
     def stay(c):
         return pltpu.make_async_copy(my_piece(c), home(core, chip, c), loc_w.at[c])
 
-    for c in range(2):
+    for c in chunks:
+        for i in range(1, heads):
+            spread(i, c).wait()
+        got = place(w_half, c, aligned(c // 2 * half + chip * piece, piece), piece)[...]
+        for i in range(1, heads):
+            got = got + place(w_part, c, (2 * i + c // 2) * piece, piece)[...]
+        my_piece(c)[...] = got
         for i in range(1, heads):
             collect(i, c).start()
         hand_over(0, c).start()
         stay(c).start()
-    for i in range(1, heads):
-        z = lax.rem(chip + i, heads)
-        for c in range(2):
+    for c in chunks:
+        for i in range(1, heads):
+            z = lax.rem(chip + i, heads)
             remote_copy(my_piece(c), home(core, z, c), send_w.at[0, c], recv_w.at[4 + z, c], me).wait_recv()
             hand_over(i, c).start()
     for o in range(1, n):
@@ -535,7 +660,7 @@
     for t in range(2):
         bias_out[t] = jnp.concatenate([bias_buf[2 * h, t, :1] + bias_buf[2 * h + 1, t, :1] for h in range(heads)], 0)
 
-    for c in range(2):
+    for c in chunks:
         stay(c).wait()
         for i in range(heads):
             remote_copy(my_piece(c), home(1 - core, i, c), send_w.at[0, c], recv_w.at[8 + i, c], me).wait_recv()
@@ -544,32 +669,26 @@
                 collect(i, c).wait_send()
     for o in range(1, n):
         bias(o).wait_send()
+    for step in range(n):
+        pl.when(out_block(0, step) != me)(sink(0, step).wait_send)
     for t in range(3):
-        for step in (groups - 2, groups - 1):
-            gd, gk = out_groups(step)
-            g = gk if t else gd
-            pair(t, g, step % 2).wait_send()
-
-            @pl.when(g != chip)
-            def _():
-                sink(t, g, step % 2).wait_send()
-
-            if t:
-                @pl.when(g == chip)
-                def _():
-                    keep(t, step % 2).wait()
+        for step in range(n - slots, n):
+            pair(t, step).wait_send()
+        if t:
+            for step in range(n):
+                to_owner(t, step, True)
+            arrived(t)
         if t:
             to_mate(t).wait_send()
         for i in range(1, heads):
             h = lax.rem(chip + i, heads)
             forward(t, h).wait_send()
             if t:
-                direct(t, i).wait_send()
-                remote_copy(send_buf.at[t, 0], sinks[t].at[h], send_s.at[t, 0], recv_s.at[t, h], me).wait_recv()
+                direct(t, h).wait_send()
     for t in (0, 1):
         for i in range(heads):
             for j in range(per_blk):
-                to = 2 * lax.rem(chip + i, heads) + owner_core(me * per_blk + j)
+                to = 2 * i + owner_core(me * per_blk + j)
 
                 @pl.when(to != me)
                 def _():
@@ -609,16 +728,16 @@
             scratch_shapes=[
                 buf((dim, rows), BF16), buf((dim, rows), BF16), buf((dim, seq), BF16), buf((dim, seq), BF16), buf((KX, seq + PAD), BF16),
                 buf((dim, rows), BF16), buf((dim, rows), BF16), buf((dim, seq), F32), buf((dim, seq), F32), buf((dim, seq + PAD), F32),
-                buf((tiles, BQ, BK), F32), buf((nslot, BQ, KX), BF16), buf((nslot, BQ, dim), BF16), buf((nslot, BQ, dim), BF16),
+                buf((tiles, BQ, BK), F32), buf((nslot, BQ, 128), BF16), buf((nslot, BQ, 128), BF16), buf((nslot, BQ, dim), BF16),
                 buf((nslot, dim, BQ), BF16), buf((nslot, dim, BQ), BF16), buf((nslot, dim, BQ), BF16),
-                buf((nslot, BQ, 128), F32), buf((nslot, BQ, 128), F32), buf((nslot, BQ, dim), F32), buf((nslot, BQ, dim), F32),
+                buf((nslot, BQ, 128), F32), buf((nslot, BQ, 128), F32), buf((nslot, BQ, 2 * dim), F32),
                 buf((GROUP + 1, BQ, 256), F32),
-                buf((3, 2, dim, blk), F32), buf((3, 2, dim, blk), BF16), buf((heads, dim, blk), BF16), buf((blk, model), BF16),
+                buf((3, 4, dim, blk // 2), F32), buf((n, dim, blk // 2), BF16), buf((2, n, dim, blk // 2), BF16), buf((heads, dim, blk), BF16), buf((blk, model), BF16),
                 buf((n, 2, 8, dim), F32),
                 dma((3, heads)), dma((3, heads)), dma((2, heads, per_blk)), dma((3, n)), dma((2, nslot)), dma((3,)), dma((2, per_blk)),
-                dma((2, nslot)), dma((2, heads, per_blk)), dma((2, per_blk)), dma((3, 2)), dma((3, 2)),
-                dma((3, 2)), dma((3, heads)), dma((3,)),
-                dma, dma((12, 2)), dma((12, 2)), dma((2,)), dma((n,)), dma((n,))],
+                dma((2, nslot)), dma((2, heads, per_blk)), dma((2, per_blk)), dma((3, 4)), dma((3, 4)),
+                dma((3, n)), dma((3, heads, 2)), dma((3,)),
+                dma, dma((12, 4)), dma((12, 4)), dma((4,)), dma((n,)), dma((n,))],
             compiler_params=pltpu.CompilerParams(collective_id=0, has_side_effects=True, vmem_limit_bytes=67043328),
             name='attention',
         )(qT, kT, vT, doT, rel_table, wT, u_bias, v_bias)

time: 165 us -> 142 us (0.86)
  Pallas kernels: 165 us -> 141 us
    pallas_call x1, Pallas kernels: 162 us -> 138 us  [local_fn(): pl.pallas_call(functools.partial(attention_kernel, n), out_shape=[sds((he...]
where the time goes in v4:
time: 142 us
  Pallas kernels  141 us (99%)
    pallas_call x1, Pallas kernels, local_fn(): pl.pallas_call(functools.partial(attention_kernel, n), out_shape=[sds((he...  138 us
    pallas_call x1, Pallas kernels, local_fn(): pl.pallas_call(hand_off_kernel, grid=(steps,), out_shape=[sds((heads, dim...  3 us

profile of v4, /device:TPU:0, one launch (start us, length us, event | category | flops | bytes accessed | tf_op | source)
XLA Modules:
  0.0 141.9 jit_solution(479322351949164546)
XLA Ops:
  0.6 138.3 %attention.1 = (bf16[4,64,768]{2,1,0:T(8,128)(2,1)}, bf16[4,64,768]{2,1,0:T(8,128)(2,1)}, bf16[4,64,768]{2,1,0:T(8,128)(2,1)}, bf16[4,64,768]{2,1,0:T(8,128)(2,1...) custom-call(bf16[4,64,768]{2,1,0:T(8,128)(2,1)} %bitcast.15, bf16[4,64,768]{2,1,0:T(8,128)(2,1)} %bitcast.16, ...), custom_call_target="tpu_custom_call" | custom-call | tf_op jit(solution)/shard_map/attention/pallas_call | solution.py:724
  138.9 3.0 %hand_off.1 = (bf16[4,64,768]{2,1,0:T(8,128)(2,1)}, bf16[4,64,768]{2,1,0:T(8,128)(2,1)}, bf16[4,64,768]{2,1,0:T(8,128)(2,1)}, bf16[4,64,768]{2,1,0:T(8,128)(2,1)...) custom-call(bf16[4,64,768]{2,1,0:T(8,128)(2,1)} %get-tuple-element.20.o, ...), custom_call_target="tpu_custom_call" | custom-call | tf_op jit(solution)/shard_map/hand_off/pallas_call | solution.py:748

commit v5 on v4

--- a/solution.py
+++ b/solution.py
@@ -11,11 +11,13 @@
 LOG2E = math.log2(math.e)
 BQ = 256
 BK = 512
-NC = BK // 128
+LANES = 128
+NC = BK // LANES
 PAD = 512
 KX = 80
 GROUP = 3
-UNROLL = 3
+UNROLL_SUM = 13
+UNROLL_GRAD = 6
 VALUES_AT = 6
 MESH_ID = pl.DeviceIdType.MESH
 
@@ -26,6 +28,10 @@
 
 def dot_nt(a, b):
     return lax.dot_general(a, b, (((1,), (1,)), ((), ())), preferred_element_type=F32)
+
+
+def lanes(m, count=1):
+    return slice(m * LANES, (m + count) * LANES)
 
 
 def aligned(x, m):
@@ -59,12 +65,15 @@
                                         device_id_type=MESH_ID)
 
 
-def barrier_all(n):
+def greet_all(n):
     me, hp = lax.axis_index('cp'), lax.axis_index('hp')
     bar = pltpu.get_barrier_semaphore()
     for o in range(1, n):
         pl.semaphore_signal(bar, 1, device_id=(hp, lax.rem(me + o, n)), device_id_type=MESH_ID)
-    pl.semaphore_wait(bar, n - 1)
+
+
+def await_all(n):
+    pl.semaphore_wait(pltpu.get_barrier_semaphore(), n - 1)
 
 
 def hand_off_kernel(o, dq, dk, dv, dw, bias, o_out, dq_out, dk_out, dv_out, dw_out, u_out, v_out):
@@ -79,8 +88,9 @@
                      s_all, q_off, q_row, do_row, q_col, qo_col, do_col, mx, total, acc, r_scr,
                      pair_buf, dr_send, send_buf, dr_buf, table, bias_buf,
                      send_d, send_f, send_q, recv_b, recv_q, loc_b, loc_q,
-                     send_o, recv_o, loc_o, send_p, recv_p, send_s, recv_s, loc_s,
-                     loc_t, send_w, recv_w, loc_w, send_b, recv_b2):
+                     send_o, recv_o, send_p, recv_p, send_s, recv_s,
+                     loc_t, send_w, recv_w, loc_w, send_b, recv_b2,
+                     recv_u, recv_d2, recv_c, recv_h, send_x):
     me = lax.axis_index('cp')
     chip, core = me // 2, lax.rem(me, 2)
     mate = 2 * chip + 1 - core
@@ -89,9 +99,17 @@
     per_blk = blk // BQ
     groups = n // 2
     nslot = qT.shape[1] // BQ
+    tiles = s_all.shape[0]
     scale = dim ** -0.5
-    pltpu.make_async_copy(table_in, table, loc_t).start()
-    barrier_all(n)
+    model = table.shape[1]
+
+    def weight_block(m):
+        return pltpu.make_async_copy(w_rel.at[:, pl.ds(m * LANES, LANES)], q_off.at[m], loc_t.at[1 + m])
+
+    greet_all(n)
+    pltpu.make_async_copy(table_in, table, loc_t.at[0]).start()
+    for m in range(model // LANES):
+        weight_block(m).start()
 
     rel_buf = dr_buf
     srcs, fulls = (rel_buf, k_in, v_in), (relX, kT, vT)
@@ -175,15 +193,19 @@
         direct(1, h).start()
         send_rows(0, h)
 
+    eye = anti_eye(BQ)
+    pltpu.make_async_copy(table_in, table, loc_t.at[0]).wait()
+    for m in range(model // LANES):
+        weight_block(m).wait()
+    weights_in = jnp.concatenate([q_off[m] for m in range(model // LANES)], 1)
+    rel = flip_lanes(dot_nt(weights_in, table[...]).astype(BF16), eye)
+    for h in range(heads):
+        rel_buf[h] = rel[h * dim:(h + 1) * dim]
+    await_all(n)
     to_mate(1).start()
     own(1).start()
     send_scores_input(side)
     send_rows(0, chip)
-    eye = anti_eye(BQ)
-    pltpu.make_async_copy(table_in, table, loc_t).wait()
-    rel = flip_lanes(dot_nt(w_rel[...], table[...]).astype(BF16), eye)
-    for h in range(heads):
-        rel_buf[h] = rel[h * dim:(h + 1) * dim]
     to_mate(0).start()
     own(0).start()
     for h in (side, *across):
@@ -212,14 +234,14 @@
     relX[pl.ds(dim, KX - dim), pl.ds(0, seq)] = jnp.zeros((KX - dim, seq), BF16)
     relX[pl.ds(dim, KX - dim), pl.ds(seq, PAD)] = jnp.where(first, -jnp.inf, 0.0).astype(BF16)
     ones_col = (lax.broadcasted_iota(jnp.int32, (BQ, KX - dim), 1) == 0).astype(F32).astype(BF16)
-    lane = lax.broadcasted_iota(jnp.int32, (128, 128), 1)
-    row = lax.broadcasted_iota(jnp.int32, (128, 128), 0)
+    lane = lax.broadcasted_iota(jnp.int32, (128, LANES), 1)
+    row = lax.broadcasted_iota(jnp.int32, (128, LANES), 0)
     past, before = lane > row, lane < row
 
     def bias_col(ref):
         pick = lax.broadcasted_iota(jnp.int32, ref.shape, 0) == chip
         r = jnp.sum(jnp.where(pick, ref[...], 0.0), axis=0, keepdims=True)
-        return jnp.broadcast_to(r, (128, dim)).T[:, :1]
+        return jnp.broadcast_to(r, (LANES, dim)).T[:, :1]
 
     u_col, v_col = bias_col(ub), bias_col(vb)
 
@@ -242,38 +264,45 @@
 
     def prepare_skew(k, i, t):
         start = seq - row_block(k) * BQ + t * BK - 256
-        t0 = dot_nn(q_off[k, :, :KX], relX[:, pl.ds(aligned(start, 128), 256)])
-        r_scr[i, :, :128], r_scr[i, :, 128:] = skew(t0[:, :128]), skew(t0[:, 128:])
-
-    def scores(tile, k, t):
+        t0 = dot_nn(q_off[k, :, :KX], relX[:, pl.ds(aligned(start, LANES), 256)])
+        for m in range(2):
+            r_scr[i, :, lanes(m)] = skew(t0[:, lanes(m)])
+
+    def score_products(k, t):
         j0 = aligned(t * BK, BK)
         base = seq - row_block(k) * BQ
-        by_offset = dot_nn(q_off[k, :, :KX], relX[:, pl.ds(aligned(base + j0, 128), BK)])
-        content = dot_nn(q_row[k, :, :dim], kT[:, pl.ds(j0, BK)])
+        by_offset = dot_nn(q_off[k, :, :KX], relX[:, pl.ds(aligned(base + j0, LANES), BK)])
+        return by_offset, dot_nn(q_row[k, :, :dim], kT[:, pl.ds(j0, BK)])
+
+    def scores(k, t, by_offset, content):
         ri = jnp.where(lax.rem(t, GROUP) == 0, lax.rem(k, GROUP), GROUP)
-        rolled = [r_scr[ri, :, :128], r_scr[ri, :, 128:]]
-        rolled += [skew(by_offset[:, m * 128:(m + 1) * 128]) for m in range(NC)]
+        rolled = [r_scr[ri, :, lanes(m)] for m in range(2)]
+        rolled += [skew(by_offset[:, lanes(m)]) for m in range(NC)]
         top_s = mx[k]
         for m in range(NC):
-            top = jnp.where(past, rolled[m + 2][:128], rolled[m + 1][:128])
-            bot = jnp.where(past, rolled[m + 1][128:], rolled[m][128:])
-            s = content[:, m * 128:(m + 1) * 128] + reverse_rows(jnp.concatenate([top, bot], 0))
+            top = jnp.where(past, rolled[m + 2][:LANES], rolled[m + 1][:LANES])
+            bot = jnp.where(past, rolled[m + 1][LANES:], rolled[m][LANES:])
+            s = content[:, lanes(m)] + reverse_rows(jnp.concatenate([top, bot], 0))
             s = s * (scale * LOG2E)
-            s_all[tile, :, m * 128:(m + 1) * 128] = s
+            s_all[tile_of(k, t), :, lanes(m)] = s
             top_s = jnp.maximum(top_s, s)
         mx[k] = top_s
-        r_scr[GROUP, :, :128], r_scr[GROUP, :, 128:] = rolled[NC], rolled[NC + 1]
-
-    def weigh(tile, k, t):
-        top_s, tot = mx[k], total[k]
+        for m in range(2):
+            r_scr[GROUP, :, lanes(m)] = rolled[NC + m]
+
+    def weights(k, t):
+        tile, top_s, tot = tile_of(k, t), mx[k], total[k]
         parts = []
         for m in range(NC):
-            p = jnp.exp2(s_all[tile, :, m * 128:(m + 1) * 128] - top_s)
-            s_all[tile, :, m * 128:(m + 1) * 128] = p
+            p = jnp.exp2(s_all[tile, :, lanes(m)] - top_s)
+            s_all[tile, :, lanes(m)] = p
             tot = tot + p
             parts.append(p.astype(BF16))
         total[k] = tot
-        acc[k, :, :dim] += dot_nt(jnp.concatenate(parts, 1), vT[:, pl.ds(aligned(t * BK, BK), BK)])
+        return jnp.concatenate(parts, 1)
+
+    def add_values(k, t, p_all):
+        acc[k, :, :dim] += dot_nt(p_all, vT[:, pl.ds(aligned(t * BK, BK), BK)])
 
     def finish_rows(k):
         do_col[k] = flip_lanes(doT[:, slot_cols(k)], eye)
@@ -281,8 +310,8 @@
         inv = 1.0 / jnp.sum(total[k], axis=1, keepdims=True)
         out = acc[k, :, :dim] * inv
         delta = jnp.sum(do_row[k].astype(F32) * out, axis=1, keepdims=True)
-        total[k] = jnp.broadcast_to(inv, (BQ, 128))
-        mx[k] = jnp.broadcast_to(delta, (BQ, 128))
+        total[k] = jnp.broadcast_to(inv, (BQ, LANES))
+        mx[k] = jnp.broadcast_to(delta, (BQ, LANES))
         oT[:, slot_cols(k)] = flip_lanes(out.T.astype(BF16), eye)
         acc[k] = jnp.zeros((BQ, 2 * dim), F32)
 
@@ -293,10 +322,10 @@
         inv, delta = total[k], mx[k]
         carry = (q_off, q_row)
         ps, dss = [], []
-        held = [jnp.where(t > 0, c[k], jnp.zeros((BQ, 128), BF16)) for c in carry]
+        held = [jnp.where(t > 0, c[k], jnp.zeros((BQ, LANES), BF16)) for c in carry]
         for m in range(NC):
-            p = s_all[tile, :, m * 128:(m + 1) * 128] * inv
-            ds = (p * ((dp[:, m * 128:(m + 1) * 128] - delta) * scale)).astype(BF16)
+            p = s_all[tile, :, lanes(m)] * inv
+            ds = (p * ((dp[:, lanes(m)] - delta) * scale)).astype(BF16)
             ps.append(p.astype(BF16))
             dss.append(ds)
             held.append(pltpu.roll(ds, 0, 1, stride=1, stride_axis=0))
@@ -304,15 +333,15 @@
             carry[m][k] = held[NC + m]
         by_offset = []
         for m in range(NC):
-            top = jnp.where(before, held[m + 1][:128], held[m + 2][:128])
-            bot = jnp.where(before, held[m][128:], held[m + 1][128:])
+            top = jnp.where(before, held[m + 1][:LANES], held[m + 2][:LANES])
+            bot = jnp.where(before, held[m][LANES:], held[m + 1][LANES:])
             by_offset.append(jnp.concatenate([top, bot], 0))
         return tuple(jnp.concatenate(x, 1) for x in (ps, dss, by_offset))
 
     def add_grads(k, t, p_all, ds_all, by_offset):
         j0 = aligned(t * BK, BK)
         base = seq - row_block(k) * BQ
-        js, us = pl.ds(j0, BK), pl.ds(aligned(base + j0 - 256, 128), BK)
+        js, us = pl.ds(j0, BK), pl.ds(aligned(base + j0 - 256, LANES), BK)
         dvT[:, js] += dot_nn(do_col[k], p_all)
         dkT[:, js] += dot_nn(q_col[k], ds_all)
         drF[:, us] += dot_nn(qo_col[k], by_offset)
@@ -320,50 +349,52 @@
         keys = jnp.concatenate([jnp.concatenate([kT[:, js], none], 0), jnp.concatenate([none, relX[:dim, us]], 0)], 1)
         acc[k] += dot_nt(jnp.concatenate([ds_all, by_offset], 1), keys)
 
-    def walk(steps, count, k, t_low, t_cap):
+    def walk(steps, count, k, t_low, t_cap, unroll):
         def some(i, kt):
             k, t = kt
             at = []
-            for u in range(UNROLL):
+            for u in range(unroll):
                 at.append((k, t))
                 last = t == jnp.minimum(k, t_cap)
                 k, t = jnp.where(last, k + 1, k), jnp.where(last, t_low, t + 1)
             steps(at)
             return k, t
 
-        lax.fori_loop(0, count // UNROLL, some, (k, t_low))
+        lax.fori_loop(0, count // unroll, some, (k, t_low))
 
     def tile_of(k, t):
         return k * (k + 1) // 2 + t
 
     def grads(at):
-        d0 = score_grads(*at[0])
-        d1 = score_grads(*at[1])
-        g0 = split_grads(tile_of(*at[0]), *at[0], d0)
-        add_grads(*at[0], *g0)
-        d2 = score_grads(*at[2])
-        g1 = split_grads(tile_of(*at[1]), *at[1], d1)
-        add_grads(*at[1], *g1)
-        g2 = split_grads(tile_of(*at[2]), *at[2], d2)
-        add_grads(*at[2], *g2)
+        count = len(at)
+        dps = [score_grads(*at[0])]
+        for u, here in enumerate(at):
+            if u + 1 < count:
+                dps.append(score_grads(*at[u + 1]))
+            add_grads(*here, *split_grads(tile_of(*here), *here, dps[u]))
 
     def group_tiles(g):
         return GROUP * GROUP * g + GROUP * (GROUP + 1) // 2
 
-    def over_tiles(step, g):
-        def steps(at):
-            for k, t in at:
-                step(tile_of(k, t), k, t)
-
-        walk(steps, group_tiles(g), GROUP * g, 0, nslot)
+    def score_tiles(at):
+        products = score_products(*at[0])
+        for u, here in enumerate(at):
+            ahead = score_products(*at[u + 1]) if u + 1 < len(at) else None
+            scores(*here, *products)
+            products = ahead
+
+    def weigh_tiles(at):
+        p_all = weights(*at[0])
+        for u, here in enumerate(at):
+            ahead = weights(*at[u + 1]) if u + 1 < len(at) else None
+            add_values(*here, p_all)
+            p_all = ahead
 
     def each(fn):
         lax.fori_loop(0, groups, lambda g, c: (fn(g), c)[1], 0)
 
-    orders = (((0, 0), (1, 1), (1, 0), (3, 0), (3, 1), (3, 3), (2, 0), (2, 1), (2, 2), (3, 2)),
-              ((1, 1), (0, 0), (1, 0), (3, 0), (3, 1), (3, 3), (2, 0), (2, 1), (2, 2), (3, 2)),
-              ((2, 2), (3, 3), (3, 2), (0, 0), (2, 0), (3, 0), (1, 1), (1, 0), (2, 1), (3, 1)),
-              ((3, 3), (2, 2), (3, 2), (0, 0), (2, 0), (3, 0), (1, 1), (1, 0), (2, 1), (3, 1)))
+    orders = ('00111030313320212232', '11001030313320212232', '22333200203011102131', '33223200203011102131')
+    orders = [[(int(word[at]), int(word[at + 1])) for at in range(0, len(word), 2)] for word in orders]
 
     def schedule(order):
         seen = ([], [], [])
@@ -412,12 +443,9 @@
         pl.when(x == VALUES_AT)(send_values)
         for i in range(GROUP):
             prepare_skew(GROUP * gq + i, i, GROUP * gk)
-        count = jnp.where(gq == gk, GROUP * (GROUP + 1) // 2, GROUP * GROUP)
-        walk(score_tiles, count, GROUP * gq, GROUP * gk, GROUP * gk + GROUP - 1)
-
-    def score_tiles(at):
-        for k, t in at:
-            scores(tile_of(k, t), k, t)
+        here = GROUP * gq, GROUP * gk, GROUP * gk + GROUP - 1
+        pl.when(gq == gk)(lambda: walk(score_tiles, GROUP * (GROUP + 1) // 2, *here, GROUP * (GROUP + 1) // 2))
+        pl.when(gq != gk)(lambda: walk(score_tiles, GROUP * GROUP, *here, GROUP * GROUP))
 
     lax.fori_loop(0, len(orders[0]), lambda x, c: (forward_scores(x), c)[1], 0)
     send_cotangent()
@@ -426,31 +454,28 @@
     def row_max(g):
         for i in range(GROUP):
             k = GROUP * g + i
-            mx[k] = jnp.broadcast_to(jnp.max(mx[k], axis=1, keepdims=True), (BQ, 128))
+            mx[k] = jnp.broadcast_to(jnp.max(mx[k], axis=1, keepdims=True), (BQ, LANES))
 
     each(row_max)
 
-    def weigh_group(g):
-        from_mate(2, g)
-        over_tiles(weigh, g)
-
-    each(weigh_group)
-
-    def out_rows(t, k, wait):
+    each(lambda g: from_mate(2, g))
+    walk(weigh_tiles, tiles, 0, 0, nslot, UNROLL_SUM)
+
+    def out_rows(t, k):
         rb = row_block(k)
         to, j = rb // per_blk, lax.rem(rb, per_blk)
         src = (oT, dqT)[t].at[:, slot_cols(k)]
         dst = (o_out, dq_out)[t].at[chip, :, pl.ds(aligned(j * BQ, BQ), BQ)]
-
-        @pl.when(to != me)
-        def _():
-            c = remote_copy(src, dst, send_o.at[t, k], recv_o.at[t, chip, j], to)
-            c.wait_send() if wait else c.start()
-
-        @pl.when(to == me)
-        def _():
-            c = pltpu.make_async_copy(src, dst, loc_o.at[t, j])
-            c.wait() if wait else c.start()
+        pl.when(to != me)(lambda: remote_copy(src, dst, send_o.at[t], recv_o.at[t], to).start())
+        pl.when(to == me)(lambda: pltpu.make_async_copy(src, dst, recv_o.at[t]).start())
+
+    def rows_done(t):
+        src, dst = (oT, dqT)[t], (o_out, dq_out)[t]
+        remote_copy(dst, dst, send_o.at[t], recv_o.at[t], mate).wait_recv()
+        kept = sum((owner_core(me * per_blk + j) == core).astype(jnp.int32) for j in range(per_blk))
+        for count in (1, 2):
+            left = src.at[:, pl.ds(0, (nslot - count) * BQ)]
+            pl.when(kept == count)(remote_copy(left, left, send_o.at[t], recv_o.at[t], mate).wait_send)
 
     def finish_group(g):
         for i in range(GROUP):
@@ -458,7 +483,7 @@
         for i in range(GROUP):
             finish_rows(GROUP * g + i)
         for i in range(GROUP):
-            out_rows(0, GROUP * g + i, False)
+            out_rows(0, GROUP * g + i)
 
     each(finish_group)
 
@@ -473,7 +498,7 @@
     def half_of(t, step, c):
         b = out_block(t, step)
         b = n - 1 - b if t == 0 else b
-        return pl.ds(aligned(b * blk + c * hw, 128), hw)
+        return pl.ds(aligned(b * blk + c * hw, LANES), hw)
 
     def pair(t, step):
         s = lax.rem(step, slots)
@@ -483,37 +508,32 @@
         return dr_send.at[step] if t == 0 else send_buf.at[t - 1, step]
 
     def sink_at(t, h, c):
-        return sinks[t].at[h, :, pl.ds(aligned(c * hw, 128), hw)]
+        return sinks[t].at[h, :, pl.ds(aligned(c * hw, LANES), hw)]
 
     def sink(t, step):
-        return remote_copy(ready(t, step), sink_at(t, chip, core), send_s.at[t, step], recv_s.at[t, chip, core], out_block(t, step))
+        return remote_copy(ready(t, step), sink_at(t, chip, core), send_s.at[t], recv_s.at[t], out_block(t, step))
 
     def keep(t, step):
-        return pltpu.make_async_copy(ready(t, step), sink_at(t, chip, core), loc_s.at[t])
+        return pltpu.make_async_copy(ready(t, step), sink_at(t, chip, core), recv_s.at[t])
 
     def combine(t, step):
         s = lax.rem(step, slots)
         mine = half_of(t, step, core)
         remote_copy(parts[t].at[:, mine], pair_buf.at[t, s], send_p.at[t, s], recv_p.at[t, s], mate).wait_recv()
         ready(t, step)[...] = (parts[t][:, mine] + pair_buf[t, s]).astype(BF16)
-
-    def to_owner(t, step, wait):
+        pair(t, step).wait_send()
+
+    def to_owner(t, step):
         b = out_block(t, step)
-
-        @pl.when(b != me)
-        def _():
-            sink(t, step).wait_send() if wait else sink(t, step).start()
-
-        @pl.when(b == me)
-        def _():
-            keep(t, step).wait() if wait else keep(t, step).start()
+        pl.when(b != me)(lambda: sink(t, step).start())
+        pl.when(b == me)(lambda: keep(t, step).start())
 
     def arrived(t):
-        for h in range(heads):
-            for c in range(2):
-                @pl.when(2 * h + c != me)
-                def _():
-                    remote_copy(ready(t, 0), sink_at(t, h, c), send_s.at[t, 0], recv_s.at[t, h, c], me).wait_recv()
+        remote_copy(sinks[t], sinks[t], send_s.at[t], recv_s.at[t], mate).wait_recv()
+
+    def departed(t):
+        others = (dr_send if t == 0 else send_buf.at[t - 1]).at[pl.ds(0, n - 1)]
+        remote_copy(others, others, send_s.at[t], recv_s.at[t], mate).wait_send()
 
     def final_slots(step, fn):
         first, end = (3 * step + 1) // 2, (3 * step + 4) // 2
@@ -526,18 +546,17 @@
 
     def exchange(step):
         for t in range(3):
-            pl.when(step >= slots)(pair(t, step - slots).wait_send)
             pair(t, step).start()
         final_slots(step, row_grads)
 
     def release(step):
         combine(0, step)
-        to_owner(0, step, False)
+        to_owner(0, step)
         for t in (1, 2):
             combine(t, step)
         for t in (1, 2):
-            to_owner(t, step, False)
-        final_slots(step, lambda k: out_rows(1, k, False))
+            to_owner(t, step)
+        final_slots(step, lambda k: out_rows(1, k))
 
     w_acc, w_in, w_half, w_part, w_mine = (9, 0), (10, 0), (10, 1), (11, 0), (11, 1)
     chunks, wide = range(4), BK // 2
@@ -553,16 +572,25 @@
 
     def swap(c):
         return remote_copy(acc_at(c, aligned((1 - core) * half, half), half), place(w_in, c, c // 2 * half, half),
-                           send_w.at[0, c], recv_w.at[0, c], mate)
-
-    def spread(i, c):
-        z = lax.rem(chip + i, heads)
-        return remote_copy(place(w_half, c, aligned(c // 2 * half + z * piece, piece), piece),
-                           place(w_part, c, (2 * i + c // 2) * piece, piece), send_w.at[i, c], recv_w.at[i, c], 2 * z + core)
+                           send_w.at[c], recv_w.at[c], mate)
+
+    def share(c, z):
+        return place(w_half, c, aligned(c // 2 * half + z * piece, piece), piece)
+
+    def from_below(c, z):
+        return place(w_part, c, aligned((2 * z + c // 2) * piece, piece), piece)
+
+    def from_above(c, z):
+        return place(w_mine, c, (2 + 2 * z + c // 2) * piece, piece)
+
+    def up(z, c):
+        return remote_copy(share(c, z), from_below(c, chip), send_x.at[0], recv_u.at[chip, c], 2 * z + core)
+
+    def down(z, c):
+        return remote_copy(share(c, z), from_above(c, z), send_x.at[0], recv_d2.at[z, c], me - 2)
 
     def table_grad():
         arrived(0)
-        keep(0, 0).wait()
         dr = jnp.concatenate([flip_lanes(dr_buf[h], eye) for h in range(heads)], 0)
         for c in chunks:
             acc_at(c, 0, 2 * half)[...] = dot_nn(dr, table[:, c * wide:(c + 1) * wide])
@@ -573,13 +601,13 @@
             place(w_half, c, c // 2 * half, half)[...] = (
                 acc_at(c, aligned(core * half, half), half)[...] + place(w_in, c, c // 2 * half, half)[...])
         for c in chunks:
-            for i in (3, 2, 1):
-                spread(i, c).start()
+            for z in range(heads - 1, 0, -1):
+                pl.when(z > chip)(up(z, c).start)
 
     bodies, done = [], 0
     for step in range(n):
         tiles_done = sum(nslot - i for i in range((3 * step + 4) // 2))
-        bodies.append(-(-tiles_done // UNROLL) - done)
+        bodies.append(-(-tiles_done // UNROLL_GRAD) - done)
         done += bodies[-1]
     phases = [c for b in bodies[:-1] for c in (min(b, 1), max(b - 1, 0))]
 
@@ -595,7 +623,7 @@
 
         def some(i, kt):
             at = []
-            for u in range(UNROLL):
+            for u in range(UNROLL_GRAD):
                 at.append(kt)
                 kt = next_tile(*kt)
             grads(at)
@@ -615,69 +643,11 @@
         bias_buf[me, t] = rows_sum[:, t * dim:(t + 1) * dim] + jnp.zeros((8, dim), F32)
 
     def bias(o):
-        return remote_copy(bias_buf.at[me], bias_buf.at[me], send_b.at[o], recv_b2.at[me], lax.rem(me + o, n))
+        return remote_copy(bias_buf.at[me], bias_buf.at[me], send_b.at[0], recv_b2.at[0], lax.rem(me + o, n))
 
     for o in range(1, n):
         bias(o).start()
-    table_grad()
-
-    def home(co, z, c):
-        return dw_out.at[pl.ds(aligned(co * half + z * piece, piece), piece), pl.ds(c * wide, wide)]
-
-    def my_piece(c):
-        return place(w_mine, c, c // 2 * piece, piece)
-
-    def collect(i, c):
-        z = lax.rem(chip + i, heads)
-        return remote_copy(my_piece(c), home(core, chip, c), send_w.at[4 + i, c], recv_w.at[4 + chip, c], 2 * z + core)
-
-    def hand_over(i, c):
-        z = lax.rem(chip + i, heads)
-        return remote_copy(my_piece(c) if i == 0 else home(core, z, c), home(core, z, c), send_w.at[8 + i, c], recv_w.at[8 + z, c], mate)
-
-    def stay(c):
-        return pltpu.make_async_copy(my_piece(c), home(core, chip, c), loc_w.at[c])
-
-    for c in chunks:
-        for i in range(1, heads):
-            spread(i, c).wait()
-        got = place(w_half, c, aligned(c // 2 * half + chip * piece, piece), piece)[...]
-        for i in range(1, heads):
-            got = got + place(w_part, c, (2 * i + c // 2) * piece, piece)[...]
-        my_piece(c)[...] = got
-        for i in range(1, heads):
-            collect(i, c).start()
-        hand_over(0, c).start()
-        stay(c).start()
-    for c in chunks:
-        for i in range(1, heads):
-            z = lax.rem(chip + i, heads)
-            remote_copy(my_piece(c), home(core, z, c), send_w.at[0, c], recv_w.at[4 + z, c], me).wait_recv()
-            hand_over(i, c).start()
-    for o in range(1, n):
-        b = lax.rem(me + o, n)
-        remote_copy(bias_buf.at[b], bias_buf.at[b], send_b.at[0], recv_b2.at[b], me).wait_recv()
-    for t in range(2):
-        bias_out[t] = jnp.concatenate([bias_buf[2 * h, t, :1] + bias_buf[2 * h + 1, t, :1] for h in range(heads)], 0)
-
-    for c in chunks:
-        stay(c).wait()
-        for i in range(heads):
-            remote_copy(my_piece(c), home(1 - core, i, c), send_w.at[0, c], recv_w.at[8 + i, c], me).wait_recv()
-            hand_over(i, c).wait_send()
-            if i:
-                collect(i, c).wait_send()
-    for o in range(1, n):
-        bias(o).wait_send()
-    for step in range(n):
-        pl.when(out_block(0, step) != me)(sink(0, step).wait_send)
     for t in range(3):
-        for step in range(n - slots, n):
-            pair(t, step).wait_send()
-        if t:
-            for step in range(n):
-                to_owner(t, step, True)
-            arrived(t)
         if t:
             to_mate(t).wait_send()
         for i in range(1, heads):
@@ -686,22 +656,99 @@
             if t:
                 direct(t, h).wait_send()
     for t in (0, 1):
-        for i in range(heads):
+        for h in range(heads):
             for j in range(per_blk):
-                to = 2 * i + owner_core(me * per_blk + j)
+                to = 2 * h + owner_core(me * per_blk + j)
 
                 @pl.when(to != me)
                 def _():
                     remote_copy((q_in, do_in)[t].at[0, :, pl.ds(0, BQ)], (qT, doT)[t].at[:, pl.ds(0, BQ)],
-                                send_q.at[t, i, j], recv_q.at[t, 0], to).wait_send()
-        for k in range(nslot):
-            out_rows(t, k, True)
-        for h in range(heads):
-            for j in range(per_blk):
-                @pl.when(2 * h + owner_core(me * per_blk + j) != me)
-                def _():
-                    remote_copy((oT, dqT)[t].at[:, pl.ds(0, BQ)], (o_out, dq_out)[t].at[h, :, pl.ds(j * BQ, BQ)],
-                                send_o.at[t, 0], recv_o.at[t, h, j], me).wait_recv()
+                                send_q.at[t, h, j], recv_q.at[t, 0], to).wait_send()
+    rows_done(0)
+    table_grad()
+
+    def up_landed(z, c):
+        remote_copy(share(c, 0), from_below(c, z), send_x.at[0], recv_u.at[z, c], me).wait_recv()
+
+    def take_above(z, c):
+        @pl.when(chip < groups - 1)
+        def _():
+            remote_copy(share(c, z), from_above(c, z), send_x.at[0], recv_d2.at[z, c], me).wait_recv()
+            share(c, z)[...] += from_above(c, z)[...]
+
+        pl.when(z < chip)(down(z, c).start)
+
+    def home(co, z, c):
+        return dw_out.at[pl.ds(aligned(co * half + z * piece, piece), piece), pl.ds(c * wide, wide)]
+
+    def my_piece(c):
+        return place(w_mine, c, c // 2 * piece, piece)
+
+    end = jnp.where(lower, heads - 1, 0)
+
+    def collect(z, c):
+        return remote_copy(my_piece(c), home(core, chip, c), send_x.at[0], recv_c.at[chip, c], 2 * z + core)
+
+    def relay(z, c):
+        return remote_copy(home(core, z, c), home(core, z, c), send_x.at[0], recv_c.at[z, c], jnp.where(lower, core, n - 2 + core))
+
+    def relays(z):
+        return ((chip == 1) & (z > 1)) | ((chip == groups - 2) & (z < groups - 2))
+
+    def hand_over(z):
+        whole = dw_out.at[pl.ds(aligned(core * half + z * piece, piece), piece)]
+        return remote_copy(whole, whole, send_x.at[0], recv_h.at[0], mate)
+
+    def hand_over_mine(c):
+        return remote_copy(my_piece(c), home(core, chip, c), send_x.at[0], recv_h.at[0], mate)
+
+    def stay(c):
+        return pltpu.make_async_copy(my_piece(c), home(core, chip, c), loc_w.at[0])
+
+    for c in chunks:
+        for z in range(heads - 1):
+            pl.when(z <= chip)(functools.partial(take_above, z, c))
+    for c in chunks:
+        for z in range(heads - 1):
+            @pl.when(z < chip)
+            def _():
+                up_landed(z, c)
+                share(c, chip)[...] += from_below(c, z)[...]
+
+        my_piece(c)[...] = share(c, chip)[...]
+        for z in range(heads):
+            pl.when((z != chip) & (z != end))(collect(z, c).start)
+        hand_over_mine(c).start()
+        stay(c).start()
+    for c in chunks:
+        for at in range(heads):
+            z = jnp.where(lower, at, heads - 1 - at)
+
+            @pl.when(z != chip)
+            def _():
+                remote_copy(my_piece(c), home(core, z, c), send_x.at[0], recv_c.at[z, c], me).wait_recv()
+                pl.when(relays(z))(relay(z, c).start)
+                if c == chunks[-1]:
+                    hand_over(z).start()
+
+    others = bias_buf.at[pl.ds(0, n - 1)]
+    remote_copy(others, others, send_b.at[0], recv_b2.at[0], mate).wait_recv()
+    for t in range(2):
+        bias_out[t] = jnp.concatenate([bias_buf[2 * h, t, :1] + bias_buf[2 * h + 1, t, :1] for h in range(heads)], 0)
+
+    my_rows = dw_out.at[pl.ds(aligned(core * half + chip * piece, piece), piece)]
+    pltpu.make_async_copy(my_rows, my_rows, loc_w.at[0]).wait()
+    remote_copy(others, others, send_b.at[0], recv_b2.at[0], mate).wait_send()
+    for t in range(3):
+        departed(t)
+        if t:
+            arrived(t)
+    rows_done(1)
+    for count, here in ((9, (chip == 0) | (chip == groups - 1)), (11, (chip > 0) & (chip < groups - 1))):
+        sent = s_all.at[pl.ds(0, count), pl.ds(0, 2 * piece)]
+        pl.when(here)(remote_copy(sent, sent, send_x.at[0], recv_h.at[0], mate).wait_send)
+    theirs = dw_out.at[pl.ds(aligned((1 - core) * half, half), half)]
+    remote_copy(theirs, theirs, send_x.at[0], recv_h.at[0], mate).wait_recv()
 
 
 def solution(mesh):
@@ -724,20 +771,20 @@
         o, dq, dk, dvv, dw, bias = pl.pallas_call(
             functools.partial(attention_kernel, n),
             out_shape=[sds((heads, dim, blk), BF16)] * 4 + [sds((heads * dim, model), F32), sds((2, heads, dim), F32)],
-            in_specs=[hbm] * 5 + [vmem] * 3, out_specs=[hbm] * 5 + [vmem],
+            in_specs=[hbm] * 6 + [vmem] * 2, out_specs=[hbm] * 5 + [vmem],
             scratch_shapes=[
                 buf((dim, rows), BF16), buf((dim, rows), BF16), buf((dim, seq), BF16), buf((dim, seq), BF16), buf((KX, seq + PAD), BF16),
                 buf((dim, rows), BF16), buf((dim, rows), BF16), buf((dim, seq), F32), buf((dim, seq), F32), buf((dim, seq + PAD), F32),
-                buf((tiles, BQ, BK), F32), buf((nslot, BQ, 128), BF16), buf((nslot, BQ, 128), BF16), buf((nslot, BQ, dim), BF16),
+                buf((tiles, BQ, BK), F32), buf((nslot, BQ, LANES), BF16), buf((nslot, BQ, LANES), BF16), buf((nslot, BQ, dim), BF16),
                 buf((nslot, dim, BQ), BF16), buf((nslot, dim, BQ), BF16), buf((nslot, dim, BQ), BF16),
-                buf((nslot, BQ, 128), F32), buf((nslot, BQ, 128), F32), buf((nslot, BQ, 2 * dim), F32),
+                buf((nslot, BQ, LANES), F32), buf((nslot, BQ, LANES), F32), buf((nslot, BQ, 2 * dim), F32),
                 buf((GROUP + 1, BQ, 256), F32),
                 buf((3, 4, dim, blk // 2), F32), buf((n, dim, blk // 2), BF16), buf((2, n, dim, blk // 2), BF16), buf((heads, dim, blk), BF16), buf((blk, model), BF16),
                 buf((n, 2, 8, dim), F32),
                 dma((3, heads)), dma((3, heads)), dma((2, heads, per_blk)), dma((3, n)), dma((2, nslot)), dma((3,)), dma((2, per_blk)),
-                dma((2, nslot)), dma((2, heads, per_blk)), dma((2, per_blk)), dma((3, 4)), dma((3, 4)),
-                dma((3, n)), dma((3, heads, 2)), dma((3,)),
-                dma, dma((12, 4)), dma((12, 4)), dma((4,)), dma((n,)), dma((n,))],
+                dma((2,)), dma((2,)), dma((3, 4)), dma((3, 4)), dma((3,)), dma((3,)),
+                dma((1 + model // LANES,)), dma((4,)), dma((4,)), dma((1,)), dma((1,)), dma((1,)),
+                *[dma((heads, 4))] * 3, dma((1,)), dma((1,))],
             compiler_params=pltpu.CompilerParams(collective_id=0, has_side_effects=True, vmem_limit_bytes=67043328),
             name='attention',
         )(qT, kT, vT, doT, rel_table, wT, u_bias, v_bias)

time: 142 us -> 134 us (0.944)
  Pallas kernels: 141 us -> 133 us
    pallas_call x1, Pallas kernels: 138 us -> 130 us  [local_fn(): pl.pallas_call(functools.partial(attention_kernel, n), out_shape=[sds((he...]
where the time goes in v5:
time: 134 us
  Pallas kernels  133 us (99%)
    pallas_call x1, Pallas kernels, local_fn(): pl.pallas_call(functools.partial(attention_kernel, n), out_shape=[sds((he...  130 us
    pallas_call x1, Pallas kernels, local_fn(): pl.pallas_call(hand_off_kernel, grid=(steps,), out_shape=[sds((heads, dim...  3 us

profile of v5, /device:TPU:0, one launch (start us, length us, event | category | flops | bytes accessed | tf_op | source)
XLA Modules:
  0.0 133.9 jit_solution(12677883257414527887)
XLA Ops:
  0.6 130.2 %attention.1 = (bf16[4,64,768]{2,1,0:T(8,128)(2,1)}, bf16[4,64,768]{2,1,0:T(8,128)(2,1)}, bf16[4,64,768]{2,1,0:T(8,128)(2,1)}, bf16[4,64,768]{2,1,0:T(8,128)(2,1...) custom-call(bf16[4,64,768]{2,1,0:T(8,128)(2,1)} %bitcast.15, bf16[4,64,768]{2,1,0:T(8,128)(2,1)} %bitcast.16, ...), custom_call_target="tpu_custom_call" | custom-call | tf_op jit(solution)/shard_map/attention/pallas_call | solution.py:771
  130.9 3.0 %hand_off.1 = (bf16[4,64,768]{2,1,0:T(8,128)(2,1)}, bf16[4,64,768]{2,1,0:T(8,128)(2,1)}, bf16[4,64,768]{2,1,0:T(8,128)(2,1)}, bf16[4,64,768]{2,1,0:T(8,128)(2,1)...) custom-call(bf16[4,64,768]{2,1,0:T(8,128)(2,1)} %get-tuple-element.20.o, ...), custom_call_target="tpu_custom_call" | custom-call | tf_op jit(solution)/shard_map/hand_off/pallas_call | solution.py:795

commit v6 on v5

--- a/solution.py
+++ b/solution.py
@@ -16,9 +16,9 @@
 PAD = 512
 KX = 80
 GROUP = 3
-UNROLL_SUM = 13
+UNROLL_SUM = 26
 UNROLL_GRAD = 6
-VALUES_AT = 6
+VALUES_AT = 5
 MESH_ID = pl.DeviceIdType.MESH
 
 
@@ -425,7 +425,7 @@
         *ahead, ahead_q = (look_up(x + 1, column) for column in range(2, 6))
 
         def arrives_now(g, q):
-            return (q >= 0) & ((g < groups // 2) != lower)
+            return (q >= 0) & ((g < groups // 2) != lower) & (chip == 0)
 
         for t, g in zip((0, 0, 1), need):
             pl.when((g >= 0) & ((x == 0) | arrives_now(g, new_q)))(functools.partial(pass_on, t, g))
@@ -549,14 +549,26 @@
             pair(t, step).start()
         final_slots(step, row_grads)
 
-    def release(step):
-        combine(0, step)
-        to_owner(0, step)
-        for t in (1, 2):
-            combine(t, step)
+    def bulk(step):
         for t in (1, 2):
             to_owner(t, step)
         final_slots(step, lambda k: out_rows(1, k))
+
+    def held(step):
+        return ((chip == 3) & ((step == 3) | (step == 4) | (step == 5)))
+
+    def release_offsets(step):
+        combine(0, step)
+        to_owner(0, step)
+
+    def release_rest(step):
+        for t in (1, 2):
+            combine(t, step)
+        pl.when(~held(step))(lambda: bulk(step))
+
+    def release(step):
+        release_offsets(step)
+        release_rest(step)
 
     w_acc, w_in, w_half, w_part, w_mine = (9, 0), (10, 0), (10, 1), (11, 0), (11, 1)
     chunks, wide = range(4), BK // 2
@@ -636,8 +648,9 @@
 
     lax.fori_loop(0, len(phases), phase, (jnp.where(lower, nslot - 1, 0), jnp.int32(0)))
     exchange(n - 1)
-    release(n - 2)
-    release(n - 1)
+    for part in (release_offsets, release_rest):
+        part(n - 2)
+        part(n - 1)
     rows_sum = jnp.sum(jnp.sum(acc[...].reshape(nslot * BQ // 8, 8, 2 * dim), axis=0), axis=0, keepdims=True)
     for t in range(2):
         bias_buf[me, t] = rows_sum[:, t * dim:(t + 1) * dim] + jnp.zeros((8, dim), F32)
@@ -708,6 +721,8 @@
     for c in chunks:
         for z in range(heads - 1):
             pl.when(z <= chip)(functools.partial(take_above, z, c))
+    for step in (3, 4, 5):
+        pl.when(held(step))(functools.partial(bulk, step))
     for c in chunks:
         for z in range(heads - 1):
             @pl.when(z < chip)

time: 134 us -> 132 us (0.985)
  Pallas kernels: 133 us -> 131 us
    pallas_call x1, Pallas kernels: 130 us -> 128 us  [local_fn(): pl.pallas_call(functools.partial(attention_kernel, n), out_shape=[sds((he...]
where the time goes in v6:
time: 132 us
  Pallas kernels  131 us (99%)
    pallas_call x1, Pallas kernels, local_fn(): pl.pallas_call(functools.partial(attention_kernel, n), out_shape=[sds((he...  128 us
    pallas_call x1, Pallas kernels, local_fn(): pl.pallas_call(hand_off_kernel, grid=(steps,), out_shape=[sds((heads, dim...  3 us

profile of v6, /device:TPU:0, one launch (start us, length us, event | category | flops | bytes accessed | tf_op | source)
XLA Modules:
  0.0 131.8 jit_solution(2890235261449951343)
XLA Ops:
  0.6 128.0 %attention.1 = (bf16[4,64,768]{2,1,0:T(8,128)(2,1)}, bf16[4,64,768]{2,1,0:T(8,128)(2,1)}, bf16[4,64,768]{2,1,0:T(8,128)(2,1)}, bf16[4,64,768]{2,1,0:T(8,128)(2,1...) custom-call(bf16[4,64,768]{2,1,0:T(8,128)(2,1)} %bitcast.15, bf16[4,64,768]{2,1,0:T(8,128)(2,1)} %bitcast.16, ...), custom_call_target="tpu_custom_call" | custom-call | tf_op jit(solution)/shard_map/attention/pallas_call | solution.py:786
  128.6 3.0 %hand_off.1 = (bf16[4,64,768]{2,1,0:T(8,128)(2,1)}, bf16[4,64,768]{2,1,0:T(8,128)(2,1)}, bf16[4,64,768]{2,1,0:T(8,128)(2,1)}, bf16[4,64,768]{2,1,0:T(8,128)(2,1)...) custom-call(bf16[4,64,768]{2,1,0:T(8,128)(2,1)} %get-tuple-element.20.o, ...), custom_call_target="tpu_custom_call" | custom-call | tf_op jit(solution)/shard_map/hand_off/pallas_call | solution.py:810

commit v7 on v6

--- a/solution.py
+++ b/solution.py
@@ -441,11 +441,15 @@
                 prepare(GROUP * new_q + i)
 
         pl.when(x == VALUES_AT)(send_values)
-        for i in range(GROUP):
-            prepare_skew(GROUP * gq + i, i, GROUP * gk)
         here = GROUP * gq, GROUP * gk, GROUP * gk + GROUP - 1
-        pl.when(gq == gk)(lambda: walk(score_tiles, GROUP * (GROUP + 1) // 2, *here, GROUP * (GROUP + 1) // 2))
-        pl.when(gq != gk)(lambda: walk(score_tiles, GROUP * GROUP, *here, GROUP * GROUP))
+
+        def score_pair(count):
+            for i in range(GROUP):
+                prepare_skew(GROUP * gq + i, i, GROUP * gk)
+            walk(score_tiles, count, *here, count)
+
+        pl.when(gq == gk)(lambda: score_pair(GROUP * (GROUP + 1) // 2))
+        pl.when(gq != gk)(lambda: score_pair(GROUP * GROUP))
 
     lax.fori_loop(0, len(orders[0]), lambda x, c: (forward_scores(x), c)[1], 0)
     send_cotangent()

time: 132 us -> 132 us (level)
  no operation moved by 1% of the time
where the time goes in v7:
time: 132 us; the launch traced here: 131 us
  Pallas kernels  131 us (99%)
    pallas_call x1, Pallas kernels, local_fn(): pl.pallas_call(functools.partial(attention_kernel, n), out_shape=[sds((he...  128 us
    pallas_call x1, Pallas kernels, local_fn(): pl.pallas_call(hand_off_kernel, grid=(steps,), out_shape=[sds((heads, dim...  3 us

profile of v7, /device:TPU:0, one launch (start us, length us, event | category | flops | bytes accessed | tf_op | source)
XLA Modules:
  0.0 131.4 jit_solution(622950469153361208)
XLA Ops:
  0.6 127.6 %attention.1 = (bf16[4,64,768]{2,1,0:T(8,128)(2,1)}, bf16[4,64,768]{2,1,0:T(8,128)(2,1)}, bf16[4,64,768]{2,1,0:T(8,128)(2,1)}, bf16[4,64,768]{2,1,0:T(8,128)(2,1...) custom-call(bf16[4,64,768]{2,1,0:T(8,128)(2,1)} %bitcast.15, bf16[4,64,768]{2,1,0:T(8,128)(2,1)} %bitcast.16, ...), custom_call_target="tpu_custom_call" | custom-call | tf_op jit(solution)/shard_map/attention/pallas_call | solution.py:790
  128.3 3.0 %hand_off.1 = (bf16[4,64,768]{2,1,0:T(8,128)(2,1)}, bf16[4,64,768]{2,1,0:T(8,128)(2,1)}, bf16[4,64,768]{2,1,0:T(8,128)(2,1)}, bf16[4,64,768]{2,1,0:T(8,128)(2,1)...) custom-call(bf16[4,64,768]{2,1,0:T(8,128)(2,1)} %get-tuple-element.20.o, ...), custom_call_target="tpu_custom_call" | custom-call | tf_op jit(solution)/shard_map/hand_off/pallas_call | solution.py:814
